TPU v7x, 128 devices: a whole 4x4x4 slice. The times are simulated.
128 devices in a mesh: wide: 16 (over y, z), narrow: 8 (over x, core).
Axes of the slice: x: 4, y: 4, z: 4, core: 2. Of those that a mesh axis runs over, the one named last changes fastest.
Arguments:
- fine_in: bfloat16 [32, 64, 128, 80], P(None, 'narrow', 'wide'), may hold values from -6 to 6
- voxel_mask: int32 [64, 128, 80], P('narrow', 'wide'), may hold values from 0 to 1, as said below
- timestep: int32 [1], replicated, may hold values from 0 to 999
- w_enc: bfloat16 [27, 32, 32], replicated, may hold values from -0.21875 to 0.21875
- b_enc: float32 [32], replicated, may hold values from -3 to 3
- w_down: bfloat16 [128, 256], replicated, may hold values from -0.375 to 0.375
- w_time: bfloat16 [128, 256], replicated, may hold values from -0.5 to 0.5
- w_coarse: bfloat16 [27, 128, 128], replicated, may hold values from -0.109375 to 0.109375
- b_coarse: float32 [128], replicated, may hold values from -3 to 3
- w_up: bfloat16 [32, 128], replicated, may hold values from -0.5 to 0.5
- w_dec: bfloat16 [27, 32, 64], replicated, may hold values from -0.15625 to 0.15625
- b_dec: float32 [32], replicated, may hold values from -3 to 3
Outputs:
- denoised: bfloat16 [32, 64, 128, 80], P(None, 'narrow', 'wide')
Inputs may be any that keep to these rules, and one draw needn't show every extreme that they name: `voxel_mask`: each device's tile of 8 x 8 x 80 voxels consists of aligned 8 x 8 x 8 blocks; a block is active when it holds a 1. Two tiles with the same narrow index whose wide indices differ by 8 hold at most 10 active blocks together, and some such pair holds exactly 10.
All inputs are finite; a program needn't handle non-finite values.
Results may differ from a plain program's by a relative error of at most 0.0044.
Values may be sent and summed in bfloat16 or wider, within the bound.
No kernel may reach another device: no remote copies, remote signals or barrier semaphores. Data moves between devices by JAX's collectives and lax.ppermute only.
A program may use at most 64 MiB of HBM per device.

v0:
```python
import math

import jax
import jax.numpy as jnp
from jax import lax
from jax.experimental import pallas as pl
from jax.experimental.pallas import tpu as pltpu
from jax.sharding import PartitionSpec as P

F32 = jnp.float32
BF16 = jnp.bfloat16
LANES = 128
ZC = 40
Z = 80
CH = 32
BITS = (0, 1)


def nn(a, b):
    return lax.dot_general(a, b, (((1,), (0,)), ((), ())), preferred_element_type=F32)


def nt(a, b):
    return lax.dot_general(a, b, (((1,), (1,)), ((), ())), preferred_element_type=F32)


def iota(shape, dim):
    return lax.broadcasted_iota(jnp.int32, shape, dim)


def silu(v):
    return v / (1.0 + jnp.exp(-v))


def rounded(v):
    return v.astype(BF16).astype(F32)


def pack_kernel(x_ref, m_ref, a_ref, k_ref):
    row = iota((Z, Z), 0)
    sel = (jnp.where(row < ZC, 2 * row, 2 * row - (Z - 1)) == iota((Z, Z), 1)).astype(F32).astype(BF16)
    src = iota((512, LANES), 0)
    y = src & 7
    goal = ((y >> 1) << 7) + ((src >> 8) << 6) + ((y & 1) << 5) + ((src >> 3) & 31) - iota((512, LANES), 1)
    perm = [(goal == LANES * i).astype(F32).astype(BF16) for i in range(4)]
    for cx in range(4):
        halves = []
        for a in BITS:
            x = 2 * cx + a
            tile = x_ref[:, x].astype(F32)
            tile = jnp.where(m_ref[x][None] > 0, tile, 0.0)
            halves.append(nt(sel, tile.reshape(8 * CH, Z).astype(BF16)).astype(BF16))
        both = jnp.concatenate(halves, axis=1)
        for cy in range(4):
            a_ref[cx, cy] = nn(both, perm[cy]).astype(BF16)
    mask = (m_ref[...] > 0).astype(F32).reshape(64, Z).astype(BF16)
    cols = nt(sel, mask)
    k_ref[...] = jnp.concatenate([cols[:ZC], cols[ZC:]], axis=1).astype(BF16)


def tap_of(out_bit, in_bit, far):
    if far:
        return 2 * (1 - in_bit) if out_bit != in_bit else None
    return in_bit - out_bit + 1


def placed(w_ref, taps, group):
    total = jnp.zeros((CH, LANES), F32)
    for g, tap in enumerate(taps):
        if tap is not None:
            total = jnp.where(group == g, w_ref[tap].astype(F32), total)
    return total


def block(w_ref, group, far_x, far_y, a_in, b_in, cz_in, shifted, cz_out):
    if shifted:
        tz = None
        if cz_out == 0 and cz_in == 1:
            tz = 0
        if cz_out == 1 and cz_in == 0:
            tz = 2
    else:
        tz = cz_in - cz_out + 1
    taps = []
    for a_out in BITS:
        for b_out in BITS:
            tx = tap_of(a_out, a_in, far_x)
            ty = tap_of(b_out, b_in, far_y)
            taps.append(None if tx is None or ty is None or tz is None else 9 * tx + 3 * ty + tz)
    return placed(w_ref, taps, group)


KINDS = ((0, 0), (1, 0), (0, 1), (1, 1))


def weights_kernel(we_ref, wd_ref, wl_ref, oe_ref, od_ref):
    group = iota((CH, LANES), 1) >> 5
    for w_ref, o_ref in ((we_ref, oe_ref), (wd_ref, od_ref)):
        for t, (fx, fy) in enumerate(KINDS):
            for cz in BITS:
                for a in BITS:
                    for b in BITS:
                        base = 256 * t + 128 * cz + 64 * a + 32 * b
                        for s in BITS:
                            for co in BITS:
                                v = block(w_ref, group, fx, fy, a, b, cz, s, co)
                                o_ref[base : base + CH, 256 * s + 128 * co : 256 * s + 128 * co + LANES] = v.astype(BF16)
    for t, (fx, fy) in enumerate(KINDS):
        for a in BITS:
            for b in BITS:
                base = 1024 + 128 * t + 64 * a + 32 * b
                for s in BITS:
                    for co in BITS:
                        v = block(wl_ref, group, fx, fy, a, b, 0, s, co) + block(wl_ref, group, fx, fy, a, b, 1, s, co)
                        od_ref[base : base + CH, 256 * s + 128 * co : 256 * s + 128 * co + LANES] = v.astype(BF16)


def moved(t, amount, edge):
    rows = t.shape[0]
    return jnp.where(edge, 0.0, pltpu.roll(t, amount % rows, 0))


def depth_of(rows):
    return iota((rows, LANES), 0) % ZC


def main_kernel(
    own_ref, left_ref, right_ref, kl_ref, ko_ref, kr_ref, m_ref, we_ref, be_ref, wdn_ref, gain_ref, shift_ref,
    wc_ref, bc_ref, wu_ref, wd_ref, bd_ref, out_ref, a_ref, v_ref, e_ref, c_ref, u_ref, l_ref,
):
    lane = iota((ZC, LANES), 1)
    low_a = lane < 64
    low_b = (lane & 32) == 0
    for xi in range(10):
        ref, at = (left_ref, xi) if xi < 3 else ((own_ref, xi - 3) if xi < 7 else (right_ref, xi - 7))
        for yi in range(10):
            v = ref[at, yi].astype(F32)
            for cz in BITS:
                a_ref[xi, cz, yi * ZC : (yi + 1) * ZC] = v[cz * ZC : (cz + 1) * ZC]
    la8 = iota((320, LANES), 1) < 64
    lb8 = (iota((320, LANES), 1) & 32) == 0
    for xi in range(10):
        for cz in BITS:
            v_ref[xi, cz] = jnp.where(lb8, a_ref[xi, cz, 80:400], a_ref[xi, cz, 0:320])
    z8 = depth_of(320)
    first8, last8 = z8 == 0, z8 == ZC - 1
    where_lane = iota((8, LANES), 1)
    blocks = {}
    for bx, ref in enumerate((kl_ref, ko_ref, kr_ref)):
        for by in range(3):
            k = ref[by * ZC : (by + 1) * ZC].astype(F32)
            m = jnp.maximum(k, pltpu.roll(k, LANES - 1, 1))
            m = jnp.maximum(m, pltpu.roll(m, LANES - 8, 1))
            m = jnp.maximum(m, pltpu.roll(m, LANES - 64, 1))
            blocks[bx, by] = (k, m)

    def spread(k, index):
        parts = []
        for i in range(5):
            parts.append(jnp.take_along_axis(k[8 * i : 8 * i + 8], index, axis=1, mode="promise_in_bounds"))
        return jnp.concatenate(parts, axis=0)

    def local(i):
        c = i - 3
        return (0, c + 4) if c < 0 else ((1, c) if c < 4 else (2, c - 4))

    on_of = {}
    for xi in range(1, 9):
        for cz in BITS:
            l_ref[:, 128 * cz : 128 * cz + 128] = a_ref[xi, cz, 40:360].astype(BF16)
            l_ref[:, 256 + 128 * cz : 384 + 128 * cz] = jnp.where(
                la8, a_ref[xi + 1, cz, 40:360], a_ref[xi - 1, cz, 40:360]
            ).astype(BF16)
            l_ref[:, 512 + 128 * cz : 640 + 128 * cz] = v_ref[xi, cz].astype(BF16)
            l_ref[:, 768 + 128 * cz : 896 + 128 * cz] = jnp.where(la8, v_ref[xi + 1, cz], v_ref[xi - 1, cz]).astype(BF16)
        o = nn(l_ref[:, 0:1024], we_ref[...])
        bx, lx = local(xi)
        expanded = [[], []]
        on = []
        for yi in range(1, 9):
            by, ly = local(yi)
            k, m = blocks[bx, by]
            for cz in BITS:
                index = 64 * cz + (2 * lx + (where_lane >> 6)) * 8 + 2 * ly + ((where_lane >> 5) & 1)
                expanded[cz].append(spread(k, index))
            on.append(spread(m, where_lane * 0 + (16 * lx + 2 * ly)))
        on = jnp.concatenate(on, axis=0) > 0.5
        pre = (
            o[:, 0:128] + moved(o[:, 256:384], 1, first8) + be_ref[...],
            o[:, 128:256] + moved(o[:, 384:512], -1, last8) + be_ref[...],
        )
        enc = []
        for cz in BITS:
            active = jnp.concatenate(expanded[cz], axis=0) > 0.5
            e = jnp.where(active, silu(pre[cz]), 0.0)
            enc.append(e.astype(BF16))
            if 2 <= xi <= 7:
                e_ref[xi - 2, cz] = rounded(e)[40:280]
        lifted = nn(jnp.concatenate(enc, axis=1), wdn_ref[...])
        c = jnp.where(on, silu(lifted * gain_ref[...] + shift_ref[...]), 0.0)
        c_ref[xi - 1] = rounded(c)
        on_of[xi] = on[40:280]
    z6 = depth_of(240)
    first6, last6 = z6 == 0, z6 == ZC - 1
    pairs = [(dx, dy) for dx in range(3) for dy in range(3)]
    for xo in range(6):
        p = None
        for i in range(0, 9, 2):
            some = pairs[i : i + 2]
            lhs = [c_ref[xo + dx, dy * ZC : dy * ZC + 240].astype(BF16) for dx, dy in some]
            rhs = [wc_ref[9 * dx + 3 * dy : 9 * dx + 3 * dy + 3].reshape(384, 128) for dx, dy in some]
            lhs = jnp.concatenate(lhs, axis=1) if len(lhs) > 1 else lhs[0]
            rhs = jnp.concatenate(rhs, axis=1) if len(rhs) > 1 else rhs[0]
            q = nt(lhs, rhs)
            p = q if p is None else p + q
        s = p[:, 128:256] + moved(p[:, 0:128], 1, first6) + moved(p[:, 256:384], -1, last6) + bc_ref[...]
        act = jnp.where(on_of[xo + 2], silu(s), 0.0).astype(BF16)
        u_ref[xo] = rounded(nn(act, wu_ref[...]))
    z4 = depth_of(160)
    first4, last4 = z4 == 0, z4 == ZC - 1
    la4 = iota((160, LANES), 1) < 64
    lb4 = (iota((160, LANES), 1) & 32) == 0

    def spans(load):
        mid = [load(i)[40:200] for i in range(3)]
        side = [jnp.where(lb4, load(i)[80:240], load(i)[0:160]) for i in range(3)]
        return mid[1], jnp.where(la4, mid[2], mid[0]), side[1], jnp.where(la4, side[2], side[0])

    row = iota((LANES, Z), 0)
    back = (jnp.where(row < ZC, 2 * row, 2 * row - (Z - 1)) == iota((LANES, Z), 1)).astype(F32).astype(BF16)
    src = iota((512, LANES), 0)
    goal = (((src >> 6) & 1) << 8) + ((src & 31) << 3) + ((src >> 7) << 1) + ((src >> 5) & 1) - iota((512, LANES), 1)
    perm = jnp.concatenate([(goal == LANES * i).astype(F32).astype(BF16) for i in range(4)], axis=1)
    for xo in range(4):
        for cz in BITS:
            for t, v in enumerate(spans(lambda i: e_ref[xo + i, cz])):
                l_ref[0:160, 256 * t + 128 * cz : 256 * t + 128 * cz + 128] = v.astype(BF16)
        for t, v in enumerate(spans(lambda i: u_ref[xo + i])):
            l_ref[0:160, 1024 + 128 * t : 1152 + 128 * t] = v.astype(BF16)
        o = nn(l_ref[0:160, :], wd_ref[...])
        d0 = (o[:, 0:128] + moved(o[:, 256:384], 1, first4) + bd_ref[...])
        d1 = (o[:, 128:256] + moved(o[:, 384:512], -1, last4) + bd_ref[...])
        d = [jnp.concatenate([v[ZC * y : ZC * y + ZC] for y in range(4)], axis=1) for v in (d0, d1)]
        d = jnp.concatenate(d + [jnp.zeros((LANES - Z, 512), F32)], axis=0).astype(BF16)
        d = nn(d, perm)
        for a in BITS:
            t = jnp.transpose(d[:, 256 * a : 256 * a + 256]).astype(BF16)
            t = nn(t, back).reshape(CH, 8, Z)
            x = 2 * xo + a
            out_ref[:, x] = jnp.where(m_ref[x][None] > 0, t, 0.0).astype(BF16)


def vmem(n):
    return [pl.BlockSpec(memory_space=pltpu.VMEM)] * n


def shifted(value, axis, step):
    peers = lax.axis_size(axis)
    return lax.ppermute(value, axis, [(i, i + step) for i in range(peers) if 0 <= i + step < peers])


def time_features(timestep, embed_width):
    halves = embed_width // 2
    freqs = jnp.exp(-math.log(10000.0) * jnp.arange(halves, dtype=F32) / halves)
    angles = timestep[0].astype(F32) * freqs
    return jnp.concatenate([jnp.sin(angles), jnp.cos(angles)]).astype(BF16)


def tiled_taps(w):
    return jnp.tile(jnp.transpose(w, (0, 2, 1)), (1, 1, 4))


def on_device(
    fine_in, voxel_mask, timestep, w_enc, b_enc, w_down, w_time, w_coarse, b_coarse, w_up, w_dec, b_dec
):
    big = pltpu.CompilerParams(vmem_limit_bytes=60 * 1024 * 1024)
    tile, mask = pl.pallas_call(
        pack_kernel,
        out_shape=[jax.ShapeDtypeStruct((4, 4, Z, LANES), BF16), jax.ShapeDtypeStruct((ZC, LANES), BF16)],
        in_specs=vmem(2),
        out_specs=vmem(2),
        compiler_params=big,
        cost_estimate=pl.CostEstimate(flops=10**9, bytes_accessed=10**6, transcendentals=0),
        name="pack",
    )(fine_in, voxel_mask)

    def joined(part, masks):
        return jnp.concatenate([part.reshape(-1, LANES), masks], axis=0)

    low = shifted(joined(tile[:, 1:4], mask), "wide", 1)
    high = shifted(joined(tile[:, 0:3], mask), "wide", -1)
    rows = 12 * Z
    wide = jnp.concatenate(
        [low[:rows].reshape(4, 3, Z, LANES), tile, high[:rows].reshape(4, 3, Z, LANES)], axis=1
    )
    masks = jnp.concatenate([low[rows:], mask, high[rows:]], axis=0)
    left = shifted(joined(wide[1:4], masks), "narrow", 1)
    right = shifted(joined(wide[0:3], masks), "narrow", -1)
    rows = 30 * Z

    embedded = time_features(timestep, w_time.shape[0])
    film = jnp.dot(embedded[None], w_time, preferred_element_type=F32)
    chans = w_down.shape[0]
    gains = 1.0 + film[:, :chans]
    shifts = film[:, chans:]

    enc_w, dec_w = pl.pallas_call(
        weights_kernel,
        out_shape=[jax.ShapeDtypeStruct((1024, 512), BF16), jax.ShapeDtypeStruct((1536, 512), BF16)],
        in_specs=vmem(3),
        out_specs=vmem(2),
        compiler_params=big,
        cost_estimate=pl.CostEstimate(flops=2 * 10**9, bytes_accessed=10**6, transcendentals=0),
        name="weights",
    )(tiled_taps(w_enc), tiled_taps(w_dec[:, :, :CH]), tiled_taps(w_dec[:, :, CH:]))
    down_w = jnp.transpose(w_down.reshape(chans, 2, 2, 2, CH), (3, 1, 2, 4, 0)).reshape(8 * CH, chans)
    up_w = jnp.tile(jnp.transpose(w_up), (1, 4))

    def four(bias):
        return jnp.tile(bias, 4)[None]

    return pl.pallas_call(
        main_kernel,
        out_shape=jax.ShapeDtypeStruct(fine_in.shape, BF16),
        in_specs=vmem(17),
        out_specs=vmem(1)[0],
        scratch_shapes=[
            pltpu.VMEM((10, 2, 400, LANES), F32),
            pltpu.VMEM((10, 2, 320, LANES), F32),
            pltpu.VMEM((6, 2, 240, LANES), F32),
            pltpu.VMEM((8, 320, LANES), F32),
            pltpu.VMEM((6, 240, LANES), F32),
            pltpu.VMEM((320, 1536), BF16),
        ],
        compiler_params=big,
        cost_estimate=pl.CostEstimate(flops=8 * 10**9, bytes_accessed=10**6, transcendentals=0),
        name="network",
    )(
        wide,
        left[:rows].reshape(3, 10, Z, LANES),
        right[:rows].reshape(3, 10, Z, LANES),
        left[rows:],
        masks,
        right[rows:],
        voxel_mask,
        enc_w,
        four(b_enc),
        down_w,
        gains,
        shifts,
        w_coarse,
        b_coarse[None],
        up_w,
        dec_w,
        four(b_dec),
    )


def solution(mesh):
    field = P(None, "narrow", "wide", None)
    return jax.shard_map(
        on_device,
        mesh=mesh,
        in_specs=(field, P("narrow", "wide", None)) + (P(),) * 10,
        out_specs=field,
        check_vma=False,
    )
```

profile of v0, /device:TPU:25, one launch (start us, length us, event | category | flops | bytes accessed | tf_op | source)
XLA Modules:
  0.0 58.0 jit_solution(668695275046404120)
XLA Ops:
  0.0 3.0 %pack.1 = (bf16[4,4,80,128]{3,2,1,0:T(8,128)(2,1)}, bf16[40,128]{1,0:T(8,128)(2,1)}) custom-call(bf16[32,8,8,80]{3,2,1,0:T(8,128)(2,1)} %x_ref.1, s32[8,8,80]{2,1,0:T(8,128)} %m_ref.3), custom_call_target="tpu_custom_call" | custom-call | flops 1000000000 | bytes 1000000 | tf_op jit(solution)/shard_map/pack/pallas_call | solution.py:277
  3.0 1.1 %fusion.5 = (bf16[4,3,80,128]{3,2,1,0:T(8,128)(2,1)S(1)}, bf16[4,3,80,128]{3,2,1,0:T(8,128)(2,1)S(1)}) fusion(bf16[4,4,80,128]{3,2,1,0:T(8,128)(2,1)} %get-tuple-element.9), kind=kLoop, calls=%fused_computation.22 | loop fusion | bytes 983040 | tf_op jit(solution)/shard_map/slice | solution.py:290
  4.1 0.7 %pad_maximum_fusion.8 = (bf16[1000,128]{1,0:T(8,128)(2,1)S(1)}, bf16[1000,128]{1,0:T(8,128)(2,1)S(1)}) fusion(bf16[40,128]{1,0:T(8,128)(2,1)} %get-tuple-element.10, bf16[960,128]{1,0:T(8,128)(2,1)S(1)} %bitcast.30, bf16[960,128]{1,0:T(8,128)(2,1)S(1)} %bitcast.31), kind=kLoop, calls=%fused_computation.8 | loop fusion | flops 896000 | bytes 1013760 | tf_op jit(solution)/shard_map/concatenate | solution.py:288
  4.8 3.5 %collective-permute-start = (bf16[1000,128]{1,0:T(8,128)(2,1)S(1)}, bf16[1000,128]{1,0:T(8,128)(2,1)S(1)}, u32[]{:S(2)}, u32[]{:S(2)}) collective-permute-start(bf16[1000,128]{1,0:T(8,128)(2,1)S(1)} %get-tuple-element.21), channel_id=1, source_target_pairs={{0,8},{8,16},{16,24},{24,32},{32,40},{40,48},{48,56},{56,64},{64,7... | collective-permute-start | bytes 768008 | tf_op jit(solution)/shard_map/ppermute | solution.py:259
  8.4 4.2 %collective-permute-start.1 = (bf16[1000,128]{1,0:T(8,128)(2,1)S(1)}, bf16[1000,128]{1,0:T(8,128)(2,1)S(1)}, u32[]{:S(2)}, u32[]{:S(2)}) collective-permute-start(bf16[1000,128]{1,0:T(8,128)(2,1)S(1)} %get-tuple-element.22), channel_id=1, source_target_pairs={{8,0},{16,8},{24,16},{32,24},{40,32},{48,40},{56,48},{64,56},{72,6... | collective-permute-start | bytes 768008 | tf_op jit(solution)/shard_map/ppermute | solution.py:259
  13.3 1.1 %tile.23.wd_ref = bf16[27,32,128]{2,1,0:T(8,128)(2,1)} reshape(bf16[27,32,4,32]{3,2,1,0:T(4,128)(2,1)S(1)} %tile.22) | data formatting | bytes 442368 | tf_op jit(solution)/shard_map/tile | solution.py:270
  15.0 1.2 %tile.25.wl_ref = bf16[27,32,128]{2,1,0:T(8,128)(2,1)} reshape(bf16[27,32,4,32]{3,2,1,0:T(4,128)(2,1)S(1)} %tile.24) | data formatting | bytes 442368 | tf_op jit(solution)/shard_map/tile | solution.py:270
  16.8 1.2 %tile.21.we_ref = bf16[27,32,128]{2,1,0:T(8,128)(2,1)} reshape(bf16[27,32,4,32]{3,2,1,0:T(4,128)(2,1)S(1)} %tile.20) | data formatting | bytes 442368 | tf_op jit(solution)/shard_map/tile | solution.py:270
  18.7 0.6 %copy.22 = bf16[2,2,2,32,128]{4,3,2,1,0:T(8,128)(2,1)} copy(bf16[2,2,2,32,128]{4,3,0,2,1:T(8,128)(2,1)S(1)} %bitcast.34) | data formatting | bytes 131072 | tf_op jit(solution)/shard_map/transpose | solution.py:316
  19.3 0.7 %copy.23.wu_ref = bf16[128,128]{1,0:T(8,128)(2,1)} copy(bf16[128,128]{0,1:T(8,128)(2,1)S(1)} %bitcast.36) | data formatting | bytes 65536 | tf_op jit(solution)/shard_map/tile | solution.py:317
  20.1 0.7 %broadcast_in_dim_tile.6.be_ref = f32[1,128]{1,0:T(1,128)} reshape(f32[4,32]{1,0:T(4,128)S(1)} %tile.26) | data formatting | bytes 1024 | tf_op jit(solution)/shard_map/broadcast_in_dim;tile | solution.py:320
  20.7 0.7 %broadcast_in_dim_tile.7.bd_ref = f32[1,128]{1,0:T(1,128)} reshape(f32[4,32]{1,0:T(4,128)S(1)} %tile.57) | data formatting | bytes 1024 | tf_op jit(solution)/shard_map/broadcast_in_dim;tile | solution.py:320
  21.4 3.0 %weights.1 = (bf16[1024,512]{1,0:T(8,128)(2,1)}, bf16[1536,512]{1,0:T(8,128)(2,1)}) custom-call(bf16[27,32,128]{2,1,0:T(8,128)(2,1)} %tile.21.we_ref, bf16[27,32,128]{2,1,0:T(8,128)(2,1)} %tile.23.wd_ref, bf16[27,32,128]{2,1,0:T(8,128)(2,1)} %tile.25.wl_ref), custom_call_target="tpu_custom_call" | custom-call | flops 2000000000 | bytes 1000000 | tf_op jit(solution)/shard_map/weights/pallas_call | solution.py:307
  25.5 3.9 %collective-permute-start.2 = (bf16[2520,128]{1,0:T(8,128)(2,1)S(1)}, bf16[2520,128]{1,0:T(8,128)(2,1)S(1)}, u32[]{:S(2)}, u32[]{:S(2)}) collective-permute-start(bf16[2520,128]{1,0:T(8,128)(2,1)S(1)} %get-tuple-element.20), channel_id=1, source_target_pairs={{0,1},{1,2},{2,3},{3,4},{4,5},{5,6},{6,7},{8,9},{9,10},{10,11},{11... | collective-permute-start | bytes 1935368 | tf_op jit(solution)/shard_map/ppermute | solution.py:259
  29.4 2.1 %collective-permute-start.3 = (bf16[2520,128]{1,0:T(8,128)(2,1)S(1)}, bf16[2520,128]{1,0:T(8,128)(2,1)S(1)}, u32[]{:S(2)}, u32[]{:S(2)}) collective-permute-start(bf16[2520,128]{1,0:T(8,128)(2,1)S(1)} %get-tuple-element.19), channel_id=1, source_target_pairs={{1,0},{2,1},{3,2},{4,3},{5,4},{6,5},{7,6},{9,8},{10,9},{11,10},{12... | collective-permute-start | bytes 1935368 | tf_op jit(solution)/shard_map/ppermute | solution.py:259
  31.8 0.6 fusion.6
  32.3 0.6 %pad_maximum_fusion.9.ko_ref = bf16[120,128]{1,0:T(8,128)(2,1)} fusion(bf16[40,128]{1,0:T(8,128)(2,1)S(1)} %slice.68, bf16[40,128]{1,0:T(8,128)(2,1)S(1)} %copy-done.5, bf16[40,128]{1,0:T(8,128)(2,1)S(1)} %slice.67), kind=kLoop, calls=%fused_computation.11 | loop fusion | flops 92160 | bytes 61440 | tf_op jit(solution)/shard_map/concatenate | solution.py:296
  33.0 3.9 %collective-permute-done.2 = bf16[2520,128]{1,0:T(8,128)(2,1)S(1)} collective-permute-done((bf16[2520,128]{1,0:T(8,128)(2,1)S(1)}, bf16[2520,128]{1,0:T(8,128)(2,1)S(1)}, u32[]{:S(2)}, u32[]{:S(2)}) %collective-permute-start.2) | collective-permute-done | bytes 645152 | tf_op jit(solution)/shard_map/ppermute | solution.py:259
  36.8 0.9 %slice.69 = bf16[2400,128]{1,0:T(8,128)(2,1)} slice(bf16[2520,128]{1,0:T(8,128)(2,1)S(1)} %collective-permute-done.2), slice={[0:2400], [0:128]} | slice | bytes 1228800 | tf_op jit(solution)/shard_map/slice | solution.py:340
  37.7 0.6 %slice.72.kl_ref = bf16[120,128]{1,0:T(8,128)(2,1)} slice(bf16[2520,128]{1,0:T(8,128)(2,1)S(1)} %collective-permute-done.2), slice={[2400:2520], [0:128]} | slice | bytes 61440 | tf_op jit(solution)/shard_map/slice | solution.py:342
  38.3 2.9 %collective-permute-done.3 = bf16[2520,128]{1,0:T(8,128)(2,1)S(1)} collective-permute-done((bf16[2520,128]{1,0:T(8,128)(2,1)S(1)}, bf16[2520,128]{1,0:T(8,128)(2,1)S(1)}, u32[]{:S(2)}, u32[]{:S(2)}) %collective-permute-start.3) | collective-permute-done | bytes 645152 | tf_op jit(solution)/shard_map/ppermute | solution.py:259
  41.2 0.9 %slice.71 = bf16[2400,128]{1,0:T(8,128)(2,1)} slice(bf16[2520,128]{1,0:T(8,128)(2,1)S(1)} %collective-permute-done.3), slice={[0:2400], [0:128]} | slice | bytes 1228800 | tf_op jit(solution)/shard_map/slice | solution.py:341
  42.1 0.6 %slice.73.kr_ref = bf16[120,128]{1,0:T(8,128)(2,1)} slice(bf16[2520,128]{1,0:T(8,128)(2,1)S(1)} %collective-permute-done.3), slice={[2400:2520], [0:128]} | slice | bytes 61440 | tf_op jit(solution)/shard_map/slice | solution.py:344
  42.7 15.3 %network.1 = bf16[32,8,8,80]{3,2,1,0:T(8,128)(2,1)} custom-call(bf16[4,10,80,128]{3,2,1,0:T(8,128)(2,1)} %copy-done.1, bf16[3,10,80,128]{3,2,1,0:T(8,128)(2,1)} %bitcast.32, bf16[3,10,80,128]{3,2,1,0:T(8,128)(2,1)} %bitcast.33, bf16[120,128]{1,0:T(8,128)(2,1)} %slice.72.kl_ref, bf16[120,128]{1,0:T(8,128)(2,1)} %pad_maximum_fusion.9.ko_ref, ...), custom_call_target="tpu_custom_call" | custom-call | flops 8000000000 | bytes 1000000 | tf_op jit(solution)/shard_map/network/pallas_call | solution.py:322
  (42 shorter events, 3.1 us)
Async XLA Ops:
  0.0 31.6 %copy-start = (bf16[128,256]{1,0:T(8,128)(2,1)S(1)}, bf16[128,256]{1,0:T(8,128)(2,1)}, u32[]{:S(2)}) copy-start(bf16[128,256]{1,0:T(8,128)(2,1)} %param.18) | copy-start | bytes 196612
  3.0 9.7 %copy-start.3 = (bf16[27,32,64]{2,1,0:T(8,128)(2,1)S(1)}, bf16[27,32,64]{2,1,0:T(8,128)(2,1)}, u32[]{:S(2)}) copy-start(bf16[27,32,64]{2,1,0:T(8,128)(2,1)} %param.22) | copy-start | bytes 331780
  4.8 19.5 %collective-permute-start = (bf16[1000,128]{1,0:T(8,128)(2,1)S(1)}, bf16[1000,128]{1,0:T(8,128)(2,1)S(1)}, u32[]{:S(2)}, u32[]{:S(2)}) collective-permute-start(bf16[1000,128]{1,0:T(8,128)(2,1)S(1)} %get-tuple-element.21), channel_id=1, source_target_pairs={{0,8},{8,16},{16,24},{24,32},{32,40},{40,48},{48,56},{56,64},{64,7... | collective-permute-start | bytes 768008 | tf_op jit(solution)/shard_map/ppermute | solution.py:259
  8.4 16.0 %collective-permute-start.1 = (bf16[1000,128]{1,0:T(8,128)(2,1)S(1)}, bf16[1000,128]{1,0:T(8,128)(2,1)S(1)}, u32[]{:S(2)}, u32[]{:S(2)}) collective-permute-start(bf16[1000,128]{1,0:T(8,128)(2,1)S(1)} %get-tuple-element.22), channel_id=1, source_target_pairs={{8,0},{16,8},{24,16},{32,24},{40,32},{48,40},{56,48},{64,56},{72,6... | collective-permute-start | bytes 768008 | tf_op jit(solution)/shard_map/ppermute | solution.py:259
  14.5 1.7 %copy-start.4 = (bf16[27,32,32]{2,1,0:T(8,128)(2,1)S(1)}, bf16[27,32,32]{2,1,0:T(8,128)(2,1)}, u32[]{:S(2)}) copy-start(bf16[27,32,32]{2,1,0:T(8,128)(2,1)} %param.15) | copy-start | bytes 165892
  16.2 2.4 %copy-start.6 = (bf16[128,256]{1,0:T(8,128)(2,1)S(1)}, bf16[128,256]{1,0:T(8,128)(2,1)}, u32[]{:S(2)}) copy-start(bf16[128,256]{1,0:T(8,128)(2,1)} %param.17) | copy-start | bytes 196612
  16.3 3.0 %copy-start.7 = (bf16[32,128]{1,0:T(8,128)(2,1)S(1)}, bf16[32,128]{1,0:T(8,128)(2,1)}, u32[]{:S(2)}) copy-start(bf16[32,128]{1,0:T(8,128)(2,1)} %param.21) | copy-start | bytes 24580
  16.3 3.7 %copy-start.8 = (f32[32]{0:T(128)S(1)}, f32[32]{0:T(128)}, u32[]{:S(2)}) copy-start(f32[32]{0:T(128)} %param.16) | copy-start | bytes 388
  16.4 4.4 %copy-start.9 = (f32[32]{0:T(128)S(1)}, f32[32]{0:T(128)}, u32[]{:S(2)}) copy-start(f32[32]{0:T(128)} %param.23) | copy-start | bytes 388
  21.4 3.0 %copy-start.2 = (bf16[4,4,80,128]{3,2,1,0:T(8,128)(2,1)S(1)}, bf16[4,4,80,128]{3,2,1,0:T(8,128)(2,1)}, u32[]{:S(2)}) copy-start(bf16[4,4,80,128]{3,2,1,0:T(8,128)(2,1)} %get-tuple-element.9) | copy-start | bytes 983044
  24.6 0.9 %copy-start.1 = (bf16[4,10,80,128]{3,2,1,0:T(8,128)(2,1)}, bf16[4,10,80,128]{3,2,1,0:T(8,128)(2,1)S(1)}, u32[]{:S(2)}) copy-start(bf16[4,10,80,128]{3,2,1,0:T(8,128)(2,1)S(1)} %pad_maximum_fusion.6.own_ref) | copy-start | bytes 2457604
  24.6 0.7 %copy-start.5 = (bf16[40,128]{1,0:T(8,128)(2,1)S(1)}, bf16[40,128]{1,0:T(8,128)(2,1)}, u32[]{:S(2)}) copy-start(bf16[40,128]{1,0:T(8,128)(2,1)} %get-tuple-element.10) | copy-start | bytes 30724
  25.5 11.4 %collective-permute-start.2 = (bf16[2520,128]{1,0:T(8,128)(2,1)S(1)}, bf16[2520,128]{1,0:T(8,128)(2,1)S(1)}, u32[]{:S(2)}, u32[]{:S(2)}) collective-permute-start(bf16[2520,128]{1,0:T(8,128)(2,1)S(1)} %get-tuple-element.20), channel_id=1, source_target_pairs={{0,1},{1,2},{2,3},{3,4},{4,5},{5,6},{6,7},{8,9},{9,10},{10,11},{11... | collective-permute-start | bytes 1935368 | tf_op jit(solution)/shard_map/ppermute | solution.py:259
  29.4 11.8 %collective-permute-start.3 = (bf16[2520,128]{1,0:T(8,128)(2,1)S(1)}, bf16[2520,128]{1,0:T(8,128)(2,1)S(1)}, u32[]{:S(2)}, u32[]{:S(2)}) collective-permute-start(bf16[2520,128]{1,0:T(8,128)(2,1)S(1)} %get-tuple-element.19), channel_id=1, source_target_pairs={{1,0},{2,1},{3,2},{4,3},{5,4},{6,5},{7,6},{9,8},{10,9},{11,10},{12... | collective-permute-start | bytes 1935368 | tf_op jit(solution)/shard_map/ppermute | solution.py:259
where the time goes:
time: 58.3 us; the launch traced here: 58 us
  Pallas kernels  21.2 us (36%)
  starting transfers between devices  13.8 us (24%)
  local copies, waits for them, and re-layouts  12.9 us (22%)
  waiting for transfers between devices  6.79 us (12%)
  other arithmetic  2.14 us (4%)
  between operations  0.89 us (2%)
    pallas_call x1, Pallas kernels, on_device(): pl.pallas_call(main_kernel, out_shape=jax.ShapeDtypeStruct(fine_in.shape,...  15.3 us
    ppermute x4, starting transfers between devices, shifted(): lax.ppermute(value, axis, [(i, i + step) for i in range(peers) if 0 <= i...  13.8 us
    ppermute x4, waiting for transfers between devices, shifted(): lax.ppermute(value, axis, [(i, i + step) for i in range(peers) if 0 <= i...  6.79 us
    another operation x6, local copies, waits for them, and re-layouts, tiled_taps(): return jnp.tile(jnp.transpose(w, (0, 2, 1)), (1, 1, 4))  4.59 us
    pallas_call x1, Pallas kernels, on_device(): pl.pallas_call(weights_kernel, out_shape=[jax.ShapeDtypeStruct((1024, 512...  2.97 us
    pallas_call x1, Pallas kernels, on_device(): pl.pallas_call(pack_kernel, out_shape=[jax.ShapeDtypeStruct((4, 4, Z, LAN...  2.96 us
    another operation x4, local copies, waits for them, and re-layouts, four(): return jnp.tile(bias, 4)[None]  1.34 us
  transfers between devices with their start and end apart: 4, of which 2 were waited for; matrix products, arithmetic and copies ran while one was open for 19% of the time, Pallas kernels for 5%

commit v1 on v0

v1 whole, which is shorter than its diff:
```python
import math

import jax
import jax.numpy as jnp
from jax import lax
from jax.experimental import pallas as pl
from jax.experimental.pallas import tpu as pltpu
from jax.sharding import PartitionSpec as P

F32 = jnp.float32
BF16 = jnp.bfloat16
LANES = 128
ZC = 40
Z = 80
CH = 32
BITS = (0, 1)


def nn(a, b):
    return lax.dot_general(a, b, (((1,), (0,)), ((), ())), preferred_element_type=F32)


def nt(a, b):
    return lax.dot_general(a, b, (((1,), (1,)), ((), ())), preferred_element_type=F32)


def iota(shape, dim):
    return lax.broadcasted_iota(jnp.int32, shape, dim)


def silu(v):
    return v / (1.0 + jnp.exp(-v))


def rounded(v):
    return v.astype(BF16).astype(F32)


UNIT = Z
OWN = 16 * UNIT
SIDE = 12 * UNIT
EDGE = 30 * UNIT


def unpick(rows, cols):
    row = iota((rows, cols), 0)
    return (jnp.where(row < ZC, 2 * row, 2 * row - (Z - 1)) == iota((rows, cols), 1)).astype(F32).astype(BF16)


def pack_kernel(x_ref, m_ref, own_ref, up_ref, dn_ref):
    sel = unpick(Z, Z)
    src = iota((512, LANES), 0)
    y = src & 7
    goal = ((y >> 1) << 7) + ((src >> 8) << 6) + ((y & 1) << 5) + ((src >> 3) & 31) - iota((512, LANES), 1)
    perm = [(goal == LANES * i).astype(F32).astype(BF16) for i in range(4)]
    for cx in range(4):
        halves = []
        for a in BITS:
            x = 2 * cx + a
            tile = x_ref[:, x].astype(F32)
            tile = jnp.where(m_ref[x][None] > 0, tile, 0.0)
            halves.append(nt(sel, tile.reshape(8 * CH, Z).astype(BF16)).astype(BF16))
        both = jnp.concatenate(halves, axis=1)
        for cy in range(4):
            column = nn(both, perm[cy]).astype(BF16)
            at = (4 * cx + cy) * UNIT
            own_ref[at : at + UNIT] = column
            if cy > 0:
                at = (3 * cx + cy - 1) * UNIT
                up_ref[at : at + UNIT] = column
            if cy < 3:
                at = (3 * cx + cy) * UNIT
                dn_ref[at : at + UNIT] = column
    mask = (m_ref[...] > 0).astype(F32).reshape(64, Z).astype(BF16)
    cols = nt(sel, mask)
    cols = jnp.concatenate([cols[:ZC], cols[ZC:]], axis=1).astype(BF16)
    own_ref[OWN : OWN + ZC] = cols
    up_ref[SIDE : SIDE + ZC] = cols
    dn_ref[SIDE : SIDE + ZC] = cols


def mid_kernel(base_ref, own_ref, low_ref, high_ref, far_ref, near_ref):
    for ref, first in ((far_ref, base_ref[0]), (near_ref, 1 - base_ref[0])):
        for i in range(3):
            x = first + i
            at = 10 * i * UNIT
            ref[at : at + 3 * UNIT] = low_ref[pl.ds(pl.multiple_of(x * 3 * UNIT, 3 * UNIT), 3 * UNIT)]
            ref[at + 3 * UNIT : at + 7 * UNIT] = own_ref[pl.ds(pl.multiple_of(x * 4 * UNIT, 4 * UNIT), 4 * UNIT)]
            ref[at + 7 * UNIT : at + 10 * UNIT] = high_ref[pl.ds(pl.multiple_of(x * 3 * UNIT, 3 * UNIT), 3 * UNIT)]
        masks = [low_ref[SIDE : SIDE + ZC], own_ref[OWN : OWN + ZC], high_ref[SIDE : SIDE + ZC]]
        masks = jnp.concatenate([m.astype(F32) for m in masks], axis=0).astype(BF16)
        ref[EDGE : EDGE + 3 * ZC] = masks


def tap_of(out_bit, in_bit, far):
    if far:
        return 2 * (1 - in_bit) if out_bit != in_bit else None
    return in_bit - out_bit + 1


def placed(w_ref, rows, taps, group):
    total = jnp.zeros((CH, LANES), F32)
    for g, tap in enumerate(taps):
        if tap is not None:
            total = jnp.where(group == g, w_ref[rows : rows + CH, LANES * tap : LANES * tap + LANES], total)
    return total


def block(w_ref, rows, group, far_x, far_y, a_in, b_in, cz_in, shifted, cz_out):
    if shifted:
        tz = None
        if cz_out == 0 and cz_in == 1:
            tz = 0
        if cz_out == 1 and cz_in == 0:
            tz = 2
    else:
        tz = cz_in - cz_out + 1
    taps = []
    for a_out in BITS:
        for b_out in BITS:
            tx = tap_of(a_out, a_in, far_x)
            ty = tap_of(b_out, b_in, far_y)
            taps.append(None if tx is None or ty is None or tz is None else 9 * tx + 3 * ty + tz)
    return placed(w_ref, rows, taps, group)


KINDS = ((0, 0), (1, 0), (0, 1), (1, 1))


def weights_kernel(we_ref, wd_ref, wn_ref, oe_ref, od_ref, on_ref, re_ref, rd_ref, te_ref, td_ref):
    for tap in range(27):
        for g in range(4):
            at = LANES * tap + CH * g
            re_ref[at : at + CH] = we_ref[tap]
            rd_ref[at : at + CH] = wd_ref[tap]
    one = (iota((CH, CH), 0) == iota((CH, CH), 1)).astype(F32).astype(BF16)
    te_ref[...] = nt(one, re_ref[...])
    one = (iota((2 * CH, 2 * CH), 0) == iota((2 * CH, 2 * CH), 1)).astype(F32).astype(BF16)
    td_ref[...] = nt(one, rd_ref[...])
    group = iota((CH, LANES), 1) >> 5
    for w_ref, o_ref in ((te_ref, oe_ref), (td_ref, od_ref)):
        for t, (fx, fy) in enumerate(KINDS):
            for cz in BITS:
                for a in BITS:
                    for b in BITS:
                        base = 256 * t + 128 * cz + 64 * a + 32 * b
                        for s in BITS:
                            for co in BITS:
                                v = block(w_ref, 0, group, fx, fy, a, b, cz, s, co)
                                o_ref[base : base + CH, 256 * s + 128 * co : 256 * s + 128 * co + LANES] = v.astype(BF16)
    for t, (fx, fy) in enumerate(KINDS):
        for a in BITS:
            for b in BITS:
                base = 1024 + 128 * t + 64 * a + 32 * b
                for s in BITS:
                    for co in BITS:
                        v = block(td_ref, CH, group, fx, fy, a, b, 0, s, co)
                        v = v + block(td_ref, CH, group, fx, fy, a, b, 1, s, co)
                        od_ref[base : base + CH, 256 * s + 128 * co : 256 * s + 128 * co + LANES] = v.astype(BF16)
    k = iota((8 * CH, LANES), 0)
    goal = (((k >> 5) & 1) << 7) + ((k >> 6) << 5) + (k & 31) - iota((8 * CH, LANES), 1)
    perm = jnp.concatenate([(goal == LANES * i).astype(F32).astype(BF16) for i in BITS], axis=1)
    on_ref[...] = nn(wn_ref[...], perm).astype(BF16)


def moved(t, amount, edge):
    rows = t.shape[0]
    return jnp.where(edge, 0.0, pltpu.roll(t, amount % rows, 0))


def depth_of(rows):
    return iota((rows, LANES), 0) % ZC


def quad(bias):
    return jnp.concatenate([bias] * 4, axis=1)


def load_own(own_ref, low_ref, high_ref, a_ref, planes):
    for x in planes:
        for yi in range(10):
            if yi < 3:
                v = low_ref[(3 * x + yi) * UNIT : (3 * x + yi + 1) * UNIT]
            elif yi < 7:
                v = own_ref[(4 * x + yi - 3) * UNIT : (4 * x + yi - 2) * UNIT]
            else:
                v = high_ref[(3 * x + yi - 7) * UNIT : (3 * x + yi - 6) * UNIT]
            v = v.astype(F32)
            for cz in BITS:
                a_ref[3 + x, cz, yi * ZC : (yi + 1) * ZC] = v[cz * ZC : (cz + 1) * ZC]


def load_side(ref, start, a_ref):
    for i in range(3):
        for yi in range(10):
            v = ref[(10 * i + yi) * UNIT : (10 * i + yi + 1) * UNIT].astype(F32)
            for cz in BITS:
                a_ref[start + i, cz, yi * ZC : (yi + 1) * ZC] = v[cz * ZC : (cz + 1) * ZC]


def load_masks(at, parts, k_ref):
    for by, part in enumerate(parts):
        k = part.astype(F32)
        m = jnp.maximum(k, pltpu.roll(k, LANES - 1, 1))
        m = jnp.maximum(m, pltpu.roll(m, LANES - 8, 1))
        m = jnp.maximum(m, pltpu.roll(m, LANES - 64, 1))
        k_ref[0, at, by] = k
        k_ref[1, at, by] = m


def spread(k, index):
    parts = [jnp.take_along_axis(k[8 * i : 8 * i + 8], index, axis=1, mode="promise_in_bounds") for i in range(5)]
    return jnp.concatenate(parts, axis=0)


def local(i):
    return (i + 1) >> 2, (i + 1) & 3


def side_select(a_ref, v_ref, x):
    low_b = (iota((320, LANES), 1) & 32) == 0
    for cz in BITS:
        v_ref[x, cz] = jnp.where(low_b, a_ref[x, cz, 80:400], a_ref[x, cz, 0:320])


def encode(xi, a_ref, v_ref, k_ref, l_ref, e_ref, c_ref, o_ref, we_ref, be, wn_ref, gain, shift):
    low_a = iota((320, LANES), 1) < 64
    z8 = depth_of(320)
    first, last = z8 == 0, z8 == ZC - 1
    lane = iota((8, LANES), 1)
    lane_at = 8 * (lane >> 6) + ((lane >> 5) & 1)
    for cz in BITS:
        l_ref[:, 128 * cz : 128 * cz + 128] = a_ref[xi, cz, 40:360].astype(BF16)
        l_ref[:, 256 + 128 * cz : 384 + 128 * cz] = jnp.where(
            low_a, a_ref[xi + 1, cz, 40:360], a_ref[xi - 1, cz, 40:360]
        ).astype(BF16)
        l_ref[:, 512 + 128 * cz : 640 + 128 * cz] = v_ref[xi, cz].astype(BF16)
        l_ref[:, 768 + 128 * cz : 896 + 128 * cz] = jnp.where(low_a, v_ref[xi + 1, cz], v_ref[xi - 1, cz]).astype(BF16)
    o = nn(l_ref[:, 0:1024], we_ref[...])
    bx, lx = local(xi)
    expanded = [[], []]
    on = []
    for yi in range(1, 9):
        by, ly = local(yi)
        k = k_ref[0, bx, by]
        for cz in BITS:
            expanded[cz].append(spread(k, lane_at + (64 * cz + 2 * ly + 16 * lx)))
        on.append(spread(k_ref[1, bx, by], lane * 0 + (2 * ly + 16 * lx)))
    on = jnp.concatenate(on, axis=0)
    pre = (
        o[:, 0:128] + moved(o[:, 256:384], 1, first) + be,
        o[:, 128:256] + moved(o[:, 384:512], -1, last) + be,
    )
    enc = []
    for cz in BITS:
        active = jnp.concatenate(expanded[cz], axis=0) > 0.5
        e = jnp.where(active, silu(pre[cz]), 0.0)
        enc.append(e.astype(BF16))
        e_ref[xi - 1, cz] = rounded(e)[40:280]
    lifted = nt(jnp.concatenate(enc, axis=1), wn_ref[...])
    c = jnp.where(on > 0.5, silu(lifted * gain + shift), 0.0)
    c_ref[xi - 1] = rounded(c)
    o_ref[xi - 1] = on[40:280]


PAIRS = [(dx, dy) for dx in range(3) for dy in range(3)]


def coarse(xo, c_ref, o_ref, u_ref, wc_ref, bc, wu_ref):
    z6 = depth_of(240)
    first, last = z6 == 0, z6 == ZC - 1
    p = None
    for i in range(0, 9, 2):
        some = PAIRS[i : i + 2]
        lhs = [c_ref[xo + dx, dy * ZC : dy * ZC + 240].astype(BF16) for dx, dy in some]
        rhs = [wc_ref[9 * dx + 3 * dy : 9 * dx + 3 * dy + 3].reshape(384, 128) for dx, dy in some]
        lhs = jnp.concatenate(lhs, axis=1) if len(lhs) > 1 else lhs[0]
        rhs = jnp.concatenate(rhs, axis=1) if len(rhs) > 1 else rhs[0]
        q = nt(lhs, rhs)
        p = q if p is None else p + q
    s = p[:, 128:256] + moved(p[:, 0:128], 1, first) + moved(p[:, 256:384], -1, last) + bc
    act = jnp.where(o_ref[xo + 1] > 0.5, silu(s), 0.0).astype(BF16)
    u_ref[xo] = rounded(nt(act, jnp.concatenate([wu_ref[...]] * 4, axis=0)))


def near_kernel(
    near_ref_index, own_ref, low_ref, high_ref, side_ref, we_ref, be_ref, wn_ref, gain_ref, shift_ref, wc_ref, bc_ref,
    wu_ref, e_ref, c_ref, o_ref, u_ref, a_ref, v_ref, k_ref, l_ref,
):
    even = near_ref_index[0]
    load_own(own_ref, low_ref, high_ref, a_ref, range(4))
    load_side(side_ref, 7 * even, a_ref)
    load_masks(1, (low_ref[SIDE : SIDE + ZC], own_ref[OWN : OWN + ZC], high_ref[SIDE : SIDE + ZC]), k_ref)
    masks = side_ref[EDGE : EDGE + 3 * ZC].astype(F32)
    load_masks(2 * even, [masks[ZC * i : ZC * i + ZC] for i in range(3)], k_ref)
    start = 3 * even
    for i in range(7):
        side_select(a_ref, v_ref, start + i)
    be = quad(be_ref[...])
    for i in range(5):
        encode(
            start + 1 + i, a_ref, v_ref, k_ref, l_ref, e_ref, c_ref, o_ref, we_ref, be, wn_ref, gain_ref[...], shift_ref[...]
        )
    for i in range(3):
        coarse(start + i, c_ref, o_ref, u_ref, wc_ref, bc_ref[...], wu_ref)


def far_kernel(
    near_ref_index, own_ref, low_ref, high_ref, side_ref, we_ref, be_ref, wn_ref, gain_ref, shift_ref, wc_ref, bc_ref,
    wu_ref, e1_ref, c1_ref, o1_ref, u1_ref, m_ref, wd_ref, bd_ref, out_ref, a_ref, v_ref, k_ref, l_ref, e_ref, c_ref,
    o_ref, u_ref,
):
    even = near_ref_index[0]
    odd = 1 - even
    load_own(own_ref, low_ref, high_ref, a_ref, range(4))
    load_side(side_ref, 7 * odd, a_ref)
    load_masks(1, (low_ref[SIDE : SIDE + ZC], own_ref[OWN : OWN + ZC], high_ref[SIDE : SIDE + ZC]), k_ref)
    masks = side_ref[EDGE : EDGE + 3 * ZC].astype(F32)
    load_masks(2 * odd, [masks[ZC * i : ZC * i + ZC] for i in range(3)], k_ref)
    start = 5 * odd
    for i in range(5):
        side_select(a_ref, v_ref, start + i)
    be = quad(be_ref[...])
    for i in range(5):
        e_ref[3 * even + i] = e1_ref[3 * even + i]
        c_ref[3 * even + i] = c1_ref[3 * even + i]
        o_ref[3 * even + i] = o1_ref[3 * even + i]
    for i in range(3):
        u_ref[3 * even + i] = u1_ref[3 * even + i]
    for i in range(3):
        encode(
            start + 1 + i, a_ref, v_ref, k_ref, l_ref, e_ref, c_ref, o_ref, we_ref, be, wn_ref, gain_ref[...], shift_ref[...]
        )
    for i in range(3):
        coarse(3 * odd + i, c_ref, o_ref, u_ref, wc_ref, bc_ref[...], wu_ref)
    z4 = depth_of(160)
    first4, last4 = z4 == 0, z4 == ZC - 1
    la4 = iota((160, LANES), 1) < 64
    lb4 = (iota((160, LANES), 1) & 32) == 0
    bd = quad(bd_ref[...])

    def spans(load):
        mid = [load(i)[40:200] for i in range(3)]
        side = [jnp.where(lb4, load(i)[80:240], load(i)[0:160]) for i in range(3)]
        return mid[1], jnp.where(la4, mid[2], mid[0]), side[1], jnp.where(la4, side[2], side[0])

    back = unpick(LANES, Z)
    src = iota((512, LANES), 0)
    goal = (((src >> 6) & 1) << 8) + ((src & 31) << 3) + ((src >> 7) << 1) + ((src >> 5) & 1) - iota((512, LANES), 1)
    perm = jnp.concatenate([(goal == LANES * i).astype(F32).astype(BF16) for i in range(4)], axis=1)
    for xo in range(4):
        for cz in BITS:
            for t, v in enumerate(spans(lambda i: e_ref[xo + 1 + i, cz])):
                l_ref[0:160, 256 * t + 128 * cz : 256 * t + 128 * cz + 128] = v.astype(BF16)
        for t, v in enumerate(spans(lambda i: u_ref[xo + i])):
            l_ref[0:160, 1024 + 128 * t : 1152 + 128 * t] = v.astype(BF16)
        o = nn(l_ref[0:160, :], wd_ref[...])
        d0 = o[:, 0:128] + moved(o[:, 256:384], 1, first4) + bd
        d1 = o[:, 128:256] + moved(o[:, 384:512], -1, last4) + bd
        d = [jnp.concatenate([v[ZC * y : ZC * y + ZC] for y in range(4)], axis=1) for v in (d0, d1)]
        d = jnp.concatenate(d + [jnp.zeros((LANES - Z, 512), F32)], axis=0).astype(BF16)
        d = nn(d, perm)
        for a in BITS:
            t = jnp.transpose(d[:, 256 * a : 256 * a + 256]).astype(BF16)
            t = nn(t, back).reshape(CH, 8, Z)
            x = 2 * xo + a
            out_ref[:, x] = jnp.where(m_ref[x][None] > 0, t, 0.0).astype(BF16)


def vmem(n):
    return [pl.BlockSpec(memory_space=pltpu.VMEM)] * n


def call(kernel, outs, ins, scratch, mib, flops, name, scalar=False):
    return pl.pallas_call(
        kernel,
        out_shape=outs,
        in_specs=([pl.BlockSpec(memory_space=pltpu.SMEM)] if scalar else []) + vmem(ins),
        out_specs=vmem(len(outs)),
        scratch_shapes=[pltpu.VMEM(s, d) for s, d in scratch],
        compiler_params=pltpu.CompilerParams(vmem_limit_bytes=mib << 20),
        cost_estimate=pl.CostEstimate(flops=flops, bytes_accessed=10**6, transcendentals=0),
        name=name,
    )


def rows(n):
    return jax.ShapeDtypeStruct((n, LANES), BF16)


def shifted(value, axis, step):
    peers = lax.axis_size(axis)
    return lax.ppermute(value, axis, [(i, i + step) for i in range(peers) if 0 <= i + step < peers])


def swapped(value, axis, first):
    peers = lax.axis_size(axis)
    pairs = []
    for i in range(first, peers - 1, 2):
        pairs += [(i, i + 1), (i + 1, i)]
    return lax.ppermute(value, axis, pairs)


def time_features(timestep, embed_width):
    halves = embed_width // 2
    freqs = jnp.exp(-math.log(10000.0) * jnp.arange(halves, dtype=F32) / halves)
    angles = timestep[0].astype(F32) * freqs
    return jnp.concatenate([jnp.sin(angles), jnp.cos(angles)]).astype(BF16)


def on_device(
    fine_in, voxel_mask, timestep, w_enc, b_enc, w_down, w_time, w_coarse, b_coarse, w_up, w_dec, b_dec
):
    own, up, down = call(
        pack_kernel, [rows(OWN + ZC), rows(SIDE + ZC), rows(SIDE + ZC)], 2, [], 12, 10**9, "pack"
    )(fine_in, voxel_mask)
    low = shifted(up, "wide", 1)
    high = shifted(down, "wide", -1)

    embedded = time_features(timestep, w_time.shape[0])
    film = jnp.dot(embedded[None], w_time, preferred_element_type=F32)
    chans = w_down.shape[0]
    gains = 1.0 + film[:, :chans]
    shifts = film[:, chans:]
    enc_w, dec_w, down_w = call(
        weights_kernel,
        [
            jax.ShapeDtypeStruct((1024, 512), BF16),
            jax.ShapeDtypeStruct((1536, 512), BF16),
            jax.ShapeDtypeStruct((128, 256), BF16),
        ],
        3,
        [((27 * 128, 32), BF16), ((27 * 128, 64), BF16), ((32, 27 * 128), F32), ((64, 27 * 128), F32)],
        16,
        4 * 10**9,
        "weights",
    )(w_enc, w_dec, w_down)

    odd = lax.axis_index("narrow").astype(jnp.int32) & 1
    far_base = odd[None]
    near_right = 1 - far_base
    far, near = call(
        mid_kernel, [rows(EDGE + 3 * ZC), rows(EDGE + 3 * ZC)], 3, [], 8, 10**8, "mid", scalar=True
    )(far_base, own, low, high)
    far_side = swapped(far, "narrow", 1)
    near_side = swapped(near, "narrow", 0)

    planes = [((10, 2, 400, LANES), F32), ((10, 2, 320, LANES), F32), ((2, 3, 3, ZC, LANES), F32)]
    shared = [((8, 2, 240, LANES), F32), ((8, 320, LANES), F32), ((8, 240, LANES), F32), ((6, 240, LANES), F32)]
    some = (enc_w, b_enc[None], down_w, gains, shifts, w_coarse, b_coarse[None], w_up)
    state = call(
        near_kernel,
        [jax.ShapeDtypeStruct(s, d) for s, d in shared],
        12,
        planes + [((320, 1024), BF16)],
        24,
        5 * 10**9,
        "near",
        scalar=True,
    )(near_right, own, low, high, near_side, *some)
    return call(
        far_kernel,
        [jax.ShapeDtypeStruct(fine_in.shape, BF16)],
        19,
        planes + [((320, 1536), BF16)] + shared,
        30,
        5 * 10**9,
        "far",
        scalar=True,
    )(near_right, own, low, high, far_side, *some, *state, voxel_mask, dec_w, b_dec[None])[0]


def solution(mesh):
    field = P(None, "narrow", "wide", None)
    return jax.shard_map(
        on_device,
        mesh=mesh,
        in_specs=(field, P("narrow", "wide", None)) + (P(),) * 10,
        out_specs=field,
        check_vma=False,
    )
```

time: 58.3 us -> 40.8 us (0.70)
  the two profiles are of different devices: /device:TPU:25 before, /device:TPU:1 now
where the time goes in v1:
time: 40.8 us; the launch traced here: 40.5 us
  Pallas kernels  17.7 us (43%)
  starting transfers between devices  10.6 us (26%)
  waiting for transfers between devices  9.32 us (23%)
  local copies, waits for them, and re-layouts  1.88 us (5%)
  between operations  0.81 us (2%)
    pallas_call x1, Pallas kernels, on_device(): call(far_kernel, [jax.ShapeDtypeStruct(fine_in.shape, BF16)], 19, planes...  9.13 us
    ppermute x2, waiting for transfers between devices, shifted(): lax.ppermute(value, axis, [(i, i + step) for i in range(peers) if 0 <= i...  7.01 us
    pallas_call x1, Pallas kernels, on_device(): call(near_kernel, [jax.ShapeDtypeStruct(s, d) for s, d in shared], 12, pl...  6.17 us
    ppermute x2, starting transfers between devices, shifted(): lax.ppermute(value, axis, [(i, i + step) for i in range(peers) if 0 <= i...  5.68 us
    ppermute x2, starting transfers between devices, swapped(): return lax.ppermute(value, axis, pairs)  4.93 us
    ppermute x2, waiting for transfers between devices, swapped(): return lax.ppermute(value, axis, pairs)  2.31 us
    unnamed x24, local copies, waits for them, and re-layouts  1.88 us
    pallas_call x1, Pallas kernels, on_device(): call(pack_kernel, [rows(OWN + ZC), rows(SIDE + ZC), rows(SIDE + ZC)], 2,...  1.2 us
  transfers between devices with their start and end apart: 4, of which 3 were waited for; matrix products, arithmetic and copies ran while one was open for 1% of the time, Pallas kernels for 18%

profile of v1, /device:TPU:1, one launch (start us, length us, event | category | flops | bytes accessed | tf_op | source)
XLA Modules:
  0.0 40.5 jit_solution(12280349615541741633)
XLA Ops:
  0.0 1.1 %copy-done.2 = bf16[32,8,8,80]{3,2,1,0:T(8,128)(2,1)S(1)} copy-done((bf16[32,8,8,80]{3,2,1,0:T(8,128)(2,1)S(1)}, bf16[32,8,8,80]{3,2,1,0:T(8,128)(2,1)}, u32[]{:S(2)}) %copy-start.2) | copy-done | bytes 327704
  1.1 0.8 %copy-done.6 = s32[8,8,80]{2,1,0:T(8,128)S(1)} copy-done((s32[8,8,80]{2,1,0:T(8,128)S(1)}, s32[8,8,80]{2,1,0:T(8,128)}, u32[]{:S(2)}) %copy-start.6) | copy-done | bytes 20504
  1.8 1.2 %pack.1 = (bf16[1320,128]{1,0:T(8,128)(2,1)S(1)}, bf16[1000,128]{1,0:T(8,128)(2,1)S(1)}, bf16[1000,128]{1,0:T(8,128)(2,1)S(1)}) custom-call(bf16[32,8,8,80]{3,2,1,0:T(8,128)(2,1)S(1)} %copy-done.2, s32[8,8,80]{2,1,0:T(8,128)S(1)} %copy-done.6), custom_call_target="tpu_custom_call" | custom-call | flops 1000000000 | bytes 1000000 | tf_op jit(solution)/shard_map/pack/pallas_call | solution.py:414
  3.0 4.4 %collective-permute-start = (bf16[1000,128]{1,0:T(8,128)(2,1)S(1)}, bf16[1000,128]{1,0:T(8,128)(2,1)S(1)}, u32[]{:S(2)}, u32[]{:S(2)}) collective-permute-start(bf16[1000,128]{1,0:T(8,128)(2,1)S(1)} %get-tuple-element.18), channel_id=1, source_target_pairs={{0,8},{8,16},{16,24},{24,32},{32,40},{40,48},{48,56},{56,64},{64,7... | collective-permute-start | bytes 768008 | tf_op jit(solution)/shard_map/ppermute | solution.py:393
  7.4 1.3 %collective-permute-start.1 = (bf16[1000,128]{1,0:T(8,128)(2,1)S(1)}, bf16[1000,128]{1,0:T(8,128)(2,1)S(1)}, u32[]{:S(2)}, u32[]{:S(2)}) collective-permute-start(bf16[1000,128]{1,0:T(8,128)(2,1)S(1)} %get-tuple-element.19), channel_id=1, source_target_pairs={{8,0},{16,8},{24,16},{32,24},{40,32},{48,40},{56,48},{64,56},{72,6... | collective-permute-start | bytes 768008 | tf_op jit(solution)/shard_map/ppermute | solution.py:393
  9.4 0.1 cosine_convert_fusion
  9.4 2.8 %collective-permute-done.low_ref = bf16[1000,128]{1,0:T(8,128)(2,1)S(1)} collective-permute-done((bf16[1000,128]{1,0:T(8,128)(2,1)S(1)}, bf16[1000,128]{1,0:T(8,128)(2,1)S(1)}, u32[]{:S(2)}, u32[]{:S(2)}) %collective-permute-start) | collective-permute-done | bytes 256032 | tf_op jit(solution)/shard_map/ppermute | solution.py:393
  12.3 4.2 %collective-permute-done.1.high_ref = bf16[1000,128]{1,0:T(8,128)(2,1)S(1)} collective-permute-done((bf16[1000,128]{1,0:T(8,128)(2,1)S(1)}, bf16[1000,128]{1,0:T(8,128)(2,1)S(1)}, u32[]{:S(2)}, u32[]{:S(2)}) %collective-permute-start.1) | collective-permute-done | bytes 256032 | tf_op jit(solution)/shard_map/ppermute | solution.py:393
  16.5 0.1 mid.1
  16.6 1.7 %collective-permute-start.3 = (bf16[2520,128]{1,0:T(8,128)(2,1)S(1)}, bf16[2520,128]{1,0:T(8,128)(2,1)S(1)}, u32[]{:S(2)}, u32[]{:S(2)}) collective-permute-start(bf16[2520,128]{1,0:T(8,128)(2,1)S(1)} %get-tuple-element.23), channel_id=1, source_target_pairs={{0,1},{1,0},{2,3},{3,2},{4,5},{5,4},{6,7},{7,6},{8,9},{9,8},{10,11... | collective-permute-start | bytes 1935368 | tf_op jit(solution)/shard_map/ppermute | solution.py:401
  18.3 0.2 fusion
  18.5 0.0 copy-done.4
  18.5 0.0 copy-start.1
  18.5 0.0 copy-start.8
  18.5 0.0 copy-start.9
  18.5 0.0 copy-start.10
  18.5 1.1 %weights.1 = (bf16[1024,512]{1,0:T(8,128)(2,1)S(1)}, bf16[1536,512]{1,0:T(8,128)(2,1)S(1)}, bf16[128,256]{1,0:T(8,128)(2,1)S(1)}) custom-call(bf16[27,32,32]{2,1,0:T(8,128)(2,1)S(1)} %copy-done.3, bf16[27,32,64]{2,1,0:T(8,128)(2,1)S(1)} %copy-done.4, bf16[128,256]{1,0:T(8,128)(2,1)S(1)} %copy-done.5), custom_call_target="tpu_custom_call" | custom-call | flops 4000000000 | bytes 1000000 | tf_op jit(solution)/shard_map/weights/pallas_call | solution.py:425
  19.6 3.2 %collective-permute-start.2 = (bf16[2520,128]{1,0:T(8,128)(2,1)S(1)}, bf16[2520,128]{1,0:T(8,128)(2,1)S(1)}, u32[]{:S(2)}, u32[]{:S(2)}) collective-permute-start(bf16[2520,128]{1,0:T(8,128)(2,1)S(1)} %get-tuple-element.20), channel_id=1, source_target_pairs={{1,2},{2,1},{3,4},{4,3},{5,6},{6,5},{9,10},{10,9},{11,12},{12,11},... | collective-permute-start | bytes 1935368 | tf_op jit(solution)/shard_map/ppermute | solution.py:401
  22.8 0.0 collective-permute-done.3.side_ref
  22.9 0.0 copy-start.7
  22.9 0.0 copy-start.11
  22.9 6.2 %near.1 = (f32[8,2,240,128]{3,2,1,0:T(8,128)S(1)}, f32[8,320,128]{2,1,0:T(8,128)S(1)}, f32[8,240,128]{2,1,0:T(8,128)S(1)}, f32[6,240,128]{2,1,0:T(8,128)S(1)}) custom-call(s32[1]{0:T(128)S(6)} %sub.3.near_ref_index, bf16[1320,128]{1,0:T(8,128)(2,1)S(1)} %get-tuple-element.17.own_ref, bf16[1000,128]{1,0:T(8,128)(2,1)S(1)} %collective-permute-done.low_ref, ...), custom_call_target="tpu_custom_call" | custom-call | flops 5000000000 | bytes 1000000 | tf_op jit(solution)/shard_map/near/pallas_call | solution.py:451
  29.1 2.3 %collective-permute-done.2.side_ref = bf16[2520,128]{1,0:T(8,128)(2,1)S(1)} collective-permute-done((bf16[2520,128]{1,0:T(8,128)(2,1)S(1)}, bf16[2520,128]{1,0:T(8,128)(2,1)S(1)}, u32[]{:S(2)}, u32[]{:S(2)}) %collective-permute-start.2) | collective-permute-done | bytes 645152 | tf_op jit(solution)/shard_map/ppermute | solution.py:401
  31.4 9.1 %far.1 = bf16[32,8,8,80]{3,2,1,0:T(8,128)(2,1)} custom-call(s32[1]{0:T(128)S(6)} %sub.3.near_ref_index, bf16[1320,128]{1,0:T(8,128)(2,1)S(1)} %get-tuple-element.17.own_ref, bf16[1000,128]{1,0:T(8,128)(2,1)S(1)} %collective-permute-done.low_ref, bf16[1000,128]{1,0:T(8,128)(2,1)S(1)} %collective-permute-done.1.high_ref, ...), custom_call_target="tpu_custom_call" | custom-call | flops 5000000000 | bytes 1000000 | tf_op jit(solution)/shard_map/far/pallas_call | solution.py:461
  (16 shorter events, 0.0 us)
Async XLA Ops:
  0.0 18.3 %copy-start = (bf16[128,256]{1,0:T(8,128)(2,1)S(1)}, bf16[128,256]{1,0:T(8,128)(2,1)}, u32[]{:S(2)}) copy-start(bf16[128,256]{1,0:T(8,128)(2,1)} %param.18) | copy-start | bytes 196612
  0.0 1.1 %copy-start.2 = (bf16[32,8,8,80]{3,2,1,0:T(8,128)(2,1)S(1)}, bf16[32,8,8,80]{3,2,1,0:T(8,128)(2,1)}, u32[]{:S(2)}) copy-start(bf16[32,8,8,80]{3,2,1,0:T(8,128)(2,1)} %x_ref.1) | copy-start | bytes 983044
  1.1 0.8 %copy-start.6 = (s32[8,8,80]{2,1,0:T(8,128)S(1)}, s32[8,8,80]{2,1,0:T(8,128)}, u32[]{:S(2)}) copy-start(s32[8,8,80]{2,1,0:T(8,128)} %m_ref.3) | copy-start | bytes 61444
  1.8 16.6 %copy-start.3 = (bf16[27,32,32]{2,1,0:T(8,128)(2,1)S(1)}, bf16[27,32,32]{2,1,0:T(8,128)(2,1)}, u32[]{:S(2)}) copy-start(bf16[27,32,32]{2,1,0:T(8,128)(2,1)} %we_ref.1) | copy-start | bytes 165892
  1.8 16.6 %copy-start.4 = (bf16[27,32,64]{2,1,0:T(8,128)(2,1)S(1)}, bf16[27,32,64]{2,1,0:T(8,128)(2,1)}, u32[]{:S(2)}) copy-start(bf16[27,32,64]{2,1,0:T(8,128)(2,1)} %wd_ref.1) | copy-start | bytes 331780
  1.8 16.6 %copy-start.5 = (bf16[128,256]{1,0:T(8,128)(2,1)S(1)}, bf16[128,256]{1,0:T(8,128)(2,1)}, u32[]{:S(2)}) copy-start(bf16[128,256]{1,0:T(8,128)(2,1)} %wn_ref.1) | copy-start | bytes 196612
  3.0 9.2 %collective-permute-start = (bf16[1000,128]{1,0:T(8,128)(2,1)S(1)}, bf16[1000,128]{1,0:T(8,128)(2,1)S(1)}, u32[]{:S(2)}, u32[]{:S(2)}) collective-permute-start(bf16[1000,128]{1,0:T(8,128)(2,1)S(1)} %get-tuple-element.18), channel_id=1, source_target_pairs={{0,8},{8,16},{16,24},{24,32},{32,40},{40,48},{48,56},{56,64},{64,7... | collective-permute-start | bytes 768008 | tf_op jit(solution)/shard_map/ppermute | solution.py:393
  7.4 9.0 %collective-permute-start.1 = (bf16[1000,128]{1,0:T(8,128)(2,1)S(1)}, bf16[1000,128]{1,0:T(8,128)(2,1)S(1)}, u32[]{:S(2)}, u32[]{:S(2)}) collective-permute-start(bf16[1000,128]{1,0:T(8,128)(2,1)S(1)} %get-tuple-element.19), channel_id=1, source_target_pairs={{8,0},{16,8},{24,16},{32,24},{40,32},{48,40},{56,48},{64,56},{72,6... | collective-permute-start | bytes 768008 | tf_op jit(solution)/shard_map/ppermute | solution.py:393
  16.6 6.3 %collective-permute-start.3 = (bf16[2520,128]{1,0:T(8,128)(2,1)S(1)}, bf16[2520,128]{1,0:T(8,128)(2,1)S(1)}, u32[]{:S(2)}, u32[]{:S(2)}) collective-permute-start(bf16[2520,128]{1,0:T(8,128)(2,1)S(1)} %get-tuple-element.23), channel_id=1, source_target_pairs={{0,1},{1,0},{2,3},{3,2},{4,5},{5,4},{6,7},{7,6},{8,9},{9,8},{10,11... | collective-permute-start | bytes 1935368 | tf_op jit(solution)/shard_map/ppermute | solution.py:401
  18.5 4.4 %copy-start.1 = (bf16[27,128,128]{2,1,0:T(8,128)(2,1)S(1)}, bf16[27,128,128]{2,1,0:T(8,128)(2,1)}, u32[]{:S(2)}) copy-start(bf16[27,128,128]{2,1,0:T(8,128)(2,1)} %wc_ref.3) | copy-start | bytes 2654212
  18.5 4.4 %copy-start.8 = (bf16[32,128]{1,0:T(8,128)(2,1)S(1)}, bf16[32,128]{1,0:T(8,128)(2,1)}, u32[]{:S(2)}) copy-start(bf16[32,128]{1,0:T(8,128)(2,1)} %wu_ref.3) | copy-start | bytes 24580
  18.5 4.4 %copy-start.9 = (f32[32]{0:T(128)S(1)}, f32[32]{0:T(128)}, u32[]{:S(2)}) copy-start(f32[32]{0:T(128)} %param.16) | copy-start | bytes 388
  18.5 4.3 %copy-start.10 = (f32[128]{0:T(128)S(1)}, f32[128]{0:T(128)}, u32[]{:S(2)}) copy-start(f32[128]{0:T(128)} %param.20) | copy-start | bytes 1540
  19.6 11.8 %collective-permute-start.2 = (bf16[2520,128]{1,0:T(8,128)(2,1)S(1)}, bf16[2520,128]{1,0:T(8,128)(2,1)S(1)}, u32[]{:S(2)}, u32[]{:S(2)}) collective-permute-start(bf16[2520,128]{1,0:T(8,128)(2,1)S(1)} %get-tuple-element.20), channel_id=1, source_target_pairs={{1,2},{2,1},{3,4},{4,3},{5,6},{6,5},{9,10},{10,9},{11,12},{12,11},... | collective-permute-start | bytes 1935368 | tf_op jit(solution)/shard_map/ppermute | solution.py:401
  22.9 8.5 %copy-start.7 = (s32[8,8,80]{2,1,0:T(8,128)S(1)}, s32[8,8,80]{2,1,0:T(8,128)}, u32[]{:S(2)}) copy-start(s32[8,8,80]{2,1,0:T(8,128)} %m_ref.3) | copy-start | bytes 61444
  22.9 8.5 %copy-start.11 = (f32[32]{0:T(128)S(1)}, f32[32]{0:T(128)}, u32[]{:S(2)}) copy-start(f32[32]{0:T(128)} %param.23) | copy-start | bytes 388

commit v2 on v1

v2 whole, which is shorter than its diff:
```python
import math

import jax
import jax.numpy as jnp
from jax import lax
from jax.experimental import pallas as pl
from jax.experimental.pallas import tpu as pltpu
from jax.sharding import PartitionSpec as P


F32 = jnp.float32
BF16 = jnp.bfloat16
LANES = 128
ZC = 40
Z = 80
CH = 32
BITS = (0, 1)


def nn(a, b):
    return lax.dot_general(a, b, (((1,), (0,)), ((), ())), preferred_element_type=F32)


def nt(a, b):
    return lax.dot_general(a, b, (((1,), (1,)), ((), ())), preferred_element_type=F32)


def iota(shape, dim):
    return lax.broadcasted_iota(jnp.int32, shape, dim)


PAIR = 2 * ZC
OWN = 16 * PAIR
SIDE = 8 * PAIR
SIDE_MASK = SIDE + 4 * ZC
SIDE_ROWS = SIDE_MASK + ZC
PLANE = 9 * PAIR
HALF = 5 * PAIR
EDGE_MASK = 2 * PLANE + HALF
EDGE_ROWS = EDGE_MASK + 3 * ZC


def one_where(truth):
    return truth.astype(F32).astype(BF16)


def unpick(rows, cols):
    row = iota((rows, cols), 0)
    return one_where(jnp.where(row < ZC, 2 * row, 2 * row - (Z - 1)) == iota((rows, cols), 1))


def low_a(rows):
    return iota((rows, LANES), 1) < 64


def low_b(rows):
    return (iota((rows, LANES), 1) & 32) == 0


def stacked(*parts):
    return jnp.concatenate(parts, axis=0)


def beside(*parts):
    return jnp.concatenate(parts, axis=1)


def pack_kernel(x_hbm, m_hbm, own_ref, up_ref, dn_ref, x_ref, m_ref, sems):
    copies = [pltpu.make_async_copy(m_hbm, m_ref, sems.at[4])]
    for cx in range(4):
        copies.append(pltpu.make_async_copy(x_hbm.at[:, pl.ds(2 * cx, 2)], x_ref.at[:, pl.ds(2 * cx, 2)], sems.at[cx]))
    for copy in copies:
        copy.start()
    sel = unpick(Z, Z)
    src = iota((512, LANES), 0)
    y = src & 7
    goal = ((y >> 1) << 7) + ((src >> 8) << 6) + ((y & 1) << 5) + ((src >> 3) & 31) - iota((512, LANES), 1)
    perm = [one_where(goal == LANES * i) for i in range(4)]
    copies[0].wait()
    mask = (m_ref[...] > 0).astype(F32).reshape(64, Z).astype(BF16)
    cols = nt(sel, mask)
    cols = beside(cols[:ZC], cols[ZC:]).astype(BF16)
    own_ref[OWN : OWN + ZC] = cols
    up_ref[SIDE_MASK:SIDE_ROWS] = cols
    dn_ref[SIDE_MASK:SIDE_ROWS] = cols
    ups, downs = [], []
    for cx in range(4):
        copies[1 + cx].wait()
        halves = []
        for a in BITS:
            x = 2 * cx + a
            tile = x_ref[:, x].astype(F32)
            tile = jnp.where(m_ref[x][None] > 0, tile, 0.0)
            halves.append(nt(sel, tile.reshape(8 * CH, Z).astype(BF16)).astype(BF16))
        both = beside(*halves)
        col = [nn(both, perm[cy]) for cy in range(4)]
        for cz in BITS:
            z = slice(ZC * cz, ZC * cz + ZC)
            first = stacked(col[0][z], col[1][z]).astype(BF16)
            second = stacked(col[2][z], col[3][z]).astype(BF16)
            own_ref[pl.ds((4 * cx + 2 * cz) * PAIR, PAIR)] = first
            own_ref[pl.ds((4 * cx + 2 * cz + 1) * PAIR, PAIR)] = second
            dn_ref[pl.ds((2 * cx + cz) * PAIR, PAIR)] = first
            up_ref[pl.ds((2 * cx + cz) * PAIR, PAIR)] = second
        ups.append(jnp.where(low_b(ZC), pltpu.roll(col[1][ZC:], LANES - 32, 1), col[1][:ZC]))
        downs.append(jnp.where(low_b(ZC), col[2][:ZC], pltpu.roll(col[2][ZC:], 32, 1)))
        if cx % 2 == 1:
            at = pl.ds(SIDE + (cx // 2) * PAIR, PAIR)
            up_ref[at] = stacked(*ups[-2:]).astype(BF16)
            dn_ref[at] = stacked(*downs[-2:]).astype(BF16)


def part(x, size):
    return pl.ds(pl.multiple_of(x * size, size), size)


def mid_kernel(odd_ref, own_ref, low_ref, high_ref, tie_ref, far_ref, near_ref, ends_ref):
    ends_ref[0] = low_ref[SIDE:SIDE_MASK].astype(F32)
    ends_ref[1] = high_ref[SIDE:SIDE_MASK].astype(F32)

    def layer(x, cz):
        return (
            low_ref[pl.ds(pl.multiple_of(x * 2 * PAIR + cz * PAIR, PAIR), PAIR)],
            own_ref[pl.ds(pl.multiple_of(x * 4 * PAIR + 2 * cz * PAIR, PAIR), 2 * PAIR)],
            high_ref[pl.ds(pl.multiple_of(x * 2 * PAIR + cz * PAIR, PAIR), PAIR)],
        )

    def ends(x):
        at = part(x, ZC)
        return stacked(ends_ref[0, at], ends_ref[1, at]).astype(BF16)

    lane_a = iota((PAIR, LANES), 1) >> 6
    for ref, right in ((far_ref, odd_ref[0]), (near_ref, 1 - odd_ref[0])):
        for i in range(2):
            x = 2 * right + i
            for cz in BITS:
                at = i * PLANE + 4 * cz * PAIR
                low, own, high = layer(x, cz)
                ref[at : at + PAIR] = low
                ref[at + PAIR : at + 3 * PAIR] = own
                ref[at + 3 * PAIR : at + 4 * PAIR] = high
            ref[i * PLANE + 8 * PAIR : (i + 1) * PLANE] = ends(x)
        x = 2 - right
        pieces = []
        for cz in BITS:
            low, own, high = layer(x, cz)
            pieces.append([v.astype(F32) for v in (low, own[:PAIR], own[PAIR:], high)])
        for i in range(4):
            v = jnp.where(lane_a == right, pieces[0][i], pltpu.roll(pieces[1][i], 64, 1))
            ref[2 * PLANE + i * PAIR : 2 * PLANE + (i + 1) * PAIR] = v.astype(BF16)
        ref[2 * PLANE + 4 * PAIR : EDGE_MASK] = ends(x)
        masks = [low_ref[SIDE_MASK:SIDE_ROWS], own_ref[OWN : OWN + ZC], high_ref[SIDE_MASK:SIDE_ROWS]]
        ref[EDGE_MASK:EDGE_ROWS] = stacked(*[m.astype(F32) for m in masks]).astype(BF16)


def tap_of(out_bit, in_bit, far):
    if far:
        return 2 * (1 - in_bit) if out_bit != in_bit else None
    return in_bit - out_bit + 1


def placed(w_ref, rows, taps, group):
    total = jnp.zeros((CH, LANES), F32)
    for g, tap in enumerate(taps):
        if tap is not None:
            total = jnp.where(group == g, w_ref[rows : rows + CH, LANES * tap : LANES * tap + LANES], total)
    return total


def block(w_ref, rows, group, far_x, far_y, a_in, b_in, cz_in, shifted, cz_out):
    if shifted:
        tz = None
        if cz_out == 0 and cz_in == 1:
            tz = 0
        if cz_out == 1 and cz_in == 0:
            tz = 2
    else:
        tz = cz_in - cz_out + 1
    taps = []
    for a_out in BITS:
        for b_out in BITS:
            tx = tap_of(a_out, a_in, far_x)
            ty = tap_of(b_out, b_in, far_y)
            taps.append(None if tx is None or ty is None or tz is None else 9 * tx + 3 * ty + tz)
    return placed(w_ref, rows, taps, group)


KINDS = ((0, 0), (1, 0), (0, 1), (1, 1))


def weights_kernel(we_ref, wd_ref, wn_ref, oe_ref, od_ref, on_ref, re_ref, rd_ref, te_ref, td_ref):
    for tap in range(27):
        for g in range(4):
            at = LANES * tap + CH * g
            re_ref[at : at + CH] = we_ref[tap]
            rd_ref[at : at + CH] = wd_ref[tap]
    one = (iota((CH, CH), 0) == iota((CH, CH), 1)).astype(F32).astype(BF16)
    te_ref[...] = nt(one, re_ref[...])
    one = (iota((2 * CH, 2 * CH), 0) == iota((2 * CH, 2 * CH), 1)).astype(F32).astype(BF16)
    td_ref[...] = nt(one, rd_ref[...])
    group = iota((CH, LANES), 1) >> 5
    for w_ref, o_ref in ((te_ref, oe_ref), (td_ref, od_ref)):
        for t, (fx, fy) in enumerate(KINDS):
            for cz in BITS:
                for a in BITS:
                    for b in BITS:
                        base = 256 * t + 128 * cz + 64 * a + 32 * b
                        for s in BITS:
                            for co in BITS:
                                v = block(w_ref, 0, group, fx, fy, a, b, cz, s, co)
                                o_ref[base : base + CH, 256 * s + 128 * co : 256 * s + 128 * co + LANES] = v.astype(BF16)
    for t, (fx, fy) in enumerate(KINDS):
        for a in BITS:
            for b in BITS:
                base = 1024 + 128 * t + 64 * a + 32 * b
                for s in BITS:
                    for co in BITS:
                        v = block(td_ref, CH, group, fx, fy, a, b, 0, s, co)
                        v = v + block(td_ref, CH, group, fx, fy, a, b, 1, s, co)
                        od_ref[base : base + CH, 256 * s + 128 * co : 256 * s + 128 * co + LANES] = v.astype(BF16)
    k = iota((8 * CH, LANES), 0)
    goal = (((k >> 5) & 1) << 7) + ((k >> 6) << 5) + (k & 31) - iota((8 * CH, LANES), 1)
    perm = jnp.concatenate([(goal == LANES * i).astype(F32).astype(BF16) for i in BITS], axis=1)
    on_ref[...] = nn(wn_ref[...], perm).astype(BF16)


def moved(t, amount, edge):
    rows = t.shape[0]
    return jnp.where(edge, 0.0, pltpu.roll(t, amount % rows, 0))


def depth_of(rows):
    return iota((rows, LANES), 0) % ZC


def quad(bias):
    return beside(bias, bias, bias, bias)


def put_plane(a_ref, v_ref, at, layers, ends):
    y0, y9 = ends[:ZC].astype(F32), ends[ZC:].astype(F32)
    for cz in BITS:
        a_ref[at, cz] = layers[cz].astype(BF16)
        f = layers[cz].astype(F32)
        if cz == 1:
            y0, y9 = pltpu.roll(y0, 32, 1), pltpu.roll(y9, LANES - 32, 1)
        f = stacked(y0, f, y9)
        v_ref[at, cz] = jnp.where(low_b(320), f[PAIR:], f[:320]).astype(BF16)


def load_own(own_ref, low_ref, high_ref, a_ref, v_ref):
    low_ends = low_ref[SIDE:SIDE_MASK].astype(F32)
    high_ends = high_ref[SIDE:SIDE_MASK].astype(F32)
    for x in range(4):
        layers = []
        for cz in BITS:
            at = (2 * x + cz) * PAIR
            mine = (4 * x + 2 * cz) * PAIR
            layers.append(
                stacked(low_ref[at : at + PAIR], own_ref[mine : mine + 2 * PAIR], high_ref[at : at + PAIR])
            )
        z = slice(ZC * x, ZC * x + ZC)
        put_plane(a_ref, v_ref, 3 + x, layers, stacked(low_ends[z], high_ends[z]))


def load_side(ref, right, a_ref, v_ref):
    for i in range(2):
        at = i * PLANE
        layers = [ref[at + 320 * cz : at + 320 * cz + 320] for cz in BITS]
        put_plane(a_ref, v_ref, 1 + 6 * right + i, layers, ref[at + 640 : at + PLANE].astype(F32))
    at = 2 * PLANE
    both = ref[at : at + 320].astype(F32)
    put_plane(a_ref, v_ref, 9 * right, [both, pltpu.roll(both, 64, 1)], ref[at + 320 : at + HALF].astype(F32))


def load_masks(at, parts, k_ref):
    for by, k in enumerate(parts):
        k = k.astype(F32)
        m = jnp.maximum(k, pltpu.roll(k, LANES - 1, 1))
        m = jnp.maximum(m, pltpu.roll(m, LANES - 8, 1))
        m = jnp.maximum(m, pltpu.roll(m, LANES - 64, 1))
        k_ref[0, at, by] = k
        k_ref[1, at, by] = m


def load_all(own_ref, low_ref, high_ref, side_ref, right, a_ref, v_ref, k_ref):
    load_own(own_ref, low_ref, high_ref, a_ref, v_ref)
    load_side(side_ref, right, a_ref, v_ref)
    load_masks(1, (low_ref[SIDE_MASK:SIDE_ROWS], own_ref[OWN : OWN + ZC], high_ref[SIDE_MASK:SIDE_ROWS]), k_ref)
    masks = side_ref[EDGE_MASK:EDGE_ROWS].astype(F32)
    load_masks(2 * right, [masks[ZC * i : ZC * i + ZC] for i in range(3)], k_ref)


def spread(k, index):
    return stacked(*[jnp.take_along_axis(k[8 * i : 8 * i + 8], index, axis=1, mode="promise_in_bounds") for i in range(5)])


def local(i):
    return (i + 1) >> 2, (i + 1) & 3


def silu(v):
    half = 0.5 * v
    return half + half * jnp.tanh(half)


def joined_x(ref, x, cz, lane_a, rows):
    return jnp.where(lane_a, ref[x + 1, cz, rows], ref[x - 1, cz, rows])


def lanes_a(rows):
    return one_where(low_a(rows)) > 0.5


def encode(xi, a_ref, v_ref, k_ref, e_ref, ev_ref, c_ref, d_ref, o_ref, we_ref, be, wn_ref, gain, shift):
    z8 = depth_of(320)
    first, last = z8 == 0, z8 == ZC - 1
    lane = iota((8, LANES), 1)
    lane_at = 8 * (lane >> 6) + ((lane >> 5) & 1)
    la = lanes_a(320)
    every = slice(0, 320)
    lhs = [a_ref[xi, cz] for cz in BITS] + [joined_x(a_ref, xi, cz, la, every) for cz in BITS]
    lhs += [v_ref[xi, cz] for cz in BITS] + [joined_x(v_ref, xi, cz, la, every) for cz in BITS]
    o = nn(beside(*lhs), we_ref[...])
    bx, lx = local(xi)
    expanded = [[], []]
    on = []
    for yi in range(1, 9):
        by, ly = local(yi)
        k = k_ref[0, bx, by]
        for cz in BITS:
            expanded[cz].append(spread(k, lane_at + (64 * cz + 2 * ly + 16 * lx)))
        on.append(spread(k_ref[1, bx, by], lane * 0 + (2 * ly + 16 * lx)))
    on = stacked(*on)
    pre = (
        o[:, 0:128] + moved(o[:, 256:384], 1, first) + be,
        o[:, 128:256] + moved(o[:, 384:512], -1, last) + be,
    )
    enc = []
    for cz in BITS:
        e = jnp.where(stacked(*expanded[cz]) > 0.5, silu(pre[cz]), 0.0)
        enc.append(e.astype(BF16))
        e_ref[xi - 1, cz] = enc[cz]
        ev_ref[xi - 1, cz] = jnp.where(low_b(160), e[120:280], e[40:200]).astype(BF16)
    lifted = nt(beside(*enc), wn_ref[...])
    c = jnp.where(on > 0.5, silu(lifted * gain + shift), 0.0)
    c_ref[xi - 1] = c.astype(BF16)
    d_ref[xi - 1] = c[40:280].astype(BF16)
    o_ref[xi - 1] = on[40:280]


def coarse(xo, c_ref, d_ref, o_ref, u_ref, wc_ref, bc, wu_ref):
    z6 = depth_of(240)
    first, last = z6 == 0, z6 == ZC - 1
    lhs, rhs = [], []
    for dx in range(3):
        for dy in range(3):
            lhs.append(d_ref[xo + dx] if dy == 1 else c_ref[xo + dx, 40 * dy : 40 * dy + 240])
            rhs.append(wc_ref[9 * dx + 3 * dy : 9 * dx + 3 * dy + 3].reshape(384, 128))
    p = nt(beside(*lhs), beside(*rhs))
    s = p[:, 128:256] + moved(p[:, 0:128], 1, first) + moved(p[:, 256:384], -1, last) + bc
    act = jnp.where(o_ref[xo + 1] > 0.5, silu(s), 0.0).astype(BF16)
    u = nt(act, stacked(*([wu_ref[...]] * 4)))
    u_ref[xo, 0] = u[40:200].astype(BF16)
    u_ref[xo, 1] = jnp.where(low_b(160), u[80:240], u[0:160]).astype(BF16)


def decode(xo, e_ref, ev_ref, u_ref, wd_ref, bd, perm, back, m_ref, out_ref):
    z4 = depth_of(160)
    first, last = z4 == 0, z4 == ZC - 1
    la = lanes_a(160)
    mid, every = slice(80, 240), slice(0, 160)
    x = xo + 2
    lhs = [e_ref[x, cz, mid] for cz in BITS] + [joined_x(e_ref, x, cz, la, mid) for cz in BITS]
    lhs += [ev_ref[x, cz] for cz in BITS] + [joined_x(ev_ref, x, cz, la, every) for cz in BITS]
    x = xo + 1
    for v in BITS:
        lhs += [u_ref[x, v], joined_x(u_ref, x, v, la, every)]
    o = nn(beside(*lhs), wd_ref[...])
    d0 = o[:, 0:128] + moved(o[:, 256:384], 1, first) + bd
    d1 = o[:, 128:256] + moved(o[:, 384:512], -1, last) + bd
    d = [beside(*[v[ZC * y : ZC * y + ZC] for y in range(4)]) for v in (d0, d1)]
    d = stacked(*d, jnp.zeros((LANES - Z, 512), F32)).astype(BF16)
    d = nn(d, perm)
    for a in BITS:
        t = jnp.transpose(d[:, 256 * a : 256 * a + 256]).astype(BF16)
        t = nn(t, back).reshape(CH, 8, Z)
        x = 2 * xo + a
        out_ref[:, x] = jnp.where(m_ref[x][None] > 0, t, 0.0).astype(BF16)


def near_kernel(
    right_ref, own_ref, low_ref, high_ref, side_ref, we_ref, be_ref, wn_ref, gain_ref, shift_ref, wc_ref, bc_ref,
    wu_ref, e_ref, ev_ref, c_ref, d_ref, o_ref, u_ref, a_ref, v_ref, k_ref,
):
    right = right_ref[0]
    load_all(own_ref, low_ref, high_ref, side_ref, right, a_ref, v_ref, k_ref)
    be = quad(be_ref[...])
    for i in range(5):
        encode(
            3 * right + 1 + i, a_ref, v_ref, k_ref, e_ref, ev_ref, c_ref, d_ref, o_ref, we_ref, be, wn_ref,
            gain_ref[...], shift_ref[...],
        )
    for i in range(3):
        coarse(3 * right + i, c_ref, d_ref, o_ref, u_ref, wc_ref, bc_ref[...], wu_ref)


def far_kernel(
    right_ref, own_ref, low_ref, high_ref, side_ref, we_ref, be_ref, wn_ref, gain_ref, shift_ref, wc_ref, bc_ref,
    wu_ref, e1_ref, ev1_ref, c1_ref, d1_ref, o1_ref, u1_ref, m_ref, wd_ref, bd_ref, out_hbm, a_ref, v_ref, k_ref,
    e_ref, ev_ref, c_ref, d_ref, o_ref, u_ref, out_ref, sems,
):
    right = 1 - right_ref[0]
    left = 1 - right
    load_all(own_ref, low_ref, high_ref, side_ref, right, a_ref, v_ref, k_ref)
    be = quad(be_ref[...])
    kept = ((e_ref, e1_ref), (ev_ref, ev1_ref), (c_ref, c1_ref), (d_ref, d1_ref), (o_ref, o1_ref))
    for i in range(5):
        for ref, given in kept:
            ref[3 * left + i] = given[3 * left + i]
    for i in range(3):
        u_ref[3 * left + i] = u1_ref[3 * left + i]
    for i in range(3):
        encode(
            5 * right + 1 + i, a_ref, v_ref, k_ref, e_ref, ev_ref, c_ref, d_ref, o_ref, we_ref, be, wn_ref,
            gain_ref[...], shift_ref[...],
        )
    for i in range(3):
        coarse(3 * right + i, c_ref, d_ref, o_ref, u_ref, wc_ref, bc_ref[...], wu_ref)
    bd = quad(bd_ref[...])
    back = unpick(LANES, Z)
    src = iota((512, LANES), 0)
    goal = (((src >> 6) & 1) << 8) + ((src & 31) << 3) + ((src >> 7) << 1) + ((src >> 5) & 1) - iota((512, LANES), 1)
    perm = beside(*[one_where(goal == LANES * i) for i in range(4)])
    copies = []
    for xo in range(4):
        decode(xo, e_ref, ev_ref, u_ref, wd_ref, bd, perm, back, m_ref, out_ref)
        at = pl.ds(2 * xo, 2)
        copies.append(pltpu.make_async_copy(out_ref.at[:, at], out_hbm.at[:, at], sems.at[xo]))
        copies[-1].start()
    for copy in copies:
        copy.wait()


def vmem(n):
    return [pl.BlockSpec(memory_space=pltpu.VMEM)] * n


def hbm(n):
    return [pl.BlockSpec(memory_space=pltpu.HBM)] * n


def call(kernel, outs, ins, out_specs, scratch, mib, flops):
    return pl.pallas_call(
        kernel,
        out_shape=outs,
        in_specs=ins,
        out_specs=out_specs,
        scratch_shapes=scratch,
        compiler_params=pltpu.CompilerParams(vmem_limit_bytes=mib << 20),
        cost_estimate=pl.CostEstimate(flops=flops, bytes_accessed=10**6, transcendentals=0),
    )


def array(*shape, kind=BF16):
    return jax.ShapeDtypeStruct(shape, kind)


def buffers(shapes):
    return [pltpu.VMEM(s, d) for s, d in shapes]


def shifted(value, axis, step):
    peers = lax.axis_size(axis)
    return lax.ppermute(value, axis, [(i, i + step) for i in range(peers) if 0 <= i + step < peers])


def swapped(value, axis, first):
    peers = lax.axis_size(axis)
    pairs = []
    for i in range(first, peers - 1, 2):
        pairs += [(i, i + 1), (i + 1, i)]
    return lax.ppermute(value, axis, pairs)


def time_features(timestep, embed_width):
    halves = embed_width // 2
    freqs = jnp.exp(-math.log(10000.0) * jnp.arange(halves, dtype=F32) / halves)
    angles = timestep[0].astype(F32) * freqs
    return jnp.concatenate([jnp.sin(angles), jnp.cos(angles)]).astype(BF16)


SCALAR = [pl.BlockSpec(memory_space=pltpu.SMEM)]
PLANES = [((10, 2, 320, LANES), BF16), ((10, 2, 320, LANES), BF16), ((2, 3, 3, ZC, LANES), F32)]
STATE = [
    ((8, 2, 320, LANES), BF16),
    ((8, 2, 160, LANES), BF16),
    ((8, 320, LANES), BF16),
    ((8, 240, LANES), BF16),
    ((8, 240, LANES), F32),
    ((6, 2, 160, LANES), BF16),
]


def on_device(
    fine_in, voxel_mask, timestep, w_enc, b_enc, w_down, w_time, w_coarse, b_coarse, w_up, w_dec, b_dec
):
    own, up, down = call(
        pack_kernel,
        [array(OWN + ZC, LANES), array(SIDE_ROWS, LANES), array(SIDE_ROWS, LANES)],
        hbm(2),
        vmem(3),
        [pltpu.VMEM(fine_in.shape, BF16), pltpu.VMEM(voxel_mask.shape, jnp.int32), pltpu.SemaphoreType.DMA((5,))],
        12,
        10**9,
    )(fine_in, voxel_mask)
    low = shifted(up, "wide", 1)
    high = shifted(down, "wide", -1)

    embedded = time_features(timestep, w_time.shape[0])
    film = jnp.dot(embedded[None], w_time, preferred_element_type=F32)
    chans = w_down.shape[0]
    gains = 1.0 + film[:, :chans]
    shifts = film[:, chans:]
    taps = 27 * LANES
    enc_w, dec_w, down_w = call(
        weights_kernel,
        [array(1024, 512), array(1536, 512), array(128, 256)],
        vmem(3),
        vmem(3),
        buffers([((taps, 32), BF16), ((taps, 64), BF16), ((32, taps), F32), ((64, taps), F32)]),
        16,
        4 * 10**9,
    )(w_enc, w_dec, w_down)

    odd = lax.axis_index("narrow").astype(jnp.int32)[None] & 1
    near_right = 1 - odd
    far, near = call(
        mid_kernel,
        [array(EDGE_ROWS, LANES), array(EDGE_ROWS, LANES)],
        SCALAR + vmem(4),
        vmem(2),
        buffers([((2, 4 * ZC, LANES), F32)]),
        8,
        10**8,
    )(odd, own, low, high, down_w)
    far_side = swapped(far, "narrow", 1)
    near_side = swapped(near, "narrow", 0)

    some = (enc_w, b_enc[None], down_w, gains, shifts, w_coarse, b_coarse[None], w_up)
    state = call(
        near_kernel, [array(*s, kind=d) for s, d in STATE], SCALAR + vmem(12), vmem(6), buffers(PLANES), 20, 5 * 10**9
    )(near_right, own, low, high, near_side, *some)
    return call(
        far_kernel,
        [array(*fine_in.shape)],
        SCALAR + vmem(21),
        hbm(1),
        buffers(PLANES + STATE) + [pltpu.VMEM(fine_in.shape, BF16), pltpu.SemaphoreType.DMA((4,))],
        24,
        5 * 10**9,
    )(near_right, own, low, high, far_side, *some, *state, voxel_mask, dec_w, b_dec[None])[0]


def solution(mesh):
    field = P(None, "narrow", "wide", None)
    return jax.shard_map(
        on_device,
        mesh=mesh,
        in_specs=(field, P("narrow", "wide", None)) + (P(),) * 10,
        out_specs=field,
        check_vma=False,
    )
```

time: 40.8 us -> 37.2 us (0.912)
  waiting for transfers between devices: 9.32 us -> 6.94 us
  Pallas kernels: 17.7 us -> 16.3 us
    ppermute x2, waiting for transfers between devices: 7.01 us -> 5.05 us  [shifted(): lax.ppermute(value, axis, [(i, i + step) for i in range(peers) if 0 <= i...]
    pallas_call x5, Pallas kernels: 17.7 us -> 16.3 us  [the longest x1 7.7 us: on_device(): call(far_kernel, [array(*fine_in.shape)], SCALAR + vmem(21), hbm(1), buff...]
    ppermute x2, waiting for transfers between devices: 2.31 us -> 1.9 us  [swapped(): return lax.ppermute(value, axis, pairs)]
  transfers between devices with their start and end apart: 4 -> 4, of which waited for: 3 -> 3; matrix products, arithmetic and copies ran while one was open for 1% -> 1% of each run, Pallas kernels for 18% -> 17%
where the time goes in v2:
time: 37.2 us; the launch traced here: 36.9 us
  Pallas kernels  16.3 us (44%)
  starting transfers between devices  10.6 us (28%)
  waiting for transfers between devices  6.94 us (19%)
  local copies, waits for them, and re-layouts  1.88 us (5%)
  between operations  1.01 us (3%)
    pallas_call x1, Pallas kernels, on_device(): call(far_kernel, [array(*fine_in.shape)], SCALAR + vmem(21), hbm(1), buff...  7.7 us
    ppermute x2, starting transfers between devices, shifted(): lax.ppermute(value, axis, [(i, i + step) for i in range(peers) if 0 <= i...  5.67 us
    pallas_call x1, Pallas kernels, on_device(): call(near_kernel, [array(*s, kind=d) for s, d in STATE], SCALAR + vmem(12...  5.05 us
    ppermute x2, waiting for transfers between devices, shifted(): lax.ppermute(value, axis, [(i, i + step) for i in range(peers) if 0 <= i...  5.05 us
    ppermute x2, starting transfers between devices, swapped(): return lax.ppermute(value, axis, pairs)  4.91 us
    pallas_call x1, Pallas kernels, on_device(): call(pack_kernel, [array(OWN + ZC, LANES), array(SIDE_ROWS, LANES), array...  2.29 us
    ppermute x2, waiting for transfers between devices, swapped(): return lax.ppermute(value, axis, pairs)  1.9 us
    unnamed x24, local copies, waits for them, and re-layouts  1.88 us
  transfers between devices with their start and end apart: 4, of which 3 were waited for; matrix products, arithmetic and copies ran while one was open for 1% of the time, Pallas kernels for 17%

profile of v2, /device:TPU:1, one launch (start us, length us, event | category | flops | bytes accessed | tf_op | source)
XLA Modules:
  0.0 36.9 jit_solution(14156486712782026110)
XLA Ops:
  0.0 1.1 %copy-done.2 = bf16[32,8,8,80]{3,2,1,0:T(8,128)(2,1)S(1)} copy-done((bf16[32,8,8,80]{3,2,1,0:T(8,128)(2,1)S(1)}, bf16[32,8,8,80]{3,2,1,0:T(8,128)(2,1)}, u32[]{:S(2)}) %copy-start.2) | copy-done | bytes 327704
  1.1 0.8 %copy-done.6 = s32[8,8,80]{2,1,0:T(8,128)S(1)} copy-done((s32[8,8,80]{2,1,0:T(8,128)S(1)}, s32[8,8,80]{2,1,0:T(8,128)}, u32[]{:S(2)}) %copy-start.6) | copy-done | bytes 20504
  1.8 2.3 %shard_map.118 = (bf16[1320,128]{1,0:T(8,128)(2,1)S(1)}, bf16[840,128]{1,0:T(8,128)(2,1)S(1)}, bf16[840,128]{1,0:T(8,128)(2,1)S(1)}) custom-call(bf16[32,8,8,80]{3,2,1,0:T(8,128)(2,1)S(1)} %copy-done.2, s32[8,8,80]{2,1,0:T(8,128)S(1)} %copy-done.6), custom_call_target="tpu_custom_call" | custom-call | flops 1000000000 | bytes 1000000 | tf_op jit(solution)/shard_map/pallas_call | solution.py:508
  4.1 4.4 %collective-permute-start = (bf16[840,128]{1,0:T(8,128)(2,1)S(1)}, bf16[840,128]{1,0:T(8,128)(2,1)S(1)}, u32[]{:S(2)}, u32[]{:S(2)}) collective-permute-start(bf16[840,128]{1,0:T(8,128)(2,1)S(1)} %get-tuple-element.20), channel_id=1, source_target_pairs={{0,8},{8,16},{16,24},{24,32},{32,40},{40,48},{48,56},{56,64},{64,7... | collective-permute-start | bytes 645128 | tf_op jit(solution)/shard_map/ppermute | solution.py:475
  8.5 1.3 %collective-permute-start.1 = (bf16[840,128]{1,0:T(8,128)(2,1)S(1)}, bf16[840,128]{1,0:T(8,128)(2,1)S(1)}, u32[]{:S(2)}, u32[]{:S(2)}) collective-permute-start(bf16[840,128]{1,0:T(8,128)(2,1)S(1)} %get-tuple-element.21), channel_id=1, source_target_pairs={{8,0},{16,8},{24,16},{32,24},{40,32},{48,40},{56,48},{64,56},{72,6... | collective-permute-start | bytes 645128 | tf_op jit(solution)/shard_map/ppermute | solution.py:475
  10.5 0.0 copy-start.1
  10.5 0.0 copy-start.8
  10.5 0.0 copy-start.9
  10.5 0.0 copy-start.10
  10.6 1.1 %shard_map.119 = (bf16[1024,512]{1,0:T(8,128)(2,1)S(1)}, bf16[1536,512]{1,0:T(8,128)(2,1)S(1)}, bf16[128,256]{1,0:T(8,128)(2,1)S(1)}) custom-call(bf16[27,32,32]{2,1,0:T(8,128)(2,1)S(1)} %copy-done.3, bf16[27,32,64]{2,1,0:T(8,128)(2,1)S(1)} %copy-done.4, bf16[128,256]{1,0:T(8,128)(2,1)S(1)} %copy-done.5), custom_call_target="tpu_custom_call" | custom-call | flops 4000000000 | bytes 1000000 | tf_op jit(solution)/shard_map/pallas_call | solution.py:526
  11.6 0.9 %collective-permute-done.low_ref = bf16[840,128]{1,0:T(8,128)(2,1)S(1)} collective-permute-done((bf16[840,128]{1,0:T(8,128)(2,1)S(1)}, bf16[840,128]{1,0:T(8,128)(2,1)S(1)}, u32[]{:S(2)}, u32[]{:S(2)}) %collective-permute-start) | collective-permute-done | bytes 215072 | tf_op jit(solution)/shard_map/ppermute | solution.py:475
  12.5 4.2 %collective-permute-done.1.high_ref = bf16[840,128]{1,0:T(8,128)(2,1)S(1)} collective-permute-done((bf16[840,128]{1,0:T(8,128)(2,1)S(1)}, bf16[840,128]{1,0:T(8,128)(2,1)S(1)}, u32[]{:S(2)}, u32[]{:S(2)}) %collective-permute-start.1) | collective-permute-done | bytes 215072 | tf_op jit(solution)/shard_map/ppermute | solution.py:475
  16.7 0.2 shard_map.120
  16.9 1.7 %collective-permute-start.3 = (bf16[1960,128]{1,0:T(8,128)(2,1)S(1)}, bf16[1960,128]{1,0:T(8,128)(2,1)S(1)}, u32[]{:S(2)}, u32[]{:S(2)}) collective-permute-start(bf16[1960,128]{1,0:T(8,128)(2,1)S(1)} %get-tuple-element.25), channel_id=1, source_target_pairs={{0,1},{1,0},{2,3},{3,2},{4,5},{5,4},{6,7},{7,6},{8,9},{9,8},{10,11... | collective-permute-start | bytes 1505288 | tf_op jit(solution)/shard_map/ppermute | solution.py:483
  18.6 0.2 fusion
  18.8 3.2 %collective-permute-start.2 = (bf16[1960,128]{1,0:T(8,128)(2,1)S(1)}, bf16[1960,128]{1,0:T(8,128)(2,1)S(1)}, u32[]{:S(2)}, u32[]{:S(2)}) collective-permute-start(bf16[1960,128]{1,0:T(8,128)(2,1)S(1)} %get-tuple-element.23), channel_id=1, source_target_pairs={{1,2},{2,1},{3,4},{4,3},{5,6},{6,5},{9,10},{10,9},{11,12},{12,11},... | collective-permute-start | bytes 1505288 | tf_op jit(solution)/shard_map/ppermute | solution.py:483
  22.0 0.0 collective-permute-done.3.side_ref
  22.0 0.0 copy-done.1
  22.1 0.0 copy-done.8
  22.1 0.0 copy-start.7
  22.1 0.0 copy-start.11
  22.1 5.1 %shard_map.121 = (bf16[8,2,320,128]{3,2,1,0:T(8,128)(2,1)S(1)}, bf16[8,2,160,128]{3,2,1,0:T(8,128)(2,1)S(1)}, bf16[8,320,128]{2,1,0:T(8,128)(2,1)S(1)}, bf16[8,2...) custom-call(s32[1]{0:T(128)S(6)} %sub.3.right_ref, ...), custom_call_target="tpu_custom_call" | custom-call | flops 5000000000 | bytes 1000000 | tf_op jit(solution)/shard_map/pallas_call | solution.py:551
  27.2 1.9 %collective-permute-done.2.side_ref = bf16[1960,128]{1,0:T(8,128)(2,1)S(1)} collective-permute-done((bf16[1960,128]{1,0:T(8,128)(2,1)S(1)}, bf16[1960,128]{1,0:T(8,128)(2,1)S(1)}, u32[]{:S(2)}, u32[]{:S(2)}) %collective-permute-start.2) | collective-permute-done | bytes 501792 | tf_op jit(solution)/shard_map/ppermute | solution.py:483
  29.1 7.7 %shard_map.122 = bf16[32,8,8,80]{3,2,1,0:T(8,128)(2,1)} custom-call(s32[1]{0:T(128)S(6)} %sub.3.right_ref, bf16[1320,128]{1,0:T(8,128)(2,1)S(1)} %get-tuple-element.19.own_ref, bf16[840,128]{1,0:T(8,128)(2,1)S(1)} %collective-permute-done.low_ref, bf16[840,128]{1,0:T(8,128)(2,1)S(1)} %collective-permute-done.1.high_ref, ...), custom_call_target="tpu_custom_call" | custom-call | flops 5000000000 | bytes 1000000 | tf_op jit(solution)/shard_map/pallas_call | solution.py:554
  (16 shorter events, 0.1 us)
Async XLA Ops:
  0.0 18.6 %copy-start = (bf16[128,256]{1,0:T(8,128)(2,1)S(1)}, bf16[128,256]{1,0:T(8,128)(2,1)}, u32[]{:S(2)}) copy-start(bf16[128,256]{1,0:T(8,128)(2,1)} %param.18) | copy-start | bytes 196612
  0.0 1.1 %copy-start.2 = (bf16[32,8,8,80]{3,2,1,0:T(8,128)(2,1)S(1)}, bf16[32,8,8,80]{3,2,1,0:T(8,128)(2,1)}, u32[]{:S(2)}) copy-start(bf16[32,8,8,80]{3,2,1,0:T(8,128)(2,1)} %x_hbm.1) | copy-start | bytes 983044
  1.1 0.8 %copy-start.6 = (s32[8,8,80]{2,1,0:T(8,128)S(1)}, s32[8,8,80]{2,1,0:T(8,128)}, u32[]{:S(2)}) copy-start(s32[8,8,80]{2,1,0:T(8,128)} %m_ref.1) | copy-start | bytes 61444
  1.8 8.6 %copy-start.3 = (bf16[27,32,32]{2,1,0:T(8,128)(2,1)S(1)}, bf16[27,32,32]{2,1,0:T(8,128)(2,1)}, u32[]{:S(2)}) copy-start(bf16[27,32,32]{2,1,0:T(8,128)(2,1)} %we_ref.1) | copy-start | bytes 165892
  1.8 8.6 %copy-start.4 = (bf16[27,32,64]{2,1,0:T(8,128)(2,1)S(1)}, bf16[27,32,64]{2,1,0:T(8,128)(2,1)}, u32[]{:S(2)}) copy-start(bf16[27,32,64]{2,1,0:T(8,128)(2,1)} %wd_ref.1) | copy-start | bytes 331780
  1.8 8.7 %copy-start.5 = (bf16[128,256]{1,0:T(8,128)(2,1)S(1)}, bf16[128,256]{1,0:T(8,128)(2,1)}, u32[]{:S(2)}) copy-start(bf16[128,256]{1,0:T(8,128)(2,1)} %wn_ref.1) | copy-start | bytes 196612
  4.1 8.3 %collective-permute-start = (bf16[840,128]{1,0:T(8,128)(2,1)S(1)}, bf16[840,128]{1,0:T(8,128)(2,1)S(1)}, u32[]{:S(2)}, u32[]{:S(2)}) collective-permute-start(bf16[840,128]{1,0:T(8,128)(2,1)S(1)} %get-tuple-element.20), channel_id=1, source_target_pairs={{0,8},{8,16},{16,24},{24,32},{32,40},{40,48},{48,56},{56,64},{64,7... | collective-permute-start | bytes 645128 | tf_op jit(solution)/shard_map/ppermute | solution.py:475
  8.5 8.1 %collective-permute-start.1 = (bf16[840,128]{1,0:T(8,128)(2,1)S(1)}, bf16[840,128]{1,0:T(8,128)(2,1)S(1)}, u32[]{:S(2)}, u32[]{:S(2)}) collective-permute-start(bf16[840,128]{1,0:T(8,128)(2,1)S(1)} %get-tuple-element.21), channel_id=1, source_target_pairs={{8,0},{16,8},{24,16},{32,24},{40,32},{48,40},{56,48},{64,56},{72,6... | collective-permute-start | bytes 645128 | tf_op jit(solution)/shard_map/ppermute | solution.py:475
  10.5 11.5 %copy-start.1 = (bf16[27,128,128]{2,1,0:T(8,128)(2,1)S(1)}, bf16[27,128,128]{2,1,0:T(8,128)(2,1)}, u32[]{:S(2)}) copy-start(bf16[27,128,128]{2,1,0:T(8,128)(2,1)} %wc_ref.3) | copy-start | bytes 2654212
  10.5 11.5 %copy-start.8 = (bf16[32,128]{1,0:T(8,128)(2,1)S(1)}, bf16[32,128]{1,0:T(8,128)(2,1)}, u32[]{:S(2)}) copy-start(bf16[32,128]{1,0:T(8,128)(2,1)} %wu_ref.3) | copy-start | bytes 24580
  10.5 11.5 %copy-start.9 = (f32[32]{0:T(128)S(1)}, f32[32]{0:T(128)}, u32[]{:S(2)}) copy-start(f32[32]{0:T(128)} %param.16) | copy-start | bytes 388
  10.5 11.5 %copy-start.10 = (f32[128]{0:T(128)S(1)}, f32[128]{0:T(128)}, u32[]{:S(2)}) copy-start(f32[128]{0:T(128)} %param.20) | copy-start | bytes 1540
  16.9 5.2 %collective-permute-start.3 = (bf16[1960,128]{1,0:T(8,128)(2,1)S(1)}, bf16[1960,128]{1,0:T(8,128)(2,1)S(1)}, u32[]{:S(2)}, u32[]{:S(2)}) collective-permute-start(bf16[1960,128]{1,0:T(8,128)(2,1)S(1)} %get-tuple-element.25), channel_id=1, source_target_pairs={{0,1},{1,0},{2,3},{3,2},{4,5},{5,4},{6,7},{7,6},{8,9},{9,8},{10,11... | collective-permute-start | bytes 1505288 | tf_op jit(solution)/shard_map/ppermute | solution.py:483
  18.8 10.3 %collective-permute-start.2 = (bf16[1960,128]{1,0:T(8,128)(2,1)S(1)}, bf16[1960,128]{1,0:T(8,128)(2,1)S(1)}, u32[]{:S(2)}, u32[]{:S(2)}) collective-permute-start(bf16[1960,128]{1,0:T(8,128)(2,1)S(1)} %get-tuple-element.23), channel_id=1, source_target_pairs={{1,2},{2,1},{3,4},{4,3},{5,6},{6,5},{9,10},{10,9},{11,12},{12,11},... | collective-permute-start | bytes 1505288 | tf_op jit(solution)/shard_map/ppermute | solution.py:483
  22.1 7.0 %copy-start.7 = (s32[8,8,80]{2,1,0:T(8,128)S(1)}, s32[8,8,80]{2,1,0:T(8,128)}, u32[]{:S(2)}) copy-start(s32[8,8,80]{2,1,0:T(8,128)} %m_ref.1) | copy-start | bytes 61444
  22.1 7.0 %copy-start.11 = (f32[32]{0:T(128)S(1)}, f32[32]{0:T(128)}, u32[]{:S(2)}) copy-start(f32[32]{0:T(128)} %param.23) | copy-start | bytes 388

commit v3 on v2

--- a/solution.py
+++ b/solution.py
@@ -188,7 +188,7 @@
 KINDS = ((0, 0), (1, 0), (0, 1), (1, 1))
 
 
-def weights_kernel(we_ref, wd_ref, wn_ref, oe_ref, od_ref, on_ref, re_ref, rd_ref, te_ref, td_ref):
+def weights_kernel(we_ref, wd_ref, wn_ref, oe_ref, od_ref, on_ref, op_ref, ob_ref, re_ref, rd_ref, te_ref, td_ref):
     for tap in range(27):
         for g in range(4):
             at = LANES * tap + CH * g
@@ -222,6 +222,12 @@
     goal = (((k >> 5) & 1) << 7) + ((k >> 6) << 5) + (k & 31) - iota((8 * CH, LANES), 1)
     perm = jnp.concatenate([(goal == LANES * i).astype(F32).astype(BF16) for i in BITS], axis=1)
     on_ref[...] = nn(wn_ref[...], perm).astype(BF16)
+    src = iota((512, LANES), 0)
+    goal = (((src >> 6) & 1) << 8) + ((src & 31) << 3) + ((src >> 7) << 1) + ((src >> 5) & 1) - iota((512, LANES), 1)
+    op_ref[...] = beside(*[one_where(goal == LANES * i) for i in range(4)])
+    column = iota((Z, LANES), 1)
+    goal = jnp.where(column < ZC, 2 * column, jnp.where(column < Z, 2 * column - (Z - 1), -1))
+    ob_ref[...] = one_where(goal == iota((Z, LANES), 0))
 
 
 def moved(t, amount, edge):
@@ -281,14 +287,6 @@
         m = jnp.maximum(m, pltpu.roll(m, LANES - 64, 1))
         k_ref[0, at, by] = k
         k_ref[1, at, by] = m
-
-
-def load_all(own_ref, low_ref, high_ref, side_ref, right, a_ref, v_ref, k_ref):
-    load_own(own_ref, low_ref, high_ref, a_ref, v_ref)
-    load_side(side_ref, right, a_ref, v_ref)
-    load_masks(1, (low_ref[SIDE_MASK:SIDE_ROWS], own_ref[OWN : OWN + ZC], high_ref[SIDE_MASK:SIDE_ROWS]), k_ref)
-    masks = side_ref[EDGE_MASK:EDGE_ROWS].astype(F32)
-    load_masks(2 * right, [masks[ZC * i : ZC * i + ZC] for i in range(3)], k_ref)
 
 
 def spread(k, index):
@@ -365,7 +363,7 @@
     u_ref[xo, 1] = jnp.where(low_b(160), u[80:240], u[0:160]).astype(BF16)
 
 
-def decode(xo, e_ref, ev_ref, u_ref, wd_ref, bd, perm, back, m_ref, out_ref):
+def decode(xo, e_ref, ev_ref, u_ref, wd_ref, bd, perm, back, m_ref, out_ref, at):
     z4 = depth_of(160)
     first, last = z4 == 0, z4 == ZC - 1
     la = lanes_a(160)
@@ -381,45 +379,31 @@
     d1 = o[:, 128:256] + moved(o[:, 384:512], -1, last) + bd
     d = [beside(*[v[ZC * y : ZC * y + ZC] for y in range(4)]) for v in (d0, d1)]
     d = stacked(*d, jnp.zeros((LANES - Z, 512), F32)).astype(BF16)
-    d = nn(d, perm)
+    d = nn(nn(back, d).astype(BF16), perm)
+    d = stacked(d, jnp.zeros((LANES - Z, 512), F32))
     for a in BITS:
-        t = jnp.transpose(d[:, 256 * a : 256 * a + 256]).astype(BF16)
-        t = nn(t, back).reshape(CH, 8, Z)
-        x = 2 * xo + a
-        out_ref[:, x] = jnp.where(m_ref[x][None] > 0, t, 0.0).astype(BF16)
-
-
-def near_kernel(
-    right_ref, own_ref, low_ref, high_ref, side_ref, we_ref, be_ref, wn_ref, gain_ref, shift_ref, wc_ref, bc_ref,
-    wu_ref, e_ref, ev_ref, c_ref, d_ref, o_ref, u_ref, a_ref, v_ref, k_ref,
-):
-    right = right_ref[0]
-    load_all(own_ref, low_ref, high_ref, side_ref, right, a_ref, v_ref, k_ref)
+        t = jnp.transpose(d[:, 256 * a : 256 * a + 256])[:, :Z].reshape(CH, 8, Z)
+        out_ref[:, at + a] = jnp.where(m_ref[2 * xo + a][None] > 0, t, 0.0).astype(BF16)
+
+
+def own_kernel(own_ref, low_ref, high_ref, we_ref, be_ref, wn_ref, gain_ref, shift_ref, *state):
+    a_ref, v_ref, k_ref, e_ref, ev_ref, c_ref, d_ref, o_ref, _ = state
+    load_own(own_ref, low_ref, high_ref, a_ref, v_ref)
+    load_masks(1, (low_ref[SIDE_MASK:SIDE_ROWS], own_ref[OWN : OWN + ZC], high_ref[SIDE_MASK:SIDE_ROWS]), k_ref)
     be = quad(be_ref[...])
-    for i in range(5):
+    for xi in (4, 5):
         encode(
-            3 * right + 1 + i, a_ref, v_ref, k_ref, e_ref, ev_ref, c_ref, d_ref, o_ref, we_ref, be, wn_ref,
-            gain_ref[...], shift_ref[...],
+            xi, a_ref, v_ref, k_ref, e_ref, ev_ref, c_ref, d_ref, o_ref, we_ref, be, wn_ref, gain_ref[...],
+            shift_ref[...],
         )
-    for i in range(3):
-        coarse(3 * right + i, c_ref, d_ref, o_ref, u_ref, wc_ref, bc_ref[...], wu_ref)
-
-
-def far_kernel(
-    right_ref, own_ref, low_ref, high_ref, side_ref, we_ref, be_ref, wn_ref, gain_ref, shift_ref, wc_ref, bc_ref,
-    wu_ref, e1_ref, ev1_ref, c1_ref, d1_ref, o1_ref, u1_ref, m_ref, wd_ref, bd_ref, out_hbm, a_ref, v_ref, k_ref,
-    e_ref, ev_ref, c_ref, d_ref, o_ref, u_ref, out_ref, sems,
-):
-    right = 1 - right_ref[0]
-    left = 1 - right
-    load_all(own_ref, low_ref, high_ref, side_ref, right, a_ref, v_ref, k_ref)
+
+
+def side_work(right, side_ref, we_ref, be_ref, wn_ref, gain_ref, shift_ref, wc_ref, bc_ref, wu_ref, state):
+    a_ref, v_ref, k_ref, e_ref, ev_ref, c_ref, d_ref, o_ref, u_ref = state
+    load_side(side_ref, right, a_ref, v_ref)
+    masks = side_ref[EDGE_MASK:EDGE_ROWS].astype(F32)
+    load_masks(2 * right, [masks[ZC * i : ZC * i + ZC] for i in range(3)], k_ref)
     be = quad(be_ref[...])
-    kept = ((e_ref, e1_ref), (ev_ref, ev1_ref), (c_ref, c1_ref), (d_ref, d1_ref), (o_ref, o1_ref))
-    for i in range(5):
-        for ref, given in kept:
-            ref[3 * left + i] = given[3 * left + i]
-    for i in range(3):
-        u_ref[3 * left + i] = u1_ref[3 * left + i]
     for i in range(3):
         encode(
             5 * right + 1 + i, a_ref, v_ref, k_ref, e_ref, ev_ref, c_ref, d_ref, o_ref, we_ref, be, wn_ref,
@@ -427,16 +411,45 @@
         )
     for i in range(3):
         coarse(3 * right + i, c_ref, d_ref, o_ref, u_ref, wc_ref, bc_ref[...], wu_ref)
+
+
+N_STATE = 9
+
+
+def near_kernel(
+    right_ref, side_ref, we_ref, be_ref, wn_ref, gain_ref, shift_ref, wc_ref, bc_ref, wu_ref, m_ref, wd_ref, bd_ref,
+    perm_ref, back_ref, *refs
+):
+    state = refs[N_STATE : 2 * N_STATE]
+    out_ref = refs[2 * N_STATE]
+    right = right_ref[0]
+    side_work(right, side_ref, we_ref, be_ref, wn_ref, gain_ref, shift_ref, wc_ref, bc_ref, wu_ref, state)
+    decode(
+        3 * right, state[3], state[4], state[8], wd_ref, quad(bd_ref[...]), perm_ref[...], back_ref[...], m_ref, out_ref, 0
+    )
+
+
+def far_kernel(
+    right_ref, side_ref, we_ref, be_ref, wn_ref, gain_ref, shift_ref, wc_ref, bc_ref, wu_ref, m_ref, wd_ref, bd_ref,
+    perm_ref, back_ref, done_ref, *refs
+):
+    state = refs[N_STATE : 2 * N_STATE]
+    out_hbm = refs[2 * N_STATE]
+    out_ref, sems = refs[2 * N_STATE + 1 :]
+    right = 1 - right_ref[0]
+    copies = [pltpu.make_async_copy(done_ref, out_hbm.at[:, pl.ds(6 * (1 - right), 2)], sems.at[3])]
+    copies[0].start()
+    side_work(right, side_ref, we_ref, be_ref, wn_ref, gain_ref, shift_ref, wc_ref, bc_ref, wu_ref, state)
     bd = quad(bd_ref[...])
-    back = unpick(LANES, Z)
-    src = iota((512, LANES), 0)
-    goal = (((src >> 6) & 1) << 8) + ((src & 31) << 3) + ((src >> 7) << 1) + ((src >> 5) & 1) - iota((512, LANES), 1)
-    perm = beside(*[one_where(goal == LANES * i) for i in range(4)])
-    copies = []
-    for xo in range(4):
-        decode(xo, e_ref, ev_ref, u_ref, wd_ref, bd, perm, back, m_ref, out_ref)
-        at = pl.ds(2 * xo, 2)
-        copies.append(pltpu.make_async_copy(out_ref.at[:, at], out_hbm.at[:, at], sems.at[xo]))
+    for i in range(3):
+        decode(
+            right + i, state[3], state[4], state[8], wd_ref, bd, perm_ref[...], back_ref[...], m_ref, out_ref, 2 * i
+        )
+        copies.append(
+            pltpu.make_async_copy(
+                out_ref.at[:, pl.ds(2 * i, 2)], out_hbm.at[:, pl.ds(2 * (right + i), 2)], sems.at[i]
+            )
+        )
         copies[-1].start()
     for copy in copies:
         copy.wait()
@@ -450,13 +463,14 @@
     return [pl.BlockSpec(memory_space=pltpu.HBM)] * n
 
 
-def call(kernel, outs, ins, out_specs, scratch, mib, flops):
+def call(kernel, outs, ins, out_specs, scratch, mib, flops, aliases=()):
     return pl.pallas_call(
         kernel,
         out_shape=outs,
         in_specs=ins,
         out_specs=out_specs,
         scratch_shapes=scratch,
+        input_output_aliases=dict(aliases),
         compiler_params=pltpu.CompilerParams(vmem_limit_bytes=mib << 20),
         cost_estimate=pl.CostEstimate(flops=flops, bytes_accessed=10**6, transcendentals=0),
     )
@@ -491,8 +505,10 @@
 
 
 SCALAR = [pl.BlockSpec(memory_space=pltpu.SMEM)]
-PLANES = [((10, 2, 320, LANES), BF16), ((10, 2, 320, LANES), BF16), ((2, 3, 3, ZC, LANES), F32)]
 STATE = [
+    ((10, 2, 320, LANES), BF16),
+    ((10, 2, 320, LANES), BF16),
+    ((2, 3, 3, ZC, LANES), F32),
     ((8, 2, 320, LANES), BF16),
     ((8, 2, 160, LANES), BF16),
     ((8, 320, LANES), BF16),
@@ -513,7 +529,7 @@
         [pltpu.VMEM(fine_in.shape, BF16), pltpu.VMEM(voxel_mask.shape, jnp.int32), pltpu.SemaphoreType.DMA((5,))],
         12,
         10**9,
-    )(fine_in, voxel_mask)
+    )(pltpu.with_memory_space_constraint(fine_in, pltpu.HBM), pltpu.with_memory_space_constraint(voxel_mask, pltpu.HBM))
     low = shifted(up, "wide", 1)
     high = shifted(down, "wide", -1)
 
@@ -523,11 +539,11 @@
     gains = 1.0 + film[:, :chans]
     shifts = film[:, chans:]
     taps = 27 * LANES
-    enc_w, dec_w, down_w = call(
+    enc_w, dec_w, down_w, perm, back = call(
         weights_kernel,
-        [array(1024, 512), array(1536, 512), array(128, 256)],
+        [array(1024, 512), array(1536, 512), array(128, 256), array(512, 512), array(Z, LANES)],
         vmem(3),
-        vmem(3),
+        vmem(5),
         buffers([((taps, 32), BF16), ((taps, 64), BF16), ((32, taps), F32), ((64, taps), F32)]),
         16,
         4 * 10**9,
@@ -547,19 +563,31 @@
     far_side = swapped(far, "narrow", 1)
     near_side = swapped(near, "narrow", 0)
 
-    some = (enc_w, b_enc[None], down_w, gains, shifts, w_coarse, b_coarse[None], w_up)
-    state = call(
-        near_kernel, [array(*s, kind=d) for s, d in STATE], SCALAR + vmem(12), vmem(6), buffers(PLANES), 20, 5 * 10**9
-    )(near_right, own, low, high, near_side, *some)
+    encoder = (enc_w, b_enc[None], down_w, gains, shifts)
+    shapes = [array(*shape, kind=kind) for shape, kind in STATE]
+    state = call(own_kernel, shapes, vmem(8), vmem(N_STATE), [], 12, 2 * 10**9)(own, low, high, *encoder)
+    some = encoder + (w_coarse, b_coarse[None], w_up, voxel_mask, dec_w, b_dec[None], perm, back)
+    rows = (fine_in.shape[0], 2) + fine_in.shape[2:]
+    *state, done = call(
+        near_kernel,
+        shapes + [array(*rows)],
+        SCALAR + vmem(14 + N_STATE),
+        vmem(N_STATE + 1),
+        [],
+        16,
+        4 * 10**9,
+        [(15 + i, i) for i in range(N_STATE)],
+    )(near_right, near_side, *some, *state)
     return call(
         far_kernel,
-        [array(*fine_in.shape)],
-        SCALAR + vmem(21),
-        hbm(1),
-        buffers(PLANES + STATE) + [pltpu.VMEM(fine_in.shape, BF16), pltpu.SemaphoreType.DMA((4,))],
-        24,
+        shapes + [array(*fine_in.shape)],
+        SCALAR + vmem(15 + N_STATE),
+        vmem(N_STATE) + hbm(1),
+        [pltpu.VMEM((fine_in.shape[0], 6) + fine_in.shape[2:], BF16), pltpu.SemaphoreType.DMA((4,))],
+        16,
         5 * 10**9,
-    )(near_right, own, low, high, far_side, *some, *state, voxel_mask, dec_w, b_dec[None])[0]
+        [(16 + i, i) for i in range(N_STATE)],
+    )(near_right, far_side, *some, done, *state)[N_STATE]
 
 
 def solution(mesh):

time: 37.2 us -> 34.9 us (0.938)
  waiting for transfers between devices: 6.94 us -> 3.84 us
  Pallas kernels: 16.3 us -> 16.7 us
    ppermute x2, waiting for transfers between devices: 1.9 us -> 0.01 us  [swapped(): return lax.ppermute(value, axis, pairs)]
    ppermute x2, waiting for transfers between devices: 5.05 us -> 3.84 us  [shifted(): lax.ppermute(value, axis, [(i, i + step) for i in range(peers) if 0 <= i...]
    pallas_call x1, Pallas kernels: 2.29 us -> 2.81 us  [on_device(): call(pack_kernel, [array(OWN + ZC, LANES), array(SIDE_ROWS, LANES), array...]
    unnamed x24 -> x26, local copies, waits for them, and re-layouts: 1.88 us -> 2.25 us
    pallas_call x2 -> x3, Pallas kernels: 12.8 us -> 12.5 us  [the longest x1 6.4 us: on_device(): call(far_kernel, shapes + [array(*fine_in.shape)], SCALAR + vmem(15 + N_S...]
  transfers between devices with their start and end apart: 4 -> 4, of which waited for: 3 -> 1; matrix products, arithmetic and copies ran while one was open for 1% -> 1% of each run, Pallas kernels for 17% -> 21%
where the time goes in v3:
time: 34.9 us; the launch traced here: 34.7 us
  Pallas kernels  16.7 us (48%)
  starting transfers between devices  10.6 us (30%)
  waiting for transfers between devices  3.84 us (11%)
  local copies, waits for them, and re-layouts  2.25 us (6%)
  between operations  1.04 us (3%)
    pallas_call x1, Pallas kernels, on_device(): call(far_kernel, shapes + [array(*fine_in.shape)], SCALAR + vmem(15 + N_S...  6.4 us
    ppermute x2, starting transfers between devices, shifted(): lax.ppermute(value, axis, [(i, i + step) for i in range(peers) if 0 <= i...  5.67 us
    ppermute x2, starting transfers between devices, swapped(): return lax.ppermute(value, axis, pairs)  4.92 us
    pallas_call x1, Pallas kernels, on_device(): call(near_kernel, shapes + [array(*rows)], SCALAR + vmem(14 + N_STATE), v...  4.54 us
    ppermute x2, waiting for transfers between devices, shifted(): lax.ppermute(value, axis, [(i, i + step) for i in range(peers) if 0 <= i...  3.84 us
    pallas_call x1, Pallas kernels, on_device(): call(pack_kernel, [array(OWN + ZC, LANES), array(SIDE_ROWS, LANES), array...  2.81 us
    unnamed x26, local copies, waits for them, and re-layouts  2.25 us
    pallas_call x1, Pallas kernels, on_device(): call(own_kernel, shapes, vmem(8), vmem(N_STATE), [], 12, 2 * 10 ** 9)  1.5 us
  transfers between devices with their start and end apart: 4, of which 1 were waited for; matrix products, arithmetic and copies ran while one was open for 1% of the time, Pallas kernels for 21%

profile of v3, /device:TPU:1, one launch (start us, length us, event | category | flops | bytes accessed | tf_op | source)
XLA Modules:
  0.0 34.7 jit_solution(13612463879311873427)
XLA Ops:
  0.0 0.0 copy-start
  0.0 0.0 copy-start.2
  0.0 2.8 %shard_map.118 = (bf16[1320,128]{1,0:T(8,128)(2,1)S(1)}, bf16[840,128]{1,0:T(8,128)(2,1)S(1)}, bf16[840,128]{1,0:T(8,128)(2,1)S(1)}) custom-call(bf16[32,8,8,80]{3,2,1,0:T(8,128)(2,1)} %x_hbm.1, s32[8,8,80]{2,1,0:T(8,128)} %m_ref.3), custom_call_target="tpu_custom_call" | custom-call | flops 1000000000 | bytes 1000000 | tf_op jit(solution)/shard_map/pallas_call | solution.py:524
  2.8 4.4 %collective-permute-start = (bf16[840,128]{1,0:T(8,128)(2,1)S(1)}, bf16[840,128]{1,0:T(8,128)(2,1)S(1)}, u32[]{:S(2)}, u32[]{:S(2)}) collective-permute-start(bf16[840,128]{1,0:T(8,128)(2,1)S(1)} %get-tuple-element.36), channel_id=1, source_target_pairs={{0,8},{8,16},{16,24},{24,32},{32,40},{40,48},{48,56},{56,64},{64,7... | collective-permute-start | bytes 645128 | tf_op jit(solution)/shard_map/ppermute | solution.py:489
  7.2 0.0 copy-start.7
  7.2 1.3 %collective-permute-start.1 = (bf16[840,128]{1,0:T(8,128)(2,1)S(1)}, bf16[840,128]{1,0:T(8,128)(2,1)S(1)}, u32[]{:S(2)}, u32[]{:S(2)}) collective-permute-start(bf16[840,128]{1,0:T(8,128)(2,1)S(1)} %get-tuple-element.37), channel_id=1, source_target_pairs={{8,0},{16,8},{24,16},{32,24},{40,32},{48,40},{56,48},{64,56},{72,6... | collective-permute-start | bytes 645128 | tf_op jit(solution)/shard_map/ppermute | solution.py:489
  8.5 0.0 copy-done.3
  8.5 0.0 copy-done.4
  8.6 1.3 %shard_map.119 = (bf16[1024,512]{1,0:T(8,128)(2,1)S(1)}, bf16[1536,512]{1,0:T(8,128)(2,1)S(1)}, bf16[128,256]{1,0:T(8,128)(2,1)S(1)}, bf16[512,512]{1,0:T(8,128)(2,1)S(1)}, bf16[80,128]{1,0:T(8,128)(2,1)S(1)}) custom-call(bf16[27,32,32]{2,1,0:T(8,128)(2,1)S(1)} %copy-done.2, bf16[27,32,64]{2,1,0:T(8,128)(2,1)S(1)} %copy-done.3, bf16[128,256]{1,0:T(8,128)(2,1)S(1)} %copy-done.4), custom_call_target="tpu_custom_call" | custom-call | flops 4000000000 | bytes 1000000 | tf_op jit(solution)/shard_map/pallas_call | solution.py:542
  9.8 1.0 %copy-done.10 = bf16[1024,512]{1,0:T(8,128)(2,1)} copy-done((bf16[1024,512]{1,0:T(8,128)(2,1)}, bf16[1024,512]{1,0:T(8,128)(2,1)S(1)}, u32[]{:S(2)}) %copy-start.10) | copy-done | bytes 1048600
  11.5 0.1 cosine_convert_fusion
  11.5 0.0 collective-permute-done.low_ref
  11.5 3.8 %collective-permute-done.1.high_ref = bf16[840,128]{1,0:T(8,128)(2,1)S(1)} collective-permute-done((bf16[840,128]{1,0:T(8,128)(2,1)S(1)}, bf16[840,128]{1,0:T(8,128)(2,1)S(1)}, u32[]{:S(2)}, u32[]{:S(2)}) %collective-permute-start.1) | collective-permute-done | bytes 215072 | tf_op jit(solution)/shard_map/ppermute | solution.py:489
  15.4 0.2 shard_map.120
  15.6 1.7 %collective-permute-start.3 = (bf16[1960,128]{1,0:T(8,128)(2,1)S(1)}, bf16[1960,128]{1,0:T(8,128)(2,1)S(1)}, u32[]{:S(2)}, u32[]{:S(2)}) collective-permute-start(bf16[1960,128]{1,0:T(8,128)(2,1)S(1)} %get-tuple-element.44), channel_id=1, source_target_pairs={{0,1},{1,0},{2,3},{3,2},{4,5},{5,4},{6,7},{7,6},{8,9},{9,8},{10,11... | collective-permute-start | bytes 1505288 | tf_op jit(solution)/shard_map/ppermute | solution.py:497
  17.3 0.2 fusion
  17.5 3.2 %collective-permute-start.2 = (bf16[1960,128]{1,0:T(8,128)(2,1)S(1)}, bf16[1960,128]{1,0:T(8,128)(2,1)S(1)}, u32[]{:S(2)}, u32[]{:S(2)}) collective-permute-start(bf16[1960,128]{1,0:T(8,128)(2,1)S(1)} %get-tuple-element.39), channel_id=1, source_target_pairs={{1,2},{2,1},{3,4},{4,3},{5,6},{6,5},{9,10},{10,9},{11,12},{12,11},... | collective-permute-start | bytes 1505288 | tf_op jit(solution)/shard_map/ppermute | solution.py:497
  20.7 1.2 %copy-done.11 = bf16[1024,512]{1,0:T(8,128)(2,1)S(1)} copy-done((bf16[1024,512]{1,0:T(8,128)(2,1)S(1)}, bf16[1024,512]{1,0:T(8,128)(2,1)}, u32[]{:S(2)}) %copy-start.11) | copy-done | bytes 1048600
  21.9 0.0 copy-start.9
  22.0 1.5 %shard_map.121 = (bf16[10,2,320,128]{3,2,1,0:T(8,128)(2,1)S(1)}, bf16[10,2,320,128]{3,2,1,0:T(8,128)(2,1)S(1)}, f32[2,3,3,40,128]{4,3,2,1,0:T(8,128)S(1)}, bf16[...) custom-call(bf16[1320,128]{1,0:T(8,128)(2,1)S(1)} %get-tuple-element, ...), custom_call_target="tpu_custom_call" | custom-call | flops 2000000000 | bytes 1000000 | tf_op jit(solution)/shard_map/pallas_call | solution.py:568
  23.5 0.0 collective-permute-done.3.side_ref
  23.5 4.5 %shard_map.122 = (bf16[10,2,320,128]{3,2,1,0:T(8,128)(2,1)S(1)}, bf16[10,2,320,128]{3,2,1,0:T(8,128)(2,1)S(1)}, f32[2,3,3,40,128]{4,3,2,1,0:T(8,128)S(1)}, bf16[...) custom-call(s32[1]{0:T(128)S(6)} %sub.3.right_ref, ...), custom_call_target="tpu_custom_call", output_to_operand_aliasing={{0}: (15, {}), {1}: (16, {}), {2}: (17, {}), {3}: (18, {}),... | custom-call | flops 4000000000 | bytes 1000000 | tf_op jit(solution)/shard_map/pallas_call | solution.py:571
  28.1 0.0 collective-permute-done.2.side_ref
  28.1 6.4 %shard_map.123 = (bf16[10,2,320,128]{3,2,1,0:T(8,128)(2,1)S(1)}, bf16[10,2,320,128]{3,2,1,0:T(8,128)(2,1)S(1)}, f32[2,3,3,40,128]{4,3,2,1,0:T(8,128)S(1)}, bf16[...) custom-call(s32[1]{0:T(128)S(6)} %sub.3.right_ref, ...), custom_call_target="tpu_custom_call", output_to_operand_aliasing={{0}: (16, {}), {1}: (17, {}), {2}: (18, {}), {3}: (19, {}),... | custom-call | flops 5000000000 | bytes 1000000 | tf_op jit(solution)/shard_map/pallas_call | solution.py:581
  (19 shorter events, 0.0 us)
Async XLA Ops:
  0.0 17.3 %copy-start = (bf16[128,256]{1,0:T(8,128)(2,1)S(1)}, bf16[128,256]{1,0:T(8,128)(2,1)}, u32[]{:S(2)}) copy-start(bf16[128,256]{1,0:T(8,128)(2,1)} %param.18) | copy-start | bytes 196612
  0.0 8.5 %copy-start.3 = (bf16[27,32,64]{2,1,0:T(8,128)(2,1)S(1)}, bf16[27,32,64]{2,1,0:T(8,128)(2,1)}, u32[]{:S(2)}) copy-start(bf16[27,32,64]{2,1,0:T(8,128)(2,1)} %wd_ref.1) | copy-start | bytes 331780
  0.0 8.5 %copy-start.4 = (bf16[128,256]{1,0:T(8,128)(2,1)S(1)}, bf16[128,256]{1,0:T(8,128)(2,1)}, u32[]{:S(2)}) copy-start(bf16[128,256]{1,0:T(8,128)(2,1)} %wn_ref.1) | copy-start | bytes 196612
  0.0 8.5 %copy-start.2 = (bf16[27,32,32]{2,1,0:T(8,128)(2,1)S(1)}, bf16[27,32,32]{2,1,0:T(8,128)(2,1)}, u32[]{:S(2)}) copy-start(bf16[27,32,32]{2,1,0:T(8,128)(2,1)} %we_ref.1) | copy-start | bytes 165892
  2.8 8.7 %collective-permute-start = (bf16[840,128]{1,0:T(8,128)(2,1)S(1)}, bf16[840,128]{1,0:T(8,128)(2,1)S(1)}, u32[]{:S(2)}, u32[]{:S(2)}) collective-permute-start(bf16[840,128]{1,0:T(8,128)(2,1)S(1)} %get-tuple-element.36), channel_id=1, source_target_pairs={{0,8},{8,16},{16,24},{24,32},{32,40},{40,48},{48,56},{56,64},{64,7... | collective-permute-start | bytes 645128 | tf_op jit(solution)/shard_map/ppermute | solution.py:489
  7.2 13.5 %copy-start.7 = (f32[32]{0:T(128)S(1)}, f32[32]{0:T(128)}, u32[]{:S(2)}) copy-start(f32[32]{0:T(128)} %param.16) | copy-start | bytes 388
  7.2 8.1 %collective-permute-start.1 = (bf16[840,128]{1,0:T(8,128)(2,1)S(1)}, bf16[840,128]{1,0:T(8,128)(2,1)S(1)}, u32[]{:S(2)}, u32[]{:S(2)}) collective-permute-start(bf16[840,128]{1,0:T(8,128)(2,1)S(1)} %get-tuple-element.37), channel_id=1, source_target_pairs={{8,0},{16,8},{24,16},{32,24},{40,32},{48,40},{56,48},{64,56},{72,6... | collective-permute-start | bytes 645128 | tf_op jit(solution)/shard_map/ppermute | solution.py:489
  9.8 1.0 %copy-start.10 = (bf16[1024,512]{1,0:T(8,128)(2,1)}, bf16[1024,512]{1,0:T(8,128)(2,1)S(1)}, u32[]{:S(2)}) copy-start(bf16[1024,512]{1,0:T(8,128)(2,1)S(1)} %get-tuple-element.40.we_ref) | copy-start | bytes 3145732
  15.6 7.9 %collective-permute-start.3 = (bf16[1960,128]{1,0:T(8,128)(2,1)S(1)}, bf16[1960,128]{1,0:T(8,128)(2,1)S(1)}, u32[]{:S(2)}, u32[]{:S(2)}) collective-permute-start(bf16[1960,128]{1,0:T(8,128)(2,1)S(1)} %get-tuple-element.44), channel_id=1, source_target_pairs={{0,1},{1,0},{2,3},{3,2},{4,5},{5,4},{6,7},{7,6},{8,9},{9,8},{10,11... | collective-permute-start | bytes 1505288 | tf_op jit(solution)/shard_map/ppermute | solution.py:497
  17.5 10.6 %collective-permute-start.2 = (bf16[1960,128]{1,0:T(8,128)(2,1)S(1)}, bf16[1960,128]{1,0:T(8,128)(2,1)S(1)}, u32[]{:S(2)}, u32[]{:S(2)}) collective-permute-start(bf16[1960,128]{1,0:T(8,128)(2,1)S(1)} %get-tuple-element.39), channel_id=1, source_target_pairs={{1,2},{2,1},{3,4},{4,3},{5,6},{6,5},{9,10},{10,9},{11,12},{12,11},... | collective-permute-start | bytes 1505288 | tf_op jit(solution)/shard_map/ppermute | solution.py:497
  20.7 1.2 %copy-start.11 = (bf16[1024,512]{1,0:T(8,128)(2,1)S(1)}, bf16[1024,512]{1,0:T(8,128)(2,1)}, u32[]{:S(2)}) copy-start(bf16[1024,512]{1,0:T(8,128)(2,1)} %copy-done.10) | copy-start | bytes 3145732
  21.9 1.6 %copy-start.1 = (bf16[27,128,128]{2,1,0:T(8,128)(2,1)S(1)}, bf16[27,128,128]{2,1,0:T(8,128)(2,1)}, u32[]{:S(2)}) copy-start(bf16[27,128,128]{2,1,0:T(8,128)(2,1)} %wc_ref.3) | copy-start | bytes 2654212
  21.9 1.6 %copy-start.5 = (s32[8,8,80]{2,1,0:T(8,128)S(1)}, s32[8,8,80]{2,1,0:T(8,128)}, u32[]{:S(2)}) copy-start(s32[8,8,80]{2,1,0:T(8,128)} %m_ref.3) | copy-start | bytes 61444
  21.9 1.6 %copy-start.6 = (bf16[32,128]{1,0:T(8,128)(2,1)S(1)}, bf16[32,128]{1,0:T(8,128)(2,1)}, u32[]{:S(2)}) copy-start(bf16[32,128]{1,0:T(8,128)(2,1)} %wu_ref.3) | copy-start | bytes 24580
  21.9 1.6 %copy-start.8 = (f32[128]{0:T(128)S(1)}, f32[128]{0:T(128)}, u32[]{:S(2)}) copy-start(f32[128]{0:T(128)} %param.20) | copy-start | bytes 1540
  21.9 1.6 %copy-start.9 = (f32[32]{0:T(128)S(1)}, f32[32]{0:T(128)}, u32[]{:S(2)}) copy-start(f32[32]{0:T(128)} %param.23) | copy-start | bytes 388
  21.9 1.6 %copy-start.12 = (bf16[1024,512]{1,0:T(8,128)(2,1)S(1)}, bf16[1024,512]{1,0:T(8,128)(2,1)}, u32[]{:S(2)}) copy-start(bf16[1024,512]{1,0:T(8,128)(2,1)} %copy-done.10) | copy-start | bytes 3145732

commit v4 on v3

--- a/solution.py
+++ b/solution.py
@@ -83,17 +83,19 @@
     own_ref[OWN : OWN + ZC] = cols
     up_ref[SIDE_MASK:SIDE_ROWS] = cols
     dn_ref[SIDE_MASK:SIDE_ROWS] = cols
-    ups, downs = [], []
+    sides = [[], []]
     for cx in range(4):
         copies[1 + cx].wait()
-        halves = []
         for a in BITS:
             x = 2 * cx + a
             tile = x_ref[:, x].astype(F32)
             tile = jnp.where(m_ref[x][None] > 0, tile, 0.0)
-            halves.append(nt(sel, tile.reshape(8 * CH, Z).astype(BF16)).astype(BF16))
-        both = beside(*halves)
-        col = [nn(both, perm[cy]) for cy in range(4)]
+            sides[a].append(nt(sel, tile.reshape(8 * CH, Z).astype(BF16)).astype(BF16))
+    both = beside(stacked(*sides[0]), stacked(*sides[1]))
+    cols = [nn(both, perm[cy]) for cy in range(4)]
+    ups, downs = [], []
+    for cx in range(4):
+        col = [v[Z * cx : Z * cx + Z] for v in cols]
         for cz in BITS:
             z = slice(ZC * cz, ZC * cz + ZC)
             first = stacked(col[0][z], col[1][z]).astype(BF16)
@@ -114,7 +116,7 @@
     return pl.ds(pl.multiple_of(x * size, size), size)
 
 
-def mid_kernel(odd_ref, own_ref, low_ref, high_ref, tie_ref, far_ref, near_ref, ends_ref):
+def mid_kernel(odd_ref, own_ref, low_ref, high_ref, tie_ref, tie2_ref, far_ref, near_ref, ends_ref):
     ends_ref[0] = low_ref[SIDE:SIDE_MASK].astype(F32)
     ends_ref[1] = high_ref[SIDE:SIDE_MASK].astype(F32)
 
@@ -188,7 +190,9 @@
 KINDS = ((0, 0), (1, 0), (0, 1), (1, 1))
 
 
-def weights_kernel(we_ref, wd_ref, wn_ref, oe_ref, od_ref, on_ref, op_ref, ob_ref, re_ref, rd_ref, te_ref, td_ref):
+def weights_kernel(
+    we_ref, wd_ref, wn_ref, wc_ref, oe_ref, od_ref, on_ref, op_ref, ob_ref, oc_ref, re_ref, rd_ref, te_ref, td_ref
+):
     for tap in range(27):
         for g in range(4):
             at = LANES * tap + CH * g
@@ -198,6 +202,9 @@
     te_ref[...] = nt(one, re_ref[...])
     one = (iota((2 * CH, 2 * CH), 0) == iota((2 * CH, 2 * CH), 1)).astype(F32).astype(BF16)
     td_ref[...] = nt(one, rd_ref[...])
+    one = one_where(iota((LANES, LANES), 0) == iota((LANES, LANES), 1))
+    for i in range(9):
+        oc_ref[LANES * i : LANES * i + LANES] = nt(one, wc_ref[3 * i : 3 * i + 3].reshape(384, LANES)).astype(BF16)
     group = iota((CH, LANES), 1) >> 5
     for w_ref, o_ref in ((te_ref, oe_ref), (td_ref, od_ref)):
         for t, (fx, fy) in enumerate(KINDS):
@@ -266,7 +273,7 @@
                 stacked(low_ref[at : at + PAIR], own_ref[mine : mine + 2 * PAIR], high_ref[at : at + PAIR])
             )
         z = slice(ZC * x, ZC * x + ZC)
-        put_plane(a_ref, v_ref, 3 + x, layers, stacked(low_ends[z], high_ends[z]))
+        put_plane(a_ref, v_ref, x, layers, stacked(low_ends[z], high_ends[z]))
 
 
 def load_side(ref, right, a_ref, v_ref):
@@ -310,15 +317,15 @@
     return one_where(low_a(rows)) > 0.5
 
 
-def encode(xi, a_ref, v_ref, k_ref, e_ref, ev_ref, c_ref, d_ref, o_ref, we_ref, be, wn_ref, gain, shift):
+def encode(xi, ai, ei, a_ref, v_ref, k_ref, e_ref, ev_ref, c_ref, d_ref, o_ref, we_ref, be, wn_ref, gain, shift):
     z8 = depth_of(320)
     first, last = z8 == 0, z8 == ZC - 1
     lane = iota((8, LANES), 1)
     lane_at = 8 * (lane >> 6) + ((lane >> 5) & 1)
     la = lanes_a(320)
     every = slice(0, 320)
-    lhs = [a_ref[xi, cz] for cz in BITS] + [joined_x(a_ref, xi, cz, la, every) for cz in BITS]
-    lhs += [v_ref[xi, cz] for cz in BITS] + [joined_x(v_ref, xi, cz, la, every) for cz in BITS]
+    lhs = [a_ref[ai, cz] for cz in BITS] + [joined_x(a_ref, ai, cz, la, every) for cz in BITS]
+    lhs += [v_ref[ai, cz] for cz in BITS] + [joined_x(v_ref, ai, cz, la, every) for cz in BITS]
     o = nn(beside(*lhs), we_ref[...])
     bx, lx = local(xi)
     expanded = [[], []]
@@ -338,24 +345,22 @@
     for cz in BITS:
         e = jnp.where(stacked(*expanded[cz]) > 0.5, silu(pre[cz]), 0.0)
         enc.append(e.astype(BF16))
-        e_ref[xi - 1, cz] = enc[cz]
-        ev_ref[xi - 1, cz] = jnp.where(low_b(160), e[120:280], e[40:200]).astype(BF16)
+        e_ref[ei, cz] = enc[cz]
+        ev_ref[ei, cz] = jnp.where(low_b(160), e[120:280], e[40:200]).astype(BF16)
     lifted = nt(beside(*enc), wn_ref[...])
     c = jnp.where(on > 0.5, silu(lifted * gain + shift), 0.0)
-    c_ref[xi - 1] = c.astype(BF16)
-    d_ref[xi - 1] = c[40:280].astype(BF16)
-    o_ref[xi - 1] = on[40:280]
+    c_ref[ei] = c.astype(BF16)
+    d_ref[ei] = c[40:280].astype(BF16)
+    o_ref[ei] = on[40:280]
 
 
 def coarse(xo, c_ref, d_ref, o_ref, u_ref, wc_ref, bc, wu_ref):
     z6 = depth_of(240)
     first, last = z6 == 0, z6 == ZC - 1
-    lhs, rhs = [], []
+    lhs = []
     for dx in range(3):
-        for dy in range(3):
-            lhs.append(d_ref[xo + dx] if dy == 1 else c_ref[xo + dx, 40 * dy : 40 * dy + 240])
-            rhs.append(wc_ref[9 * dx + 3 * dy : 9 * dx + 3 * dy + 3].reshape(384, 128))
-    p = nt(beside(*lhs), beside(*rhs))
+        lhs += [c_ref[xo + dx, 0:240], d_ref[xo + dx], c_ref[xo + dx, 80:320]]
+    p = nn(beside(*lhs), wc_ref[...])
     s = p[:, 128:256] + moved(p[:, 0:128], 1, first) + moved(p[:, 256:384], -1, last) + bc
     act = jnp.where(o_ref[xo + 1] > 0.5, silu(s), 0.0).astype(BF16)
     u = nt(act, stacked(*([wu_ref[...]] * 4)))
@@ -386,65 +391,77 @@
         out_ref[:, at + a] = jnp.where(m_ref[2 * xo + a][None] > 0, t, 0.0).astype(BF16)
 
 
-def own_kernel(own_ref, low_ref, high_ref, we_ref, be_ref, wn_ref, gain_ref, shift_ref, *state):
-    a_ref, v_ref, k_ref, e_ref, ev_ref, c_ref, d_ref, o_ref, _ = state
+def own_kernel(
+    own_ref, low_ref, high_ref, we_ref, be_ref, wn_ref, gain_ref, shift_ref, a_ref, v_ref, e_ref, ev_ref, c_ref, d_ref,
+    o_ref, k_ref
+):
     load_own(own_ref, low_ref, high_ref, a_ref, v_ref)
     load_masks(1, (low_ref[SIDE_MASK:SIDE_ROWS], own_ref[OWN : OWN + ZC], high_ref[SIDE_MASK:SIDE_ROWS]), k_ref)
     be = quad(be_ref[...])
-    for xi in (4, 5):
+    for i in range(2):
         encode(
-            xi, a_ref, v_ref, k_ref, e_ref, ev_ref, c_ref, d_ref, o_ref, we_ref, be, wn_ref, gain_ref[...],
-            shift_ref[...],
+            4 + i, 1 + i, i, a_ref, v_ref, k_ref, e_ref, ev_ref, c_ref, d_ref, o_ref, we_ref, be, wn_ref,
+            gain_ref[...], shift_ref[...],
         )
 
 
-def side_work(right, side_ref, we_ref, be_ref, wn_ref, gain_ref, shift_ref, wc_ref, bc_ref, wu_ref, state):
-    a_ref, v_ref, k_ref, e_ref, ev_ref, c_ref, d_ref, o_ref, u_ref = state
+def side_work(right, side_ref, weights, own, scratch):
+    we_ref, be_ref, wn_ref, gain_ref, shift_ref, wc_ref, bc_ref, wu_ref = weights
+    a_ref, v_ref, e_ref, ev_ref, c_ref, d_ref, o_ref, k_ref, u_ref = scratch
+    for i in range(2):
+        for ref, given in zip((a_ref, v_ref), own[0:2]):
+            ref[3 + 2 * right + i] = given[2 * right + i]
+        for ref, given in zip((e_ref, ev_ref, c_ref, d_ref, o_ref), own[2:7]):
+            ref[3 + i] = given[i]
+        k_ref[i, 1] = own[7][i, 1]
     load_side(side_ref, right, a_ref, v_ref)
     masks = side_ref[EDGE_MASK:EDGE_ROWS].astype(F32)
     load_masks(2 * right, [masks[ZC * i : ZC * i + ZC] for i in range(3)], k_ref)
     be = quad(be_ref[...])
     for i in range(3):
+        xi = 5 * right + 1 + i
         encode(
-            5 * right + 1 + i, a_ref, v_ref, k_ref, e_ref, ev_ref, c_ref, d_ref, o_ref, we_ref, be, wn_ref,
+            xi, xi, xi - 1, a_ref, v_ref, k_ref, e_ref, ev_ref, c_ref, d_ref, o_ref, we_ref, be, wn_ref,
             gain_ref[...], shift_ref[...],
         )
     for i in range(3):
         coarse(3 * right + i, c_ref, d_ref, o_ref, u_ref, wc_ref, bc_ref[...], wu_ref)
 
 
-N_STATE = 9
-
-
-def near_kernel(
-    right_ref, side_ref, we_ref, be_ref, wn_ref, gain_ref, shift_ref, wc_ref, bc_ref, wu_ref, m_ref, wd_ref, bd_ref,
-    perm_ref, back_ref, *refs
-):
-    state = refs[N_STATE : 2 * N_STATE]
-    out_ref = refs[2 * N_STATE]
+def near_kernel(right_ref, side_ref, *refs):
+    weights, (m_ref, wd_ref, bd_ref, perm_ref, back_ref), own = refs[:8], refs[8:13], refs[13:21]
+    done_ref, e1_ref, ev1_ref, u1_ref = refs[21:25]
+    scratch = refs[25:]
     right = right_ref[0]
-    side_work(right, side_ref, we_ref, be_ref, wn_ref, gain_ref, shift_ref, wc_ref, bc_ref, wu_ref, state)
+    side_work(right, side_ref, weights, own, scratch)
+    e_ref, ev_ref, u_ref = scratch[2], scratch[3], scratch[8]
     decode(
-        3 * right, state[3], state[4], state[8], wd_ref, quad(bd_ref[...]), perm_ref[...], back_ref[...], m_ref, out_ref, 0
+        3 * right, e_ref, ev_ref, u_ref, wd_ref, quad(bd_ref[...]), perm_ref[...], back_ref[...], m_ref, done_ref, 0
     )
-
-
-def far_kernel(
-    right_ref, side_ref, we_ref, be_ref, wn_ref, gain_ref, shift_ref, wc_ref, bc_ref, wu_ref, m_ref, wd_ref, bd_ref,
-    perm_ref, back_ref, done_ref, *refs
-):
-    state = refs[N_STATE : 2 * N_STATE]
-    out_hbm = refs[2 * N_STATE]
-    out_ref, sems = refs[2 * N_STATE + 1 :]
-    right = 1 - right_ref[0]
-    copies = [pltpu.make_async_copy(done_ref, out_hbm.at[:, pl.ds(6 * (1 - right), 2)], sems.at[3])]
+    e1_ref[...] = e_ref[2 + 3 * right]
+    ev1_ref[...] = ev_ref[2 + 3 * right]
+    for i in range(2):
+        u1_ref[i] = u_ref[1 + 2 * right + i]
+
+
+def far_kernel(right_ref, side_ref, *refs):
+    weights, (m_ref, wd_ref, bd_ref, perm_ref, back_ref), own = refs[:8], refs[8:13], refs[13:21]
+    done_ref, e1_ref, ev1_ref, u1_ref, out_hbm = refs[21:26]
+    scratch = refs[26:35]
+    out_ref, sems = refs[35:]
+    left = right_ref[0]
+    right = 1 - left
+    copies = [pltpu.make_async_copy(done_ref, out_hbm.at[:, pl.ds(6 * left, 2)], sems.at[3])]
     copies[0].start()
-    side_work(right, side_ref, we_ref, be_ref, wn_ref, gain_ref, shift_ref, wc_ref, bc_ref, wu_ref, state)
+    side_work(right, side_ref, weights, own, scratch)
+    e_ref, ev_ref, u_ref = scratch[2], scratch[3], scratch[8]
+    e_ref[2 + 3 * left] = e1_ref[...]
+    ev_ref[2 + 3 * left] = ev1_ref[...]
+    for i in range(2):
+        u_ref[1 + 2 * left + i] = u1_ref[i]
     bd = quad(bd_ref[...])
     for i in range(3):
-        decode(
-            right + i, state[3], state[4], state[8], wd_ref, bd, perm_ref[...], back_ref[...], m_ref, out_ref, 2 * i
-        )
+        decode(right + i, e_ref, ev_ref, u_ref, wd_ref, bd, perm_ref[...], back_ref[...], m_ref, out_ref, 2 * i)
         copies.append(
             pltpu.make_async_copy(
                 out_ref.at[:, pl.ds(2 * i, 2)], out_hbm.at[:, pl.ds(2 * (right + i), 2)], sems.at[i]
@@ -463,14 +480,13 @@
     return [pl.BlockSpec(memory_space=pltpu.HBM)] * n
 
 
-def call(kernel, outs, ins, out_specs, scratch, mib, flops, aliases=()):
+def call(kernel, outs, ins, out_specs, scratch, mib, flops):
     return pl.pallas_call(
         kernel,
         out_shape=outs,
         in_specs=ins,
         out_specs=out_specs,
         scratch_shapes=scratch,
-        input_output_aliases=dict(aliases),
         compiler_params=pltpu.CompilerParams(vmem_limit_bytes=mib << 20),
         cost_estimate=pl.CostEstimate(flops=flops, bytes_accessed=10**6, transcendentals=0),
     )
@@ -505,17 +521,23 @@
 
 
 SCALAR = [pl.BlockSpec(memory_space=pltpu.SMEM)]
-STATE = [
-    ((10, 2, 320, LANES), BF16),
-    ((10, 2, 320, LANES), BF16),
-    ((2, 3, 3, ZC, LANES), F32),
-    ((8, 2, 320, LANES), BF16),
-    ((8, 2, 160, LANES), BF16),
-    ((8, 320, LANES), BF16),
-    ((8, 240, LANES), BF16),
-    ((8, 240, LANES), F32),
-    ((6, 2, 160, LANES), BF16),
-]
+
+
+def state(own, planes):
+    masks = (2, 3, 3, ZC, LANES)
+    return [
+        ((own, 2, 320, LANES), BF16),
+        ((own, 2, 320, LANES), BF16),
+        ((planes, 2, 320, LANES), BF16),
+        ((planes, 2, 160, LANES), BF16),
+        ((planes, 320, LANES), BF16),
+        ((planes, 240, LANES), BF16),
+        ((planes, 240, LANES), F32),
+        (masks, F32),
+    ]
+
+
+LIFTED = (6, 2, 160, LANES)
 
 
 def on_device(
@@ -539,55 +561,57 @@
     gains = 1.0 + film[:, :chans]
     shifts = film[:, chans:]
     taps = 27 * LANES
-    enc_w, dec_w, down_w, perm, back = call(
+    enc_w, dec_w, down_w, perm, back, coarse_w = call(
         weights_kernel,
-        [array(1024, 512), array(1536, 512), array(128, 256), array(512, 512), array(Z, LANES)],
-        vmem(3),
-        vmem(5),
+        [array(1024, 512), array(1536, 512), array(128, 256), array(512, 512), array(Z, LANES)]
+        + [array(9 * LANES, 384)],
+        vmem(4),
+        vmem(6),
         buffers([((taps, 32), BF16), ((taps, 64), BF16), ((32, taps), F32), ((64, taps), F32)]),
         16,
         4 * 10**9,
-    )(w_enc, w_dec, w_down)
+    )(w_enc, w_dec, w_down, w_coarse)
 
     odd = lax.axis_index("narrow").astype(jnp.int32)[None] & 1
     near_right = 1 - odd
     far, near = call(
         mid_kernel,
         [array(EDGE_ROWS, LANES), array(EDGE_ROWS, LANES)],
-        SCALAR + vmem(4),
+        SCALAR + vmem(5),
         vmem(2),
         buffers([((2, 4 * ZC, LANES), F32)]),
         8,
         10**8,
-    )(odd, own, low, high, down_w)
+    )(odd, own, low, high, down_w, gains)
     far_side = swapped(far, "narrow", 1)
     near_side = swapped(near, "narrow", 0)
 
     encoder = (enc_w, b_enc[None], down_w, gains, shifts)
-    shapes = [array(*shape, kind=kind) for shape, kind in STATE]
-    state = call(own_kernel, shapes, vmem(8), vmem(N_STATE), [], 12, 2 * 10**9)(own, low, high, *encoder)
-    some = encoder + (w_coarse, b_coarse[None], w_up, voxel_mask, dec_w, b_dec[None], perm, back)
-    rows = (fine_in.shape[0], 2) + fine_in.shape[2:]
-    *state, done = call(
+    mine = call(
+        own_kernel, [array(*d, kind=k) for d, k in state(4, 2)], vmem(8), vmem(8), [], 12, 2 * 10**9
+    )(own, low, high, *encoder)
+    some = encoder + (coarse_w, b_coarse[None], w_up, voxel_mask, dec_w, b_dec[None], perm, back) + tuple(mine)
+    scratch = buffers(state(10, 8) + [(LIFTED, BF16)])
+    pair = (fine_in.shape[0], 2) + fine_in.shape[2:]
+    done = call(
         near_kernel,
-        shapes + [array(*rows)],
-        SCALAR + vmem(14 + N_STATE),
-        vmem(N_STATE + 1),
-        [],
-        16,
+        [array(*pair), array(2, 320, LANES), array(2, 160, LANES), array(2, 2, 160, LANES)],
+        SCALAR + vmem(22),
+        vmem(4),
+        scratch,
+        24,
         4 * 10**9,
-        [(15 + i, i) for i in range(N_STATE)],
-    )(near_right, near_side, *some, *state)
+    )(near_right, near_side, *some)
+    rest = (fine_in.shape[0], 6) + fine_in.shape[2:]
     return call(
         far_kernel,
-        shapes + [array(*fine_in.shape)],
-        SCALAR + vmem(15 + N_STATE),
-        vmem(N_STATE) + hbm(1),
-        [pltpu.VMEM((fine_in.shape[0], 6) + fine_in.shape[2:], BF16), pltpu.SemaphoreType.DMA((4,))],
-        16,
+        [array(*fine_in.shape)],
+        SCALAR + vmem(26),
+        hbm(1),
+        scratch + [pltpu.VMEM(rest, BF16), pltpu.SemaphoreType.DMA((4,))],
+        24,
         5 * 10**9,
-        [(16 + i, i) for i in range(N_STATE)],
-    )(near_right, far_side, *some, done, *state)[N_STATE]
+    )(near_right, far_side, *some, *done)[0]
 
 
 def solution(mesh):

time: 34.9 us -> 34.1 us (0.977)
  local copies, waits for them, and re-layouts: 2.25 us -> 0.05 us
  waiting for transfers between devices: 3.84 us -> 5.06 us
    unnamed x26 -> x20, local copies, waits for them, and re-layouts: 2.25 us -> 0.05 us
    ppermute x2, waiting for transfers between devices: 0.01 us -> 0.65 us  [swapped(): return lax.ppermute(value, axis, pairs)]
    ppermute x2, waiting for transfers between devices: 3.84 us -> 4.4 us  [shifted(): lax.ppermute(value, axis, [(i, i + step) for i in range(peers) if 0 <= i...]
    pallas_call x3, Pallas kernels: 12.5 us -> 13 us  [the longest x1 6.7 us: on_device(): call(far_kernel, [array(*fine_in.shape)], SCALAR + vmem(26), hbm(1), scra...]
    pallas_call x1, Pallas kernels: 2.81 us -> 2.32 us  [on_device(): call(pack_kernel, [array(OWN + ZC, LANES), array(SIDE_ROWS, LANES), array...]
  transfers between devices with their start and end apart: 4 -> 4, of which waited for: 1 -> 3; matrix products, arithmetic and copies ran while one was open for 1% -> 1% of each run, Pallas kernels for 21% -> 23%
where the time goes in v4:
time: 34.1 us; the launch traced here: 33.9 us
  Pallas kernels  17 us (50%)
  starting transfers between devices  10.6 us (31%)
  waiting for transfers between devices  5.06 us (15%)
  between operations  1.01 us (3%)
    pallas_call x1, Pallas kernels, on_device(): call(far_kernel, [array(*fine_in.shape)], SCALAR + vmem(26), hbm(1), scra...  6.7 us
    ppermute x2, starting transfers between devices, shifted(): lax.ppermute(value, axis, [(i, i + step) for i in range(peers) if 0 <= i...  5.66 us
    ppermute x2, starting transfers between devices, swapped(): return lax.ppermute(value, axis, pairs)  4.91 us
    pallas_call x1, Pallas kernels, on_device(): call(near_kernel, [array(*pair), array(2, 320, LANES), array(2, 160, LANE...  4.72 us
    ppermute x2, waiting for transfers between devices, shifted(): lax.ppermute(value, axis, [(i, i + step) for i in range(peers) if 0 <= i...  4.4 us
    pallas_call x1, Pallas kernels, on_device(): call(pack_kernel, [array(OWN + ZC, LANES), array(SIDE_ROWS, LANES), array...  2.32 us
    pallas_call x1, Pallas kernels, on_device(): call(own_kernel, [array(*d, kind=k) for d, k in state(4, 2)], vmem(8), vm...  1.54 us
    pallas_call x1, Pallas kernels, on_device(): call(weights_kernel, [array(1024, 512), array(1536, 512), array(128, 256)...  1.49 us
  transfers between devices with their start and end apart: 4, of which 3 were waited for; matrix products, arithmetic and copies ran while one was open for 1% of the time, Pallas kernels for 23%

profile of v4, /device:TPU:1, one launch (start us, length us, event | category | flops | bytes accessed | tf_op | source)
XLA Modules:
  0.0 33.9 jit_solution(5829417413753729038)
XLA Ops:
  0.0 2.3 %shard_map.118 = (bf16[1320,128]{1,0:T(8,128)(2,1)S(1)}, bf16[840,128]{1,0:T(8,128)(2,1)S(1)}, bf16[840,128]{1,0:T(8,128)(2,1)S(1)}) custom-call(bf16[32,8,8,80]{3,2,1,0:T(8,128)(2,1)} %x_hbm.1, s32[8,8,80]{2,1,0:T(8,128)} %refs_8_.3), custom_call_target="tpu_custom_call" | custom-call | flops 1000000000 | bytes 1000000 | tf_op jit(solution)/shard_map/pallas_call | solution.py:546
  2.4 4.4 %collective-permute-start = (bf16[840,128]{1,0:T(8,128)(2,1)S(1)}, bf16[840,128]{1,0:T(8,128)(2,1)S(1)}, u32[]{:S(2)}, u32[]{:S(2)}) collective-permute-start(bf16[840,128]{1,0:T(8,128)(2,1)S(1)} %get-tuple-element.29), channel_id=1, source_target_pairs={{0,8},{8,16},{16,24},{24,32},{32,40},{40,48},{48,56},{56,64},{64,7... | collective-permute-start | bytes 645128 | tf_op jit(solution)/shard_map/ppermute | solution.py:505
  6.7 1.3 %collective-permute-start.1 = (bf16[840,128]{1,0:T(8,128)(2,1)S(1)}, bf16[840,128]{1,0:T(8,128)(2,1)S(1)}, u32[]{:S(2)}, u32[]{:S(2)}) collective-permute-start(bf16[840,128]{1,0:T(8,128)(2,1)S(1)} %get-tuple-element.30), channel_id=1, source_target_pairs={{8,0},{16,8},{24,16},{32,24},{40,32},{48,40},{56,48},{64,56},{72,6... | collective-permute-start | bytes 645128 | tf_op jit(solution)/shard_map/ppermute | solution.py:505
  8.7 0.1 cosine_convert_fusion
  8.7 0.0 copy-done
  8.7 0.2 fusion
  8.9 0.0 copy-done.2
  9.0 0.0 copy-start.7
  9.0 1.5 %shard_map.119 = (bf16[1024,512]{1,0:T(8,128)(2,1)S(1)}, bf16[1536,512]{1,0:T(8,128)(2,1)S(1)}, bf16[128,256]{1,0:T(8,128)(2,1)S(1)}, bf16[512,512]{1,0:T(8,128)...) custom-call(bf16[27,32,32]{2,1,0:T(8,128)(2,1)S(1)} %copy-done.2, ...), custom_call_target="tpu_custom_call" | custom-call | flops 4000000000 | bytes 1000000 | tf_op jit(solution)/shard_map/pallas_call | solution.py:564
  10.5 0.2 collective-permute-done.low_ref
  10.7 4.2 %collective-permute-done.1.high_ref = bf16[840,128]{1,0:T(8,128)(2,1)S(1)} collective-permute-done((bf16[840,128]{1,0:T(8,128)(2,1)S(1)}, bf16[840,128]{1,0:T(8,128)(2,1)S(1)}, u32[]{:S(2)}, u32[]{:S(2)}) %collective-permute-start.1) | collective-permute-done | bytes 215072 | tf_op jit(solution)/shard_map/ppermute | solution.py:505
  14.9 0.2 shard_map.120
  15.1 1.7 %collective-permute-start.3 = (bf16[1960,128]{1,0:T(8,128)(2,1)S(1)}, bf16[1960,128]{1,0:T(8,128)(2,1)S(1)}, u32[]{:S(2)}, u32[]{:S(2)}) collective-permute-start(bf16[1960,128]{1,0:T(8,128)(2,1)S(1)} %get-tuple-element.46), channel_id=1, source_target_pairs={{0,1},{1,0},{2,3},{3,2},{4,5},{5,4},{6,7},{7,6},{8,9},{9,8},{10,11... | collective-permute-start | bytes 1505288 | tf_op jit(solution)/shard_map/ppermute | solution.py:513
  16.8 3.2 %collective-permute-start.2 = (bf16[1960,128]{1,0:T(8,128)(2,1)S(1)}, bf16[1960,128]{1,0:T(8,128)(2,1)S(1)}, u32[]{:S(2)}, u32[]{:S(2)}) collective-permute-start(bf16[1960,128]{1,0:T(8,128)(2,1)S(1)} %get-tuple-element.32), channel_id=1, source_target_pairs={{1,2},{2,1},{3,4},{4,3},{5,6},{6,5},{9,10},{10,9},{11,12},{12,11},... | collective-permute-start | bytes 1505288 | tf_op jit(solution)/shard_map/ppermute | solution.py:513
  20.0 0.0 copy-done.7
  20.0 0.0 copy-start.5
  20.0 0.0 copy-start.6
  20.0 0.0 copy-start.8
  20.0 0.0 copy-start.9
  20.1 1.5 %shard_map.121 = (bf16[4,2,320,128]{3,2,1,0:T(8,128)(2,1)S(1)}, bf16[4,2,320,128]{3,2,1,0:T(8,128)(2,1)S(1)}, bf16[2,2,320,128]{3,2,1,0:T(8,128)(2,1)S(1)}, bf16...) custom-call(bf16[1320,128]{1,0:T(8,128)(2,1)S(1)} %get-tuple-element, ...), custom_call_target="tpu_custom_call" | custom-call | flops 2000000000 | bytes 1000000 | tf_op jit(solution)/shard_map/pallas_call | solution.py:590
  21.6 0.0 collective-permute-done.3.side_ref
  21.6 4.7 %shard_map.122 = (bf16[32,2,8,80]{3,2,1,0:T(8,128)(2,1)S(1)}, bf16[2,320,128]{2,1,0:T(8,128)(2,1)S(1)}, bf16[2,160,128]{2,1,0:T(8,128)(2,1)S(1)}, bf16[2,2,160,128]{3,2,1,0:T(8,128)(2,1)S(1)}) custom-call(s32[1]{0:T(128)S(6)} %sub.3.right_ref, bf16[1960,128]{1,0:T(8,128)(2,1)S(1)} %collective-permute-done.3.side_ref, ...), custom_call_target="tpu_custom_call" | custom-call | flops 4000000000 | bytes 1000000 | tf_op jit(solution)/shard_map/pallas_call | solution.py:596
  26.4 0.7 %collective-permute-done.2.side_ref = bf16[1960,128]{1,0:T(8,128)(2,1)S(1)} collective-permute-done((bf16[1960,128]{1,0:T(8,128)(2,1)S(1)}, bf16[1960,128]{1,0:T(8,128)(2,1)S(1)}, u32[]{:S(2)}, u32[]{:S(2)}) %collective-permute-start.2) | collective-permute-done | bytes 501792 | tf_op jit(solution)/shard_map/ppermute | solution.py:513
  27.0 6.7 %shard_map.123 = bf16[32,8,8,80]{3,2,1,0:T(8,128)(2,1)} custom-call(s32[1]{0:T(128)S(6)} %sub.3.right_ref, bf16[1960,128]{1,0:T(8,128)(2,1)S(1)} %collective-permute-done.2.side_ref, bf16[1024,512]{1,0:T(8,128)(2,1)S(1)} %get-tuple-element.33.we_ref.refs_0_, f32[1,32]{1,0:T(1,128)S(1)} %bitcast.12, ...), custom_call_target="tpu_custom_call" | custom-call | flops 5000000000 | bytes 1000000 | tf_op jit(solution)/shard_map/pallas_call | solution.py:606
  (13 shorter events, 0.0 us)
Async XLA Ops:
  0.0 8.7 %copy-start = (bf16[128,256]{1,0:T(8,128)(2,1)S(1)}, bf16[128,256]{1,0:T(8,128)(2,1)}, u32[]{:S(2)}) copy-start(bf16[128,256]{1,0:T(8,128)(2,1)} %param.18) | copy-start | bytes 196612
  0.0 8.9 %copy-start.3 = (bf16[27,32,64]{2,1,0:T(8,128)(2,1)S(1)}, bf16[27,32,64]{2,1,0:T(8,128)(2,1)}, u32[]{:S(2)}) copy-start(bf16[27,32,64]{2,1,0:T(8,128)(2,1)} %wd_ref.1) | copy-start | bytes 331780
  0.0 8.9 %copy-start.1 = (bf16[27,128,128]{2,1,0:T(8,128)(2,1)S(1)}, bf16[27,128,128]{2,1,0:T(8,128)(2,1)}, u32[]{:S(2)}) copy-start(bf16[27,128,128]{2,1,0:T(8,128)(2,1)} %wc_ref.1) | copy-start | bytes 2654212
  0.0 8.9 %copy-start.4 = (bf16[128,256]{1,0:T(8,128)(2,1)S(1)}, bf16[128,256]{1,0:T(8,128)(2,1)}, u32[]{:S(2)}) copy-start(bf16[128,256]{1,0:T(8,128)(2,1)} %wn_ref.1) | copy-start | bytes 196612
  0.0 8.9 %copy-start.2 = (bf16[27,32,32]{2,1,0:T(8,128)(2,1)S(1)}, bf16[27,32,32]{2,1,0:T(8,128)(2,1)}, u32[]{:S(2)}) copy-start(bf16[27,32,32]{2,1,0:T(8,128)(2,1)} %we_ref.1) | copy-start | bytes 165892
  2.4 8.3 %collective-permute-start = (bf16[840,128]{1,0:T(8,128)(2,1)S(1)}, bf16[840,128]{1,0:T(8,128)(2,1)S(1)}, u32[]{:S(2)}, u32[]{:S(2)}) collective-permute-start(bf16[840,128]{1,0:T(8,128)(2,1)S(1)} %get-tuple-element.29), channel_id=1, source_target_pairs={{0,8},{8,16},{16,24},{24,32},{32,40},{40,48},{48,56},{56,64},{64,7... | collective-permute-start | bytes 645128 | tf_op jit(solution)/shard_map/ppermute | solution.py:505
  6.7 8.1 %collective-permute-start.1 = (bf16[840,128]{1,0:T(8,128)(2,1)S(1)}, bf16[840,128]{1,0:T(8,128)(2,1)S(1)}, u32[]{:S(2)}, u32[]{:S(2)}) collective-permute-start(bf16[840,128]{1,0:T(8,128)(2,1)S(1)} %get-tuple-element.30), channel_id=1, source_target_pairs={{8,0},{16,8},{24,16},{32,24},{40,32},{48,40},{56,48},{64,56},{72,6... | collective-permute-start | bytes 645128 | tf_op jit(solution)/shard_map/ppermute | solution.py:505
  9.0 11.0 %copy-start.7 = (f32[32]{0:T(128)S(1)}, f32[32]{0:T(128)}, u32[]{:S(2)}) copy-start(f32[32]{0:T(128)} %param.16) | copy-start | bytes 388
  15.1 6.5 %collective-permute-start.3 = (bf16[1960,128]{1,0:T(8,128)(2,1)S(1)}, bf16[1960,128]{1,0:T(8,128)(2,1)S(1)}, u32[]{:S(2)}, u32[]{:S(2)}) collective-permute-start(bf16[1960,128]{1,0:T(8,128)(2,1)S(1)} %get-tuple-element.46), channel_id=1, source_target_pairs={{0,1},{1,0},{2,3},{3,2},{4,5},{5,4},{6,7},{7,6},{8,9},{9,8},{10,11... | collective-permute-start | bytes 1505288 | tf_op jit(solution)/shard_map/ppermute | solution.py:513
  16.8 10.2 %collective-permute-start.2 = (bf16[1960,128]{1,0:T(8,128)(2,1)S(1)}, bf16[1960,128]{1,0:T(8,128)(2,1)S(1)}, u32[]{:S(2)}, u32[]{:S(2)}) collective-permute-start(bf16[1960,128]{1,0:T(8,128)(2,1)S(1)} %get-tuple-element.32), channel_id=1, source_target_pairs={{1,2},{2,1},{3,4},{4,3},{5,6},{6,5},{9,10},{10,9},{11,12},{12,11},... | collective-permute-start | bytes 1505288 | tf_op jit(solution)/shard_map/ppermute | solution.py:513
  20.0 1.6 %copy-start.5 = (s32[8,8,80]{2,1,0:T(8,128)S(1)}, s32[8,8,80]{2,1,0:T(8,128)}, u32[]{:S(2)}) copy-start(s32[8,8,80]{2,1,0:T(8,128)} %refs_8_.3) | copy-start | bytes 61444
  20.0 1.6 %copy-start.6 = (bf16[32,128]{1,0:T(8,128)(2,1)S(1)}, bf16[32,128]{1,0:T(8,128)(2,1)}, u32[]{:S(2)}) copy-start(bf16[32,128]{1,0:T(8,128)(2,1)} %refs_7_.3) | copy-start | bytes 24580
  20.0 1.6 %copy-start.8 = (f32[128]{0:T(128)S(1)}, f32[128]{0:T(128)}, u32[]{:S(2)}) copy-start(f32[128]{0:T(128)} %param.20) | copy-start | bytes 1540
  20.0 1.6 %copy-start.9 = (f32[32]{0:T(128)S(1)}, f32[32]{0:T(128)}, u32[]{:S(2)}) copy-start(f32[32]{0:T(128)} %param.23) | copy-start | bytes 388

commit v5 on v4

--- a/solution.py
+++ b/solution.py
@@ -47,10 +47,6 @@
 def unpick(rows, cols):
     row = iota((rows, cols), 0)
     return one_where(jnp.where(row < ZC, 2 * row, 2 * row - (Z - 1)) == iota((rows, cols), 1))
-
-
-def low_a(rows):
-    return iota((rows, LANES), 1) < 64
 
 
 def low_b(rows):
@@ -134,7 +130,7 @@
     lane_a = iota((PAIR, LANES), 1) >> 6
     for ref, right in ((far_ref, odd_ref[0]), (near_ref, 1 - odd_ref[0])):
         for i in range(2):
-            x = 2 * right + i
+            x = 3 * right + i * (1 - 2 * right)
             for cz in BITS:
                 at = i * PLANE + 4 * cz * PAIR
                 low, own, high = layer(x, cz)
@@ -276,14 +272,14 @@
         put_plane(a_ref, v_ref, x, layers, stacked(low_ends[z], high_ends[z]))
 
 
-def load_side(ref, right, a_ref, v_ref):
+def load_side(ref, a_ref, v_ref):
     for i in range(2):
         at = i * PLANE
         layers = [ref[at + 320 * cz : at + 320 * cz + 320] for cz in BITS]
-        put_plane(a_ref, v_ref, 1 + 6 * right + i, layers, ref[at + 640 : at + PLANE].astype(F32))
+        put_plane(a_ref, v_ref, 2 + i, layers, ref[at + 640 : at + PLANE].astype(F32))
     at = 2 * PLANE
     both = ref[at : at + 320].astype(F32)
-    put_plane(a_ref, v_ref, 9 * right, [both, pltpu.roll(both, 64, 1)], ref[at + 320 : at + HALF].astype(F32))
+    put_plane(a_ref, v_ref, 4, [both, pltpu.roll(both, 64, 1)], ref[at + 320 : at + HALF].astype(F32))
 
 
 def load_masks(at, parts, k_ref):
@@ -292,16 +288,12 @@
         m = jnp.maximum(k, pltpu.roll(k, LANES - 1, 1))
         m = jnp.maximum(m, pltpu.roll(m, LANES - 8, 1))
         m = jnp.maximum(m, pltpu.roll(m, LANES - 64, 1))
-        k_ref[0, at, by] = k
-        k_ref[1, at, by] = m
+        k_ref[0, at, by, 0:ZC] = k
+        k_ref[1, at, by, 0:ZC] = m
 
 
 def spread(k, index):
     return stacked(*[jnp.take_along_axis(k[8 * i : 8 * i + 8], index, axis=1, mode="promise_in_bounds") for i in range(5)])
-
-
-def local(i):
-    return (i + 1) >> 2, (i + 1) & 3
 
 
 def silu(v):
@@ -309,77 +301,86 @@
     return half + half * jnp.tanh(half)
 
 
-def joined_x(ref, x, cz, lane_a, rows):
-    return jnp.where(lane_a, ref[x + 1, cz, rows], ref[x - 1, cz, rows])
-
-
-def lanes_a(rows):
-    return one_where(low_a(rows)) > 0.5
-
-
-def encode(xi, ai, ei, a_ref, v_ref, k_ref, e_ref, ev_ref, c_ref, d_ref, o_ref, we_ref, be, wn_ref, gain, shift):
+def joined_x(ref, p, part, right, rows):
+    count = rows.stop - rows.start
+    takes_next = one_where((1 - (iota((count, LANES), 1) >> 6)) == right) > 0.5
+    return jnp.where(takes_next, ref[p + 1, part, rows], ref[p - 1, part, rows])
+
+
+def spans(ref, p, parts, right, rows):
+    return [ref[p, part, rows] for part in parts] + [joined_x(ref, p, part, right, rows) for part in parts]
+
+
+def encode_dot(p, right, a_ref, v_ref, we_ref):
+    every = slice(0, 320)
+    return nn(beside(*spans(a_ref, p, BITS, right, every), *spans(v_ref, p, BITS, right, every)), we_ref[...])
+
+
+def encode_finish(o, at, block, lx, k_ref, e_ref, ev_ref, be, wn_ref):
     z8 = depth_of(320)
     first, last = z8 == 0, z8 == ZC - 1
     lane = iota((8, LANES), 1)
-    lane_at = 8 * (lane >> 6) + ((lane >> 5) & 1)
-    la = lanes_a(320)
-    every = slice(0, 320)
-    lhs = [a_ref[ai, cz] for cz in BITS] + [joined_x(a_ref, ai, cz, la, every) for cz in BITS]
-    lhs += [v_ref[ai, cz] for cz in BITS] + [joined_x(v_ref, ai, cz, la, every) for cz in BITS]
-    o = nn(beside(*lhs), we_ref[...])
-    bx, lx = local(xi)
-    expanded = [[], []]
-    on = []
-    for yi in range(1, 9):
-        by, ly = local(yi)
-        k = k_ref[0, bx, by]
-        for cz in BITS:
-            expanded[cz].append(spread(k, lane_at + (64 * cz + 2 * ly + 16 * lx)))
-        on.append(spread(k_ref[1, bx, by], lane * 0 + (2 * ly + 16 * lx)))
-    on = stacked(*on)
+    lane_at = 8 * (lane >> 6) + ((lane >> 5) & 1) + 16 * lx
     pre = (
         o[:, 0:128] + moved(o[:, 256:384], 1, first) + be,
         o[:, 128:256] + moved(o[:, 384:512], -1, last) + be,
     )
     enc = []
     for cz in BITS:
-        e = jnp.where(stacked(*expanded[cz]) > 0.5, silu(pre[cz]), 0.0)
+        active = []
+        for yi in range(1, 9):
+            by, ly = (yi + 1) >> 2, (yi + 1) & 3
+            active.append(spread(k_ref[0, block, by, 0:ZC], lane_at + (64 * cz + 2 * ly)))
+        e = jnp.where(stacked(*active) > 0.5, silu(pre[cz]), 0.0)
         enc.append(e.astype(BF16))
-        e_ref[ei, cz] = enc[cz]
-        ev_ref[ei, cz] = jnp.where(low_b(160), e[120:280], e[40:200]).astype(BF16)
-    lifted = nt(beside(*enc), wn_ref[...])
+        e_ref[at, cz] = enc[cz]
+        ev_ref[at, cz, 0:160] = jnp.where(low_b(160), e[120:280], e[40:200]).astype(BF16)
+    return nt(beside(*enc), wn_ref[...])
+
+
+def strided_finish(lifted, at, block, lx, k_ref, c_ref, d_ref, o_ref, gain, shift):
+    where = iota((8, LANES), 1) * 0 + 16 * lx
+    on = []
+    for yi in range(1, 9):
+        by, ly = (yi + 1) >> 2, (yi + 1) & 3
+        on.append(spread(k_ref[1, block, by, 0:ZC], where + 2 * ly))
+    on = stacked(*on)
     c = jnp.where(on > 0.5, silu(lifted * gain + shift), 0.0)
-    c_ref[ei] = c.astype(BF16)
-    d_ref[ei] = c[40:280].astype(BF16)
-    o_ref[ei] = on[40:280]
-
-
-def coarse(xo, c_ref, d_ref, o_ref, u_ref, wc_ref, bc, wu_ref):
+    c_ref[at] = c.astype(BF16)
+    d_ref[at, 0:240] = c[40:280].astype(BF16)
+    o_ref[at, 0:240] = on[40:280]
+
+
+def coarse_dot(q, right, c_ref, d_ref, wc_ref):
+    lhs, rhs = [], []
+    for i in range(3):
+        lhs += [c_ref[q - 1 + i, 0:240], d_ref[q - 1 + i, 0:240], c_ref[q - 1 + i, 80:320]]
+        first = 768 * (1 - right) + 384 * i * (2 * right - 1)
+        rhs.append(wc_ref[pl.ds(pl.multiple_of(first, 384), 384)])
+    return nn(beside(*lhs), stacked(*rhs))
+
+
+def coarse_finish(p, q, at, o_ref, u_ref, bc, wu_ref):
     z6 = depth_of(240)
     first, last = z6 == 0, z6 == ZC - 1
-    lhs = []
-    for dx in range(3):
-        lhs += [c_ref[xo + dx, 0:240], d_ref[xo + dx], c_ref[xo + dx, 80:320]]
-    p = nn(beside(*lhs), wc_ref[...])
     s = p[:, 128:256] + moved(p[:, 0:128], 1, first) + moved(p[:, 256:384], -1, last) + bc
-    act = jnp.where(o_ref[xo + 1] > 0.5, silu(s), 0.0).astype(BF16)
+    act = jnp.where(o_ref[q, 0:240] > 0.5, silu(s), 0.0).astype(BF16)
     u = nt(act, stacked(*([wu_ref[...]] * 4)))
-    u_ref[xo, 0] = u[40:200].astype(BF16)
-    u_ref[xo, 1] = jnp.where(low_b(160), u[80:240], u[0:160]).astype(BF16)
-
-
-def decode(xo, e_ref, ev_ref, u_ref, wd_ref, bd, perm, back, m_ref, out_ref, at):
+    u_ref[at, 0, 0:160] = u[40:200].astype(BF16)
+    u_ref[at, 1, 0:160] = jnp.where(low_b(160), u[80:240], u[0:160]).astype(BF16)
+
+
+def decode_dot(p, right, e_ref, ev_ref, u_ref, wd_ref):
+    mid, every = slice(80, 240), slice(0, 160)
+    lhs = spans(e_ref, p, BITS, right, mid) + spans(ev_ref, p, BITS, right, every)
+    for v in BITS:
+        lhs += spans(u_ref, p, (v,), right, every)
+    return nn(beside(*lhs), wd_ref[...])
+
+
+def decode_finish(o, xo, bd, perm, back, m_ref, out_ref, at):
     z4 = depth_of(160)
     first, last = z4 == 0, z4 == ZC - 1
-    la = lanes_a(160)
-    mid, every = slice(80, 240), slice(0, 160)
-    x = xo + 2
-    lhs = [e_ref[x, cz, mid] for cz in BITS] + [joined_x(e_ref, x, cz, la, mid) for cz in BITS]
-    lhs += [ev_ref[x, cz] for cz in BITS] + [joined_x(ev_ref, x, cz, la, every) for cz in BITS]
-    x = xo + 1
-    for v in BITS:
-        lhs += [u_ref[x, v], joined_x(u_ref, x, v, la, every)]
-    o = nn(beside(*lhs), wd_ref[...])
     d0 = o[:, 0:128] + moved(o[:, 256:384], 1, first) + bd
     d1 = o[:, 128:256] + moved(o[:, 384:512], -1, last) + bd
     d = [beside(*[v[ZC * y : ZC * y + ZC] for y in range(4)]) for v in (d0, d1)]
@@ -398,54 +399,102 @@
     load_own(own_ref, low_ref, high_ref, a_ref, v_ref)
     load_masks(1, (low_ref[SIDE_MASK:SIDE_ROWS], own_ref[OWN : OWN + ZC], high_ref[SIDE_MASK:SIDE_ROWS]), k_ref)
     be = quad(be_ref[...])
+    dots = [encode_dot(1 + i, 1, a_ref, v_ref, we_ref) for i in range(2)]
+    lifted = [encode_finish(dots[i], i, 1, 1 + i, k_ref, e_ref, ev_ref, be, wn_ref) for i in range(2)]
     for i in range(2):
-        encode(
-            4 + i, 1 + i, i, a_ref, v_ref, k_ref, e_ref, ev_ref, c_ref, d_ref, o_ref, we_ref, be, wn_ref,
-            gain_ref[...], shift_ref[...],
-        )
-
-
-def side_work(right, side_ref, weights, own, scratch):
+        strided_finish(lifted[i], i, 1, 1 + i, k_ref, c_ref, d_ref, o_ref, gain_ref[...], shift_ref[...])
+
+
+def side_kernel(right, side_ref, weights, misc, own, scratch, decoded, given, emit):
     we_ref, be_ref, wn_ref, gain_ref, shift_ref, wc_ref, bc_ref, wu_ref = weights
+    m_ref, wd_ref, bd_ref, perm_ref, back_ref = misc
     a_ref, v_ref, e_ref, ev_ref, c_ref, d_ref, o_ref, k_ref, u_ref = scratch
     for i in range(2):
-        for ref, given in zip((a_ref, v_ref), own[0:2]):
-            ref[3 + 2 * right + i] = given[2 * right + i]
-        for ref, given in zip((e_ref, ev_ref, c_ref, d_ref, o_ref), own[2:7]):
-            ref[3 + i] = given[i]
+        at = right * (1 + 2 * i) + 1 - i
+        for ref, source in zip((a_ref, v_ref), own[0:2]):
+            ref[i] = source[at]
+        at = right * (2 * i - 1) + 1 - i
+        for ref, source in zip((c_ref, d_ref, o_ref), own[4:7]):
+            ref[i] = source[at]
+        for ref, source in zip((e_ref, ev_ref), own[2:4]):
+            ref[1 + i] = source[at]
         k_ref[i, 1] = own[7][i, 1]
-    load_side(side_ref, right, a_ref, v_ref)
+    if given is not None:
+        e_ref[0] = given[0][...]
+        ev_ref[0] = given[1][...]
+        for i in range(2):
+            u_ref[i] = given[2][1 - i]
+    load_side(side_ref, a_ref, v_ref)
     masks = side_ref[EDGE_MASK:EDGE_ROWS].astype(F32)
-    load_masks(2 * right, [masks[ZC * i : ZC * i + ZC] for i in range(3)], k_ref)
-    be = quad(be_ref[...])
-    for i in range(3):
-        xi = 5 * right + 1 + i
-        encode(
-            xi, xi, xi - 1, a_ref, v_ref, k_ref, e_ref, ev_ref, c_ref, d_ref, o_ref, we_ref, be, wn_ref,
-            gain_ref[...], shift_ref[...],
-        )
-    for i in range(3):
-        coarse(3 * right + i, c_ref, d_ref, o_ref, u_ref, wc_ref, bc_ref[...], wu_ref)
+    load_masks(0, [masks[ZC * i : ZC * i + ZC] for i in range(3)], k_ref)
+    be, bd = quad(be_ref[...]), quad(bd_ref[...])
+    gain, shift = gain_ref[...], shift_ref[...]
+    perm, back = perm_ref[...], back_ref[...]
+    block = (1, 0, 0)
+    lx = (3 * right, 3 - 3 * right, 2 - right)
+
+    def e_dot(i):
+        return encode_dot(1 + i, right, a_ref, v_ref, we_ref)
+
+    def e_finish(i, dot):
+        return encode_finish(dot, 3 + i, block[i], lx[i], k_ref, e_ref, ev_ref, be, wn_ref)
+
+    def s_finish(i, lifted):
+        strided_finish(lifted, 2 + i, block[i], lx[i], k_ref, c_ref, d_ref, o_ref, gain, shift)
+
+    def c_dot(i):
+        return coarse_dot(1 + i, right, c_ref, d_ref, wc_ref)
+
+    def c_finish(i, dot):
+        coarse_finish(dot, 1 + i, 2 + i, o_ref, u_ref, bc_ref[...], wu_ref)
+
+    def d_dot(i):
+        return decode_dot(1 + i, right, e_ref, ev_ref, u_ref, wd_ref)
+
+    def d_finish(i, dot):
+        emit(i, dot, bd, perm, back, m_ref)
+
+    e0 = e_dot(0)
+    e1 = e_dot(1)
+    l0 = e_finish(0, e0)
+    e2 = e_dot(2)
+    s_finish(0, l0)
+    l1 = e_finish(1, e1)
+    c0 = c_dot(0)
+    s_finish(1, l1)
+    l2 = e_finish(2, e2)
+    c_finish(0, c0)
+    c1 = c_dot(1)
+    s_finish(2, l2)
+    d0 = d_dot(0) if 0 in decoded else None
+    c_finish(1, c1)
+    c2 = c_dot(2)
+    if 0 in decoded:
+        d_finish(0, d0)
+    d1 = d_dot(1) if 1 in decoded else None
+    c_finish(2, c2)
+    d2 = d_dot(2)
+    if 1 in decoded:
+        d_finish(1, d1)
+    d_finish(2, d2)
 
 
 def near_kernel(right_ref, side_ref, *refs):
-    weights, (m_ref, wd_ref, bd_ref, perm_ref, back_ref), own = refs[:8], refs[8:13], refs[13:21]
     done_ref, e1_ref, ev1_ref, u1_ref = refs[21:25]
     scratch = refs[25:]
     right = right_ref[0]
-    side_work(right, side_ref, weights, own, scratch)
-    e_ref, ev_ref, u_ref = scratch[2], scratch[3], scratch[8]
-    decode(
-        3 * right, e_ref, ev_ref, u_ref, wd_ref, quad(bd_ref[...]), perm_ref[...], back_ref[...], m_ref, done_ref, 0
-    )
-    e1_ref[...] = e_ref[2 + 3 * right]
-    ev1_ref[...] = ev_ref[2 + 3 * right]
+
+    def emit(i, dot, bd, perm, back, m_ref):
+        decode_finish(dot, 3 * right, bd, perm, back, m_ref, done_ref, 0)
+
+    side_kernel(right, side_ref, refs[:8], refs[8:13], refs[13:21], scratch, (2,), None, emit)
+    e1_ref[...] = scratch[2][3]
+    ev1_ref[...] = scratch[3][3]
     for i in range(2):
-        u1_ref[i] = u_ref[1 + 2 * right + i]
+        u1_ref[i] = scratch[8][2 + i]
 
 
 def far_kernel(right_ref, side_ref, *refs):
-    weights, (m_ref, wd_ref, bd_ref, perm_ref, back_ref), own = refs[:8], refs[8:13], refs[13:21]
     done_ref, e1_ref, ev1_ref, u1_ref, out_hbm = refs[21:26]
     scratch = refs[26:35]
     out_ref, sems = refs[35:]
@@ -453,21 +502,18 @@
     right = 1 - left
     copies = [pltpu.make_async_copy(done_ref, out_hbm.at[:, pl.ds(6 * left, 2)], sems.at[3])]
     copies[0].start()
-    side_work(right, side_ref, weights, own, scratch)
-    e_ref, ev_ref, u_ref = scratch[2], scratch[3], scratch[8]
-    e_ref[2 + 3 * left] = e1_ref[...]
-    ev_ref[2 + 3 * left] = ev1_ref[...]
-    for i in range(2):
-        u_ref[1 + 2 * left + i] = u1_ref[i]
-    bd = quad(bd_ref[...])
-    for i in range(3):
-        decode(right + i, e_ref, ev_ref, u_ref, wd_ref, bd, perm_ref[...], back_ref[...], m_ref, out_ref, 2 * i)
+
+    def emit(i, dot, bd, perm, back, m_ref):
+        xo = right * (2 * i - 1) + 2 - i
+        decode_finish(dot, xo, bd, perm, back, m_ref, out_ref, 2 * i)
         copies.append(
-            pltpu.make_async_copy(
-                out_ref.at[:, pl.ds(2 * i, 2)], out_hbm.at[:, pl.ds(2 * (right + i), 2)], sems.at[i]
-            )
+            pltpu.make_async_copy(out_ref.at[:, pl.ds(2 * i, 2)], out_hbm.at[:, pl.ds(2 * xo, 2)], sems.at[i])
         )
         copies[-1].start()
+
+    side_kernel(
+        right, side_ref, refs[:8], refs[8:13], refs[13:21], scratch, (0, 1, 2), (e1_ref, ev1_ref, u1_ref), emit
+    )
     for copy in copies:
         copy.wait()
 
@@ -523,21 +569,21 @@
 SCALAR = [pl.BlockSpec(memory_space=pltpu.SMEM)]
 
 
-def state(own, planes):
-    masks = (2, 3, 3, ZC, LANES)
+def state(own, planes, more):
+    masks = (2, 2, 3, 64, LANES)
     return [
         ((own, 2, 320, LANES), BF16),
         ((own, 2, 320, LANES), BF16),
-        ((planes, 2, 320, LANES), BF16),
-        ((planes, 2, 160, LANES), BF16),
+        ((planes + more, 2, 320, LANES), BF16),
+        ((planes + more, 2, 192, LANES), BF16),
         ((planes, 320, LANES), BF16),
-        ((planes, 240, LANES), BF16),
-        ((planes, 240, LANES), F32),
+        ((planes, 256, LANES), BF16),
+        ((planes, 256, LANES), F32),
         (masks, F32),
     ]
 
 
-LIFTED = (6, 2, 160, LANES)
+LIFTED = (5, 2, 192, LANES)
 
 
 def on_device(
@@ -588,14 +634,14 @@
 
     encoder = (enc_w, b_enc[None], down_w, gains, shifts)
     mine = call(
-        own_kernel, [array(*d, kind=k) for d, k in state(4, 2)], vmem(8), vmem(8), [], 12, 2 * 10**9
+        own_kernel, [array(*d, kind=k) for d, k in state(4, 2, 0)], vmem(8), vmem(8), [], 12, 2 * 10**9
     )(own, low, high, *encoder)
     some = encoder + (coarse_w, b_coarse[None], w_up, voxel_mask, dec_w, b_dec[None], perm, back) + tuple(mine)
-    scratch = buffers(state(10, 8) + [(LIFTED, BF16)])
+    scratch = buffers(state(5, 5, 1) + [(LIFTED, BF16)])
     pair = (fine_in.shape[0], 2) + fine_in.shape[2:]
     done = call(
         near_kernel,
-        [array(*pair), array(2, 320, LANES), array(2, 160, LANES), array(2, 2, 160, LANES)],
+        [array(*pair), array(2, 320, LANES), array(2, 192, LANES), array(2, 2, 192, LANES)],
         SCALAR + vmem(22),
         vmem(4),
         scratch,

time: 34.1 us -> 32.3 us (0.947)
  Pallas kernels: 17 us -> 14.3 us
  waiting for transfers between devices: 5.06 us -> 6.2 us
    pallas_call x1, Pallas kernels: 6.7 us -> 5.06 us  [on_device(): call(far_kernel, [array(*fine_in.shape)], SCALAR + vmem(26), hbm(1), scra...]
    ppermute x2, waiting for transfers between devices: 0.65 us -> 1.81 us  [swapped(): return lax.ppermute(value, axis, pairs)]
    pallas_call x2, Pallas kernels: 6.26 us -> 5.29 us  [the longest x1 3.91 us: on_device(): call(near_kernel, [array(*pair), array(2, 320, LANES), array(2, 192, LANE...]
  transfers between devices with their start and end apart: 4 -> 4, of which waited for: 3 -> 3; matrix products, arithmetic and copies ran while one was open for 1% -> 1% of each run, Pallas kernels for 23% -> 21%
where the time goes in v5:
time: 32.3 us; the launch traced here: 32.1 us
  Pallas kernels  14.3 us (44%)
  starting transfers between devices  10.4 us (32%)
  waiting for transfers between devices  6.2 us (19%)
  between operations  0.85 us (3%)
    ppermute x2, starting transfers between devices, shifted(): lax.ppermute(value, axis, [(i, i + step) for i in range(peers) if 0 <= i...  5.67 us
    pallas_call x1, Pallas kernels, on_device(): call(far_kernel, [array(*fine_in.shape)], SCALAR + vmem(26), hbm(1), scra...  5.06 us
    ppermute x2, starting transfers between devices, swapped(): return lax.ppermute(value, axis, pairs)  4.75 us
    ppermute x2, waiting for transfers between devices, shifted(): lax.ppermute(value, axis, [(i, i + step) for i in range(peers) if 0 <= i...  4.39 us
    pallas_call x1, Pallas kernels, on_device(): call(near_kernel, [array(*pair), array(2, 320, LANES), array(2, 192, LANE...  3.91 us
    pallas_call x1, Pallas kernels, on_device(): call(pack_kernel, [array(OWN + ZC, LANES), array(SIDE_ROWS, LANES), array...  2.31 us
    ppermute x2, waiting for transfers between devices, swapped(): return lax.ppermute(value, axis, pairs)  1.81 us
    pallas_call x1, Pallas kernels, on_device(): call(weights_kernel, [array(1024, 512), array(1536, 512), array(128, 256)...  1.49 us
  transfers between devices with their start and end apart: 4, of which 3 were waited for; matrix products, arithmetic and copies ran while one was open for 1% of the time, Pallas kernels for 21%

profile of v5, /device:TPU:1, one launch (start us, length us, event | category | flops | bytes accessed | tf_op | source)
XLA Modules:
  0.0 32.1 jit_solution(15058566915328955237)
XLA Ops:
  0.0 2.3 %shard_map.118 = (bf16[1320,128]{1,0:T(8,128)(2,1)S(1)}, bf16[840,128]{1,0:T(8,128)(2,1)S(1)}, bf16[840,128]{1,0:T(8,128)(2,1)S(1)}) custom-call(bf16[32,8,8,80]{3,2,1,0:T(8,128)(2,1)} %x_hbm.1, s32[8,8,80]{2,1,0:T(8,128)} %refs_8_.3), custom_call_target="tpu_custom_call" | custom-call | flops 1000000000 | bytes 1000000 | tf_op jit(solution)/shard_map/pallas_call | solution.py:592
  2.4 4.4 %collective-permute-start = (bf16[840,128]{1,0:T(8,128)(2,1)S(1)}, bf16[840,128]{1,0:T(8,128)(2,1)S(1)}, u32[]{:S(2)}, u32[]{:S(2)}) collective-permute-start(bf16[840,128]{1,0:T(8,128)(2,1)S(1)} %get-tuple-element.29), channel_id=1, source_target_pairs={{0,8},{8,16},{16,24},{24,32},{32,40},{40,48},{48,56},{56,64},{64,7... | collective-permute-start | bytes 645128 | tf_op jit(solution)/shard_map/ppermute | solution.py:551
  6.7 1.3 %collective-permute-start.1 = (bf16[840,128]{1,0:T(8,128)(2,1)S(1)}, bf16[840,128]{1,0:T(8,128)(2,1)S(1)}, u32[]{:S(2)}, u32[]{:S(2)}) collective-permute-start(bf16[840,128]{1,0:T(8,128)(2,1)S(1)} %get-tuple-element.30), channel_id=1, source_target_pairs={{8,0},{16,8},{24,16},{32,24},{40,32},{48,40},{56,48},{64,56},{72,6... | collective-permute-start | bytes 645128 | tf_op jit(solution)/shard_map/ppermute | solution.py:551
  8.7 0.1 cosine_convert_fusion
  8.8 0.2 fusion
  8.9 0.0 copy-done.3
  8.9 0.0 copy-done.4
  8.9 0.0 copy-done.2
  9.0 0.0 copy-start.7
  9.0 1.5 %shard_map.119 = (bf16[1024,512]{1,0:T(8,128)(2,1)S(1)}, bf16[1536,512]{1,0:T(8,128)(2,1)S(1)}, bf16[128,256]{1,0:T(8,128)(2,1)S(1)}, bf16[512,512]{1,0:T(8,128)...) custom-call(bf16[27,32,32]{2,1,0:T(8,128)(2,1)S(1)} %copy-done.2, ...), custom_call_target="tpu_custom_call" | custom-call | flops 4000000000 | bytes 1000000 | tf_op jit(solution)/shard_map/pallas_call | solution.py:610
  10.5 0.2 collective-permute-done.low_ref
  10.7 4.2 %collective-permute-done.1.high_ref = bf16[840,128]{1,0:T(8,128)(2,1)S(1)} collective-permute-done((bf16[840,128]{1,0:T(8,128)(2,1)S(1)}, bf16[840,128]{1,0:T(8,128)(2,1)S(1)}, u32[]{:S(2)}, u32[]{:S(2)}) %collective-permute-start.1) | collective-permute-done | bytes 215072 | tf_op jit(solution)/shard_map/ppermute | solution.py:551
  14.9 0.2 shard_map.120
  15.1 1.7 %collective-permute-start.3 = (bf16[1960,128]{1,0:T(8,128)(2,1)S(1)}, bf16[1960,128]{1,0:T(8,128)(2,1)S(1)}, u32[]{:S(2)}, u32[]{:S(2)}) collective-permute-start(bf16[1960,128]{1,0:T(8,128)(2,1)S(1)} %get-tuple-element.46), channel_id=1, source_target_pairs={{0,1},{1,0},{2,3},{3,2},{4,5},{5,4},{6,7},{7,6},{8,9},{9,8},{10,11... | collective-permute-start | bytes 1505288 | tf_op jit(solution)/shard_map/ppermute | solution.py:559
  16.8 3.0 %collective-permute-start.2 = (bf16[1960,128]{1,0:T(8,128)(2,1)S(1)}, bf16[1960,128]{1,0:T(8,128)(2,1)S(1)}, u32[]{:S(2)}, u32[]{:S(2)}) collective-permute-start(bf16[1960,128]{1,0:T(8,128)(2,1)S(1)} %get-tuple-element.32), channel_id=1, source_target_pairs={{1,2},{2,1},{3,4},{4,3},{5,6},{6,5},{9,10},{10,9},{11,12},{12,11},... | collective-permute-start | bytes 1505288 | tf_op jit(solution)/shard_map/ppermute | solution.py:559
  19.8 0.0 copy-start.5
  19.8 0.0 copy-start.6
  19.8 0.0 copy-start.8
  19.9 0.0 copy-start.9
  19.9 1.4 %shard_map.121 = (bf16[4,2,320,128]{3,2,1,0:T(8,128)(2,1)S(1)}, bf16[4,2,320,128]{3,2,1,0:T(8,128)(2,1)S(1)}, bf16[2,2,320,128]{3,2,1,0:T(8,128)(2,1)S(1)}, bf16...) custom-call(bf16[1320,128]{1,0:T(8,128)(2,1)S(1)} %get-tuple-element, ...), custom_call_target="tpu_custom_call" | custom-call | flops 2000000000 | bytes 1000000 | tf_op jit(solution)/shard_map/pallas_call | solution.py:636
  21.3 0.0 collective-permute-done.3.side_ref
  21.3 3.9 %shard_map.122 = (bf16[32,2,8,80]{3,2,1,0:T(8,128)(2,1)S(1)}, bf16[2,320,128]{2,1,0:T(8,128)(2,1)S(1)}, bf16[2,192,128]{2,1,0:T(8,128)(2,1)S(1)}, bf16[2,2,192,128]{3,2,1,0:T(8,128)(2,1)S(1)}) custom-call(s32[1]{0:T(128)S(6)} %sub.3.right_ref, bf16[1960,128]{1,0:T(8,128)(2,1)S(1)} %collective-permute-done.3.side_ref, ...), custom_call_target="tpu_custom_call" | custom-call | flops 4000000000 | bytes 1000000 | tf_op jit(solution)/shard_map/pallas_call | solution.py:642
  25.2 1.8 %collective-permute-done.2.side_ref = bf16[1960,128]{1,0:T(8,128)(2,1)S(1)} collective-permute-done((bf16[1960,128]{1,0:T(8,128)(2,1)S(1)}, bf16[1960,128]{1,0:T(8,128)(2,1)S(1)}, u32[]{:S(2)}, u32[]{:S(2)}) %collective-permute-start.2) | collective-permute-done | bytes 501792 | tf_op jit(solution)/shard_map/ppermute | solution.py:559
  27.0 5.1 %shard_map.123 = bf16[32,8,8,80]{3,2,1,0:T(8,128)(2,1)} custom-call(s32[1]{0:T(128)S(6)} %sub.3.right_ref, bf16[1960,128]{1,0:T(8,128)(2,1)S(1)} %collective-permute-done.2.side_ref, bf16[1024,512]{1,0:T(8,128)(2,1)S(1)} %get-tuple-element.33.we_ref.refs_0_, f32[1,32]{1,0:T(1,128)S(1)} %bitcast.12, ...), custom_call_target="tpu_custom_call" | custom-call | flops 5000000000 | bytes 1000000 | tf_op jit(solution)/shard_map/pallas_call | solution.py:652
  (13 shorter events, 0.0 us)
Async XLA Ops:
  0.0 8.7 %copy-start = (bf16[128,256]{1,0:T(8,128)(2,1)S(1)}, bf16[128,256]{1,0:T(8,128)(2,1)}, u32[]{:S(2)}) copy-start(bf16[128,256]{1,0:T(8,128)(2,1)} %param.18) | copy-start | bytes 196612
  0.0 8.9 %copy-start.3 = (bf16[27,32,64]{2,1,0:T(8,128)(2,1)S(1)}, bf16[27,32,64]{2,1,0:T(8,128)(2,1)}, u32[]{:S(2)}) copy-start(bf16[27,32,64]{2,1,0:T(8,128)(2,1)} %wd_ref.1) | copy-start | bytes 331780
  0.0 8.9 %copy-start.1 = (bf16[27,128,128]{2,1,0:T(8,128)(2,1)S(1)}, bf16[27,128,128]{2,1,0:T(8,128)(2,1)}, u32[]{:S(2)}) copy-start(bf16[27,128,128]{2,1,0:T(8,128)(2,1)} %wc_ref.1) | copy-start | bytes 2654212
  0.0 8.9 %copy-start.4 = (bf16[128,256]{1,0:T(8,128)(2,1)S(1)}, bf16[128,256]{1,0:T(8,128)(2,1)}, u32[]{:S(2)}) copy-start(bf16[128,256]{1,0:T(8,128)(2,1)} %wn_ref.1) | copy-start | bytes 196612
  0.0 8.9 %copy-start.2 = (bf16[27,32,32]{2,1,0:T(8,128)(2,1)S(1)}, bf16[27,32,32]{2,1,0:T(8,128)(2,1)}, u32[]{:S(2)}) copy-start(bf16[27,32,32]{2,1,0:T(8,128)(2,1)} %we_ref.1) | copy-start | bytes 165892
  2.4 8.3 %collective-permute-start = (bf16[840,128]{1,0:T(8,128)(2,1)S(1)}, bf16[840,128]{1,0:T(8,128)(2,1)S(1)}, u32[]{:S(2)}, u32[]{:S(2)}) collective-permute-start(bf16[840,128]{1,0:T(8,128)(2,1)S(1)} %get-tuple-element.29), channel_id=1, source_target_pairs={{0,8},{8,16},{16,24},{24,32},{32,40},{40,48},{48,56},{56,64},{64,7... | collective-permute-start | bytes 645128 | tf_op jit(solution)/shard_map/ppermute | solution.py:551
  6.7 8.1 %collective-permute-start.1 = (bf16[840,128]{1,0:T(8,128)(2,1)S(1)}, bf16[840,128]{1,0:T(8,128)(2,1)S(1)}, u32[]{:S(2)}, u32[]{:S(2)}) collective-permute-start(bf16[840,128]{1,0:T(8,128)(2,1)S(1)} %get-tuple-element.30), channel_id=1, source_target_pairs={{8,0},{16,8},{24,16},{32,24},{40,32},{48,40},{56,48},{64,56},{72,6... | collective-permute-start | bytes 645128 | tf_op jit(solution)/shard_map/ppermute | solution.py:551
  9.0 10.9 %copy-start.7 = (f32[32]{0:T(128)S(1)}, f32[32]{0:T(128)}, u32[]{:S(2)}) copy-start(f32[32]{0:T(128)} %param.16) | copy-start | bytes 388
  15.1 6.2 %collective-permute-start.3 = (bf16[1960,128]{1,0:T(8,128)(2,1)S(1)}, bf16[1960,128]{1,0:T(8,128)(2,1)S(1)}, u32[]{:S(2)}, u32[]{:S(2)}) collective-permute-start(bf16[1960,128]{1,0:T(8,128)(2,1)S(1)} %get-tuple-element.46), channel_id=1, source_target_pairs={{0,1},{1,0},{2,3},{3,2},{4,5},{5,4},{6,7},{7,6},{8,9},{9,8},{10,11... | collective-permute-start | bytes 1505288 | tf_op jit(solution)/shard_map/ppermute | solution.py:559
  16.8 10.2 %collective-permute-start.2 = (bf16[1960,128]{1,0:T(8,128)(2,1)S(1)}, bf16[1960,128]{1,0:T(8,128)(2,1)S(1)}, u32[]{:S(2)}, u32[]{:S(2)}) collective-permute-start(bf16[1960,128]{1,0:T(8,128)(2,1)S(1)} %get-tuple-element.32), channel_id=1, source_target_pairs={{1,2},{2,1},{3,4},{4,3},{5,6},{6,5},{9,10},{10,9},{11,12},{12,11},... | collective-permute-start | bytes 1505288 | tf_op jit(solution)/shard_map/ppermute | solution.py:559
  19.8 1.4 %copy-start.5 = (s32[8,8,80]{2,1,0:T(8,128)S(1)}, s32[8,8,80]{2,1,0:T(8,128)}, u32[]{:S(2)}) copy-start(s32[8,8,80]{2,1,0:T(8,128)} %refs_8_.3) | copy-start | bytes 61444
  19.8 1.4 %copy-start.6 = (bf16[32,128]{1,0:T(8,128)(2,1)S(1)}, bf16[32,128]{1,0:T(8,128)(2,1)}, u32[]{:S(2)}) copy-start(bf16[32,128]{1,0:T(8,128)(2,1)} %refs_7_.3) | copy-start | bytes 24580
  19.8 1.4 %copy-start.8 = (f32[128]{0:T(128)S(1)}, f32[128]{0:T(128)}, u32[]{:S(2)}) copy-start(f32[128]{0:T(128)} %param.20) | copy-start | bytes 1540
  19.9 1.4 %copy-start.9 = (f32[32]{0:T(128)S(1)}, f32[32]{0:T(128)}, u32[]{:S(2)}) copy-start(f32[32]{0:T(128)} %param.23) | copy-start | bytes 388

commit v6 on v5

--- a/solution.py
+++ b/solution.py
@@ -36,8 +36,7 @@
 SIDE_ROWS = SIDE_MASK + ZC
 PLANE = 9 * PAIR
 HALF = 5 * PAIR
-EDGE_MASK = 2 * PLANE + HALF
-EDGE_ROWS = EDGE_MASK + 3 * ZC
+MASKS = 3 * ZC
 
 
 def one_where(truth):
@@ -112,7 +111,7 @@
     return pl.ds(pl.multiple_of(x * size, size), size)
 
 
-def mid_kernel(odd_ref, own_ref, low_ref, high_ref, tie_ref, tie2_ref, far_ref, near_ref, ends_ref):
+def mid_kernel(odd_ref, own_ref, low_ref, high_ref, tie_ref, tie2_ref, far_a_ref, far_b_ref, near_ref, ends_ref):
     ends_ref[0] = low_ref[SIDE:SIDE_MASK].astype(F32)
     ends_ref[1] = high_ref[SIDE:SIDE_MASK].astype(F32)
 
@@ -128,27 +127,38 @@
         return stacked(ends_ref[0, at], ends_ref[1, at]).astype(BF16)
 
     lane_a = iota((PAIR, LANES), 1) >> 6
-    for ref, right in ((far_ref, odd_ref[0]), (near_ref, 1 - odd_ref[0])):
-        for i in range(2):
-            x = 3 * right + i * (1 - 2 * right)
-            for cz in BITS:
-                at = i * PLANE + 4 * cz * PAIR
-                low, own, high = layer(x, cz)
-                ref[at : at + PAIR] = low
-                ref[at + PAIR : at + 3 * PAIR] = own
-                ref[at + 3 * PAIR : at + 4 * PAIR] = high
-            ref[i * PLANE + 8 * PAIR : (i + 1) * PLANE] = ends(x)
-        x = 2 - right
+
+    def full(ref, at, x):
+        for cz in BITS:
+            low, own, high = layer(x, cz)
+            ref[at : at + PAIR] = low
+            ref[at + PAIR : at + 3 * PAIR] = own
+            ref[at + 3 * PAIR : at + 4 * PAIR] = high
+            at = at + 4 * PAIR
+        ref[at : at + PAIR] = ends(x)
+
+    def half(ref, at, x, right):
         pieces = []
         for cz in BITS:
             low, own, high = layer(x, cz)
             pieces.append([v.astype(F32) for v in (low, own[:PAIR], own[PAIR:], high)])
         for i in range(4):
             v = jnp.where(lane_a == right, pieces[0][i], pltpu.roll(pieces[1][i], 64, 1))
-            ref[2 * PLANE + i * PAIR : 2 * PLANE + (i + 1) * PAIR] = v.astype(BF16)
-        ref[2 * PLANE + 4 * PAIR : EDGE_MASK] = ends(x)
-        masks = [low_ref[SIDE_MASK:SIDE_ROWS], own_ref[OWN : OWN + ZC], high_ref[SIDE_MASK:SIDE_ROWS]]
-        ref[EDGE_MASK:EDGE_ROWS] = stacked(*[m.astype(F32) for m in masks]).astype(BF16)
+            ref[at + i * PAIR : at + (i + 1) * PAIR] = v.astype(BF16)
+        ref[at + 4 * PAIR : at + HALF] = ends(x)
+
+    def masks(ref, at):
+        parts = [low_ref[SIDE_MASK:SIDE_ROWS], own_ref[OWN : OWN + ZC], high_ref[SIDE_MASK:SIDE_ROWS]]
+        ref[at : at + MASKS] = stacked(*[m.astype(F32) for m in parts]).astype(BF16)
+
+    for (a_ref, a_at), (b_ref, b_at), (m_ref, m_at), right in (
+        ((far_a_ref, 0), (far_b_ref, 0), (far_a_ref, PLANE), odd_ref[0]),
+        ((near_ref, 0), (near_ref, PLANE), (near_ref, 2 * PLANE + HALF), 1 - odd_ref[0]),
+    ):
+        full(a_ref, a_at, 3 * right)
+        full(b_ref, b_at, 1 + right)
+        half(b_ref, b_at + PLANE, 2 - right, right)
+        masks(m_ref, m_at)
 
 
 def tap_of(out_bit, in_bit, far):
@@ -246,15 +256,15 @@
     return beside(bias, bias, bias, bias)
 
 
-def put_plane(a_ref, v_ref, at, layers, ends):
+def put_plane(a_ref, v_ref, layers, ends):
     y0, y9 = ends[:ZC].astype(F32), ends[ZC:].astype(F32)
     for cz in BITS:
-        a_ref[at, cz] = layers[cz].astype(BF16)
+        a_ref[cz] = layers[cz].astype(BF16)
         f = layers[cz].astype(F32)
         if cz == 1:
             y0, y9 = pltpu.roll(y0, 32, 1), pltpu.roll(y9, LANES - 32, 1)
         f = stacked(y0, f, y9)
-        v_ref[at, cz] = jnp.where(low_b(320), f[PAIR:], f[:320]).astype(BF16)
+        v_ref[cz] = jnp.where(low_b(320), f[PAIR:], f[:320]).astype(BF16)
 
 
 def load_own(own_ref, low_ref, high_ref, a_ref, v_ref):
@@ -269,27 +279,32 @@
                 stacked(low_ref[at : at + PAIR], own_ref[mine : mine + 2 * PAIR], high_ref[at : at + PAIR])
             )
         z = slice(ZC * x, ZC * x + ZC)
-        put_plane(a_ref, v_ref, x, layers, stacked(low_ends[z], high_ends[z]))
-
-
-def load_side(ref, a_ref, v_ref):
-    for i in range(2):
-        at = i * PLANE
-        layers = [ref[at + 320 * cz : at + 320 * cz + 320] for cz in BITS]
-        put_plane(a_ref, v_ref, 2 + i, layers, ref[at + 640 : at + PLANE].astype(F32))
-    at = 2 * PLANE
+        put_plane(a_ref.at[x], v_ref.at[x], layers, stacked(low_ends[z], high_ends[z]))
+
+
+def load_full(ref, at, a_ref, v_ref):
+    layers = [ref[at + 320 * cz : at + 320 * cz + 320] for cz in BITS]
+    put_plane(a_ref, v_ref, layers, ref[at + 640 : at + PLANE].astype(F32))
+
+
+def load_half(ref, at, a_ref, v_ref):
     both = ref[at : at + 320].astype(F32)
-    put_plane(a_ref, v_ref, 4, [both, pltpu.roll(both, 64, 1)], ref[at + 320 : at + HALF].astype(F32))
-
-
-def load_masks(at, parts, k_ref):
+    put_plane(a_ref, v_ref, [both, pltpu.roll(both, 64, 1)], ref[at + 320 : at + HALF].astype(F32))
+
+
+def load_masks(parts, k_ref):
     for by, k in enumerate(parts):
         k = k.astype(F32)
         m = jnp.maximum(k, pltpu.roll(k, LANES - 1, 1))
         m = jnp.maximum(m, pltpu.roll(m, LANES - 8, 1))
         m = jnp.maximum(m, pltpu.roll(m, LANES - 64, 1))
-        k_ref[0, at, by, 0:ZC] = k
-        k_ref[1, at, by, 0:ZC] = m
+        k_ref[0, by, 0:ZC] = k
+        k_ref[1, by, 0:ZC] = m
+
+
+def load_side_masks(ref, at, k_ref):
+    masks = ref[at : at + MASKS].astype(F32)
+    load_masks([masks[ZC * i : ZC * i + ZC] for i in range(3)], k_ref)
 
 
 def spread(k, index):
@@ -301,22 +316,22 @@
     return half + half * jnp.tanh(half)
 
 
-def joined_x(ref, p, part, right, rows):
+def joined_x(planes, p, part, right, rows):
     count = rows.stop - rows.start
     takes_next = one_where((1 - (iota((count, LANES), 1) >> 6)) == right) > 0.5
-    return jnp.where(takes_next, ref[p + 1, part, rows], ref[p - 1, part, rows])
-
-
-def spans(ref, p, parts, right, rows):
-    return [ref[p, part, rows] for part in parts] + [joined_x(ref, p, part, right, rows) for part in parts]
-
-
-def encode_dot(p, right, a_ref, v_ref, we_ref):
+    return jnp.where(takes_next, planes[p + 1][part, rows], planes[p - 1][part, rows])
+
+
+def spans(planes, p, parts, right, rows):
+    return [planes[p][part, rows] for part in parts] + [joined_x(planes, p, part, right, rows) for part in parts]
+
+
+def encode_dot(p, right, a, v, we_ref):
     every = slice(0, 320)
-    return nn(beside(*spans(a_ref, p, BITS, right, every), *spans(v_ref, p, BITS, right, every)), we_ref[...])
-
-
-def encode_finish(o, at, block, lx, k_ref, e_ref, ev_ref, be, wn_ref):
+    return nn(beside(*spans(a, p, BITS, right, every), *spans(v, p, BITS, right, every)), we_ref[...])
+
+
+def encode_finish(o, lx, k_ref, e_ref, ev_ref, be, wn_ref):
     z8 = depth_of(320)
     first, last = z8 == 0, z8 == ZC - 1
     lane = iota((8, LANES), 1)
@@ -330,51 +345,53 @@
         active = []
         for yi in range(1, 9):
             by, ly = (yi + 1) >> 2, (yi + 1) & 3
-            active.append(spread(k_ref[0, block, by, 0:ZC], lane_at + (64 * cz + 2 * ly)))
+            active.append(spread(k_ref[0, by, 0:ZC], lane_at + (64 * cz + 2 * ly)))
         e = jnp.where(stacked(*active) > 0.5, silu(pre[cz]), 0.0)
         enc.append(e.astype(BF16))
-        e_ref[at, cz] = enc[cz]
-        ev_ref[at, cz, 0:160] = jnp.where(low_b(160), e[120:280], e[40:200]).astype(BF16)
+        if e_ref is None:
+            continue
+        e_ref[cz] = enc[cz]
+        ev_ref[cz, 0:160] = jnp.where(low_b(160), e[120:280], e[40:200]).astype(BF16)
     return nt(beside(*enc), wn_ref[...])
 
 
-def strided_finish(lifted, at, block, lx, k_ref, c_ref, d_ref, o_ref, gain, shift):
+def strided_finish(lifted, lx, k_ref, c_ref, d_ref, o_ref, gain, shift):
     where = iota((8, LANES), 1) * 0 + 16 * lx
     on = []
     for yi in range(1, 9):
         by, ly = (yi + 1) >> 2, (yi + 1) & 3
-        on.append(spread(k_ref[1, block, by, 0:ZC], where + 2 * ly))
+        on.append(spread(k_ref[1, by, 0:ZC], where + 2 * ly))
     on = stacked(*on)
     c = jnp.where(on > 0.5, silu(lifted * gain + shift), 0.0)
-    c_ref[at] = c.astype(BF16)
-    d_ref[at, 0:240] = c[40:280].astype(BF16)
-    o_ref[at, 0:240] = on[40:280]
-
-
-def coarse_dot(q, right, c_ref, d_ref, wc_ref):
+    c_ref[...] = c.astype(BF16)
+    d_ref[0:240] = c[40:280].astype(BF16)
+    o_ref[0:240] = on[40:280]
+
+
+def coarse_dot(q, right, c, d, wc_ref):
     lhs, rhs = [], []
     for i in range(3):
-        lhs += [c_ref[q - 1 + i, 0:240], d_ref[q - 1 + i, 0:240], c_ref[q - 1 + i, 80:320]]
+        lhs += [c[q - 1 + i][0:240], d[q - 1 + i][0:240], c[q - 1 + i][80:320]]
         first = 768 * (1 - right) + 384 * i * (2 * right - 1)
         rhs.append(wc_ref[pl.ds(pl.multiple_of(first, 384), 384)])
     return nn(beside(*lhs), stacked(*rhs))
 
 
-def coarse_finish(p, q, at, o_ref, u_ref, bc, wu_ref):
+def coarse_finish(p, o_ref, u_ref, bc, wu_ref):
     z6 = depth_of(240)
     first, last = z6 == 0, z6 == ZC - 1
     s = p[:, 128:256] + moved(p[:, 0:128], 1, first) + moved(p[:, 256:384], -1, last) + bc
-    act = jnp.where(o_ref[q, 0:240] > 0.5, silu(s), 0.0).astype(BF16)
+    act = jnp.where(o_ref[0:240] > 0.5, silu(s), 0.0).astype(BF16)
     u = nt(act, stacked(*([wu_ref[...]] * 4)))
-    u_ref[at, 0, 0:160] = u[40:200].astype(BF16)
-    u_ref[at, 1, 0:160] = jnp.where(low_b(160), u[80:240], u[0:160]).astype(BF16)
-
-
-def decode_dot(p, right, e_ref, ev_ref, u_ref, wd_ref):
+    u_ref[0, 0:160] = u[40:200].astype(BF16)
+    u_ref[1, 0:160] = jnp.where(low_b(160), u[80:240], u[0:160]).astype(BF16)
+
+
+def decode_dot(p, right, e, ev, u, wd_ref):
     mid, every = slice(80, 240), slice(0, 160)
-    lhs = spans(e_ref, p, BITS, right, mid) + spans(ev_ref, p, BITS, right, every)
+    lhs = spans(e, p, BITS, right, mid) + spans(ev, p, BITS, right, every)
     for v in BITS:
-        lhs += spans(u_ref, p, (v,), right, every)
+        lhs += spans(u, p, (v,), right, every)
     return nn(beside(*lhs), wd_ref[...])
 
 
@@ -397,123 +414,169 @@
     o_ref, k_ref
 ):
     load_own(own_ref, low_ref, high_ref, a_ref, v_ref)
-    load_masks(1, (low_ref[SIDE_MASK:SIDE_ROWS], own_ref[OWN : OWN + ZC], high_ref[SIDE_MASK:SIDE_ROWS]), k_ref)
+    load_masks((low_ref[SIDE_MASK:SIDE_ROWS], own_ref[OWN : OWN + ZC], high_ref[SIDE_MASK:SIDE_ROWS]), k_ref)
     be = quad(be_ref[...])
-    dots = [encode_dot(1 + i, 1, a_ref, v_ref, we_ref) for i in range(2)]
-    lifted = [encode_finish(dots[i], i, 1, 1 + i, k_ref, e_ref, ev_ref, be, wn_ref) for i in range(2)]
+    a, v = ([ref.at[x] for x in range(4)] for ref in (a_ref, v_ref))
+    dots = [encode_dot(1 + i, 1, a, v, we_ref) for i in range(2)]
+    lifted = [encode_finish(dots[i], 1 + i, k_ref, e_ref.at[i], ev_ref.at[i], be, wn_ref) for i in range(2)]
     for i in range(2):
-        strided_finish(lifted[i], i, 1, 1 + i, k_ref, c_ref, d_ref, o_ref, gain_ref[...], shift_ref[...])
-
-
-def side_kernel(right, side_ref, weights, misc, own, scratch, decoded, given, emit):
-    we_ref, be_ref, wn_ref, gain_ref, shift_ref, wc_ref, bc_ref, wu_ref = weights
-    m_ref, wd_ref, bd_ref, perm_ref, back_ref = misc
-    a_ref, v_ref, e_ref, ev_ref, c_ref, d_ref, o_ref, k_ref, u_ref = scratch
+        strided_finish(
+            lifted[i], 1 + i, k_ref, c_ref.at[i], d_ref.at[i], o_ref.at[i], gain_ref[...], shift_ref[...]
+        )
+
+
+def own_planes(right, own):
+    two = [right * (1 + 2 * i) + 1 - i for i in range(2)]
+    one = [right * (2 * i - 1) + 1 - i for i in range(2)]
+    a, v = ([ref.at[at] for at in two] for ref in own[0:2])
+    e, ev, c, d, o = ([ref.at[at] for at in one] for ref in own[2:7])
+    return a, v, e, ev, c, d, o
+
+
+class Stages:
+    def __init__(self, right, weights, misc, planes, side_k, own_k, emit):
+        self.right, self.planes, self.emit = right, planes, emit
+        self.we, be, self.wn, gain, shift, self.wc, bc, self.wu = weights
+        self.m, self.wd, bd, perm, back = misc
+        self.be, self.bd = quad(be[...]), quad(bd[...])
+        self.gain, self.shift, self.bc = gain[...], shift[...], bc[...]
+        self.perm, self.back = perm[...], back[...]
+        self.k = (own_k, side_k, side_k)
+        self.lx = (3 * right, 3 - 3 * right, 2 - right)
+
+    def e_dot(self, i):
+        return encode_dot(1 + i, self.right, self.planes[0], self.planes[1], self.we)
+
+    def e_finish(self, i, dot):
+        e, ev = self.planes[2], self.planes[3]
+        at = (e[3 + i], ev[3 + i]) if i < 2 else (None, None)
+        return encode_finish(dot, self.lx[i], self.k[i], *at, self.be, self.wn)
+
+    def s_finish(self, i, lifted):
+        c, d, o = self.planes[4:7]
+        strided_finish(lifted, self.lx[i], self.k[i], c[2 + i], d[2 + i], o[2 + i], self.gain, self.shift)
+
+    def c_dot(self, i):
+        return coarse_dot(1 + i, self.right, self.planes[4], self.planes[5], self.wc)
+
+    def c_finish(self, i, dot):
+        coarse_finish(dot, self.planes[6][1 + i], self.planes[7][2 + i], self.bc, self.wu)
+
+    def d_dot(self, i):
+        return decode_dot(1 + i, self.right, self.planes[2], self.planes[3], self.planes[7], self.wd)
+
+    def d_finish(self, i, dot):
+        self.emit(i, dot, self.bd, self.perm, self.back, self.m)
+
+
+def near_kernel(right_ref, side_ref, *refs):
+    weights, misc, own = refs[:8], refs[8:13], refs[13:21]
+    done_ref, e1_ref, ev1_ref, u1_ref = refs[21:25]
+    a_ref, v_ref, e_ref, ev_ref, c_ref, d_ref, o_ref, k_ref, u_ref = refs[25:]
+    right = right_ref[0]
+    a, v, e, ev, c, d, o = own_planes(right, own)
+    a, v, c, d, o = (x + [r.at[i] for i in range(3)] for x, r in zip((a, v, c, d, o), (a_ref, v_ref, c_ref, d_ref, o_ref)))
+    e, ev = [None] + e + [e1_ref, e_ref.at[0]], [None] + ev + [ev1_ref, ev_ref.at[0]]
+    u = [None, None, u1_ref.at[0], u1_ref.at[1], u_ref.at[0]]
     for i in range(2):
-        at = right * (1 + 2 * i) + 1 - i
-        for ref, source in zip((a_ref, v_ref), own[0:2]):
-            ref[i] = source[at]
-        at = right * (2 * i - 1) + 1 - i
-        for ref, source in zip((c_ref, d_ref, o_ref), own[4:7]):
-            ref[i] = source[at]
-        for ref, source in zip((e_ref, ev_ref), own[2:4]):
-            ref[1 + i] = source[at]
-        k_ref[i, 1] = own[7][i, 1]
-    if given is not None:
-        e_ref[0] = given[0][...]
-        ev_ref[0] = given[1][...]
-        for i in range(2):
-            u_ref[i] = given[2][1 - i]
-    load_side(side_ref, a_ref, v_ref)
-    masks = side_ref[EDGE_MASK:EDGE_ROWS].astype(F32)
-    load_masks(0, [masks[ZC * i : ZC * i + ZC] for i in range(3)], k_ref)
-    be, bd = quad(be_ref[...]), quad(bd_ref[...])
-    gain, shift = gain_ref[...], shift_ref[...]
-    perm, back = perm_ref[...], back_ref[...]
-    block = (1, 0, 0)
-    lx = (3 * right, 3 - 3 * right, 2 - right)
-
-    def e_dot(i):
-        return encode_dot(1 + i, right, a_ref, v_ref, we_ref)
-
-    def e_finish(i, dot):
-        return encode_finish(dot, 3 + i, block[i], lx[i], k_ref, e_ref, ev_ref, be, wn_ref)
-
-    def s_finish(i, lifted):
-        strided_finish(lifted, 2 + i, block[i], lx[i], k_ref, c_ref, d_ref, o_ref, gain, shift)
-
-    def c_dot(i):
-        return coarse_dot(1 + i, right, c_ref, d_ref, wc_ref)
-
-    def c_finish(i, dot):
-        coarse_finish(dot, 1 + i, 2 + i, o_ref, u_ref, bc_ref[...], wu_ref)
-
-    def d_dot(i):
-        return decode_dot(1 + i, right, e_ref, ev_ref, u_ref, wd_ref)
-
-    def d_finish(i, dot):
-        emit(i, dot, bd, perm, back, m_ref)
-
-    e0 = e_dot(0)
-    e1 = e_dot(1)
-    l0 = e_finish(0, e0)
-    e2 = e_dot(2)
-    s_finish(0, l0)
-    l1 = e_finish(1, e1)
-    c0 = c_dot(0)
-    s_finish(1, l1)
-    l2 = e_finish(2, e2)
-    c_finish(0, c0)
-    c1 = c_dot(1)
-    s_finish(2, l2)
-    d0 = d_dot(0) if 0 in decoded else None
-    c_finish(1, c1)
-    c2 = c_dot(2)
-    if 0 in decoded:
-        d_finish(0, d0)
-    d1 = d_dot(1) if 1 in decoded else None
-    c_finish(2, c2)
-    d2 = d_dot(2)
-    if 1 in decoded:
-        d_finish(1, d1)
-    d_finish(2, d2)
-
-
-def near_kernel(right_ref, side_ref, *refs):
-    done_ref, e1_ref, ev1_ref, u1_ref = refs[21:25]
-    scratch = refs[25:]
-    right = right_ref[0]
+        load_full(side_ref, i * PLANE, a[2 + i], v[2 + i])
+    load_half(side_ref, 2 * PLANE, a[4], v[4])
+    load_side_masks(side_ref, 2 * PLANE + HALF, k_ref)
 
     def emit(i, dot, bd, perm, back, m_ref):
         decode_finish(dot, 3 * right, bd, perm, back, m_ref, done_ref, 0)
 
-    side_kernel(right, side_ref, refs[:8], refs[8:13], refs[13:21], scratch, (2,), None, emit)
-    e1_ref[...] = scratch[2][3]
-    ev1_ref[...] = scratch[3][3]
-    for i in range(2):
-        u1_ref[i] = scratch[8][2 + i]
-
-
-def far_kernel(right_ref, side_ref, *refs):
-    done_ref, e1_ref, ev1_ref, u1_ref, out_hbm = refs[21:26]
-    scratch = refs[26:35]
-    out_ref, sems = refs[35:]
+    w = Stages(right, weights, misc, (a, v, e, ev, c, d, o, u), k_ref, own[7], emit)
+    e0 = w.e_dot(0)
+    e1 = w.e_dot(1)
+    l0 = w.e_finish(0, e0)
+    e2 = w.e_dot(2)
+    w.s_finish(0, l0)
+    l1 = w.e_finish(1, e1)
+    c0 = w.c_dot(0)
+    w.s_finish(1, l1)
+    l2 = w.e_finish(2, e2)
+    w.c_finish(0, c0)
+    c1 = w.c_dot(1)
+    w.s_finish(2, l2)
+    w.c_finish(1, c1)
+    c2 = w.c_dot(2)
+    w.c_finish(2, c2)
+    w.d_finish(2, w.d_dot(2))
+
+
+def far_place(right, i):
+    return right * (2 * i - 1) + 2 - i
+
+
+def first_kernel(right_ref, side_ref, *refs):
+    weights, misc, own = refs[:8], refs[8:13], refs[13:21]
+    e1_ref, ev1_ref, u1_ref = refs[21:24]
+    done_ref, a_ref, v_ref, e_ref, ev_ref, c_ref, d_ref, o_ref, k_ref, u_ref = refs[24:]
+    right = 1 - right_ref[0]
+    a, v, e, ev, c, d, o = own_planes(right, own)
+    a, v, c, d, o = (x + [r] for x, r in zip((a, v, c, d, o), (a_ref, v_ref, c_ref, d_ref, o_ref)))
+    e, ev = [e1_ref] + e + [e_ref], [ev1_ref] + ev + [ev_ref]
+    u = [u1_ref.at[1], u1_ref.at[0], u_ref]
+    load_full(side_ref, 0, a[2], v[2])
+    load_side_masks(side_ref, PLANE, k_ref)
+
+    def emit(i, dot, bd, perm, back, m_ref):
+        decode_finish(dot, far_place(right, i), bd, perm, back, m_ref, done_ref, 0)
+
+    w = Stages(right, weights, misc, (a, v, e, ev, c, d, o, u), k_ref, own[7], emit)
+    w.s_finish(0, w.e_finish(0, w.e_dot(0)))
+    w.c_finish(0, w.c_dot(0))
+    w.d_finish(0, w.d_dot(0))
+
+
+def last_kernel(right_ref, side_ref, *refs):
+    weights, misc, own = refs[:8], refs[8:13], refs[13:21]
+    near_done_ref, u1_ref = refs[21:23]
+    done_ref, a1_ref, v1_ref, e1_ref, ev1_ref, c1_ref, d1_ref, o1_ref, k_ref, u0_ref = refs[23:33]
+    out_hbm = refs[33]
+    a_ref, v_ref, e_ref, ev_ref, c_ref, d_ref, o_ref, u_ref, out_ref, sems = refs[34:]
     left = right_ref[0]
     right = 1 - left
-    copies = [pltpu.make_async_copy(done_ref, out_hbm.at[:, pl.ds(6 * left, 2)], sems.at[3])]
-    copies[0].start()
+    copies = [
+        pltpu.make_async_copy(near_done_ref, out_hbm.at[:, pl.ds(6 * left, 2)], sems.at[2]),
+        pltpu.make_async_copy(done_ref, out_hbm.at[:, pl.ds(2 * far_place(right, 0), 2)], sems.at[3]),
+    ]
+    for copy in copies:
+        copy.start()
+    a, v, e, ev, c, d, o = own_planes(right, own)
+    a, v, c, d, o = (
+        x + [g] + [r.at[i] for i in range(2)]
+        for x, g, r in zip(
+            (a, v, c, d, o), (a1_ref, v1_ref, c1_ref, d1_ref, o1_ref), (a_ref, v_ref, c_ref, d_ref, o_ref)
+        )
+    )
+    e, ev = [None] + e + [e1_ref, e_ref], [None] + ev + [ev1_ref, ev_ref]
+    u = [None, u1_ref.at[0], u0_ref, u_ref.at[0], u_ref.at[1]]
+    load_full(side_ref, 0, a[3], v[3])
+    load_half(side_ref, PLANE, a[4], v[4])
 
     def emit(i, dot, bd, perm, back, m_ref):
-        xo = right * (2 * i - 1) + 2 - i
-        decode_finish(dot, xo, bd, perm, back, m_ref, out_ref, 2 * i)
-        copies.append(
-            pltpu.make_async_copy(out_ref.at[:, pl.ds(2 * i, 2)], out_hbm.at[:, pl.ds(2 * xo, 2)], sems.at[i])
-        )
+        xo = far_place(right, i)
+        at = pl.ds(2 * i - 2, 2)
+        decode_finish(dot, xo, bd, perm, back, m_ref, out_ref, 2 * i - 2)
+        copies.append(pltpu.make_async_copy(out_ref.at[:, at], out_hbm.at[:, pl.ds(2 * xo, 2)], sems.at[i - 1]))
         copies[-1].start()
 
-    side_kernel(
-        right, side_ref, refs[:8], refs[8:13], refs[13:21], scratch, (0, 1, 2), (e1_ref, ev1_ref, u1_ref), emit
-    )
+    w = Stages(right, weights, misc, (a, v, e, ev, c, d, o, u), k_ref, own[7], emit)
+    e1 = w.e_dot(1)
+    e2 = w.e_dot(2)
+    l1 = w.e_finish(1, e1)
+    w.s_finish(1, l1)
+    c1 = w.c_dot(1)
+    l2 = w.e_finish(2, e2)
+    w.s_finish(2, l2)
+    w.c_finish(1, c1)
+    c2 = w.c_dot(2)
+    d1 = w.d_dot(1)
+    w.c_finish(2, c2)
+    w.d_finish(1, d1)
+    w.d_finish(2, w.d_dot(2))
     for copy in copies:
         copy.wait()
 
@@ -569,21 +632,24 @@
 SCALAR = [pl.BlockSpec(memory_space=pltpu.SMEM)]
 
 
-def state(own, planes, more):
-    masks = (2, 2, 3, 64, LANES)
+def state(own, planes, encoded):
     return [
-        ((own, 2, 320, LANES), BF16),
-        ((own, 2, 320, LANES), BF16),
-        ((planes + more, 2, 320, LANES), BF16),
-        ((planes + more, 2, 192, LANES), BF16),
-        ((planes, 320, LANES), BF16),
-        ((planes, 256, LANES), BF16),
-        ((planes, 256, LANES), F32),
-        (masks, F32),
+        (own + (2, 320, LANES), BF16),
+        (own + (2, 320, LANES), BF16),
+        (encoded + (2, 320, LANES), BF16),
+        (encoded + (2, 192, LANES), BF16),
+        (planes + (320, LANES), BF16),
+        (planes + (256, LANES), BF16),
+        (planes + (256, LANES), F32),
+        ((2, 3, 64, LANES), F32),
     ]
 
 
-LIFTED = (5, 2, 192, LANES)
+LIFTED = (2, 192, LANES)
+
+
+def arrays(shapes):
+    return [array(*shape, kind=kind) for shape, kind in shapes]
 
 
 def on_device(
@@ -620,44 +686,53 @@
 
     odd = lax.axis_index("narrow").astype(jnp.int32)[None] & 1
     near_right = 1 - odd
-    far, near = call(
+    far_a, far_b, near = call(
         mid_kernel,
-        [array(EDGE_ROWS, LANES), array(EDGE_ROWS, LANES)],
+        [array(PLANE + MASKS, LANES), array(PLANE + HALF, LANES), array(2 * PLANE + HALF + MASKS, LANES)],
         SCALAR + vmem(5),
-        vmem(2),
+        vmem(3),
         buffers([((2, 4 * ZC, LANES), F32)]),
         8,
         10**8,
     )(odd, own, low, high, down_w, gains)
-    far_side = swapped(far, "narrow", 1)
-    near_side = swapped(near, "narrow", 0)
+    far_a = swapped(far_a, "narrow", 1)
+    far_b = swapped(far_b, "narrow", 1)
+    near = swapped(near, "narrow", 0)
 
     encoder = (enc_w, b_enc[None], down_w, gains, shifts)
-    mine = call(
-        own_kernel, [array(*d, kind=k) for d, k in state(4, 2, 0)], vmem(8), vmem(8), [], 12, 2 * 10**9
-    )(own, low, high, *encoder)
+    mine = call(own_kernel, arrays(state((4,), (2,), (2,))), vmem(8), vmem(8), [], 12, 2 * 10**9)(
+        own, low, high, *encoder
+    )
     some = encoder + (coarse_w, b_coarse[None], w_up, voxel_mask, dec_w, b_dec[None], perm, back) + tuple(mine)
-    scratch = buffers(state(5, 5, 1) + [(LIFTED, BF16)])
-    pair = (fine_in.shape[0], 2) + fine_in.shape[2:]
-    done = call(
+    pair = array(fine_in.shape[0], 2, *fine_in.shape[2:])
+    near_done, e1, ev1, u1 = call(
         near_kernel,
-        [array(*pair), array(2, 320, LANES), array(2, 192, LANES), array(2, 2, 192, LANES)],
+        [pair] + arrays(state((), (), ())[2:4] + [((2,) + LIFTED, BF16)]),
         SCALAR + vmem(22),
         vmem(4),
-        scratch,
+        buffers(state((3,), (3,), (1,)) + [((1,) + LIFTED, BF16)]),
         24,
         4 * 10**9,
-    )(near_right, near_side, *some)
-    rest = (fine_in.shape[0], 6) + fine_in.shape[2:]
+    )(near_right, near, *some)
+    first = call(
+        first_kernel,
+        [pair] + arrays(state((), (), ()) + [(LIFTED, BF16)]),
+        SCALAR + vmem(25),
+        vmem(10),
+        [],
+        24,
+        2 * 10**9,
+    )(near_right, far_a, *some, e1, ev1, u1)
+    rest = pltpu.VMEM((fine_in.shape[0], 4) + fine_in.shape[2:], BF16)
     return call(
-        far_kernel,
+        last_kernel,
         [array(*fine_in.shape)],
-        SCALAR + vmem(26),
+        SCALAR + vmem(34),
         hbm(1),
-        scratch + [pltpu.VMEM(rest, BF16), pltpu.SemaphoreType.DMA((4,))],
+        buffers(state((2,), (2,), ())[:7] + [((2,) + LIFTED, BF16)]) + [rest, pltpu.SemaphoreType.DMA((4,))],
         24,
-        5 * 10**9,
-    )(near_right, far_side, *some, *done)[0]
+        4 * 10**9,
+    )(near_right, far_b, *some, near_done, u1, *first)[0]
 
 
 def solution(mesh):

time: 32.3 us -> 33.6 us (1.040)
  starting transfers between devices: 10.4 us -> 12.9 us
  waiting for transfers between devices: 6.2 us -> 4.4 us
  Pallas kernels: 14.3 us -> 14.9 us
    ppermute x2 -> x3, starting transfers between devices: 4.75 us -> 7.27 us  [swapped(): return lax.ppermute(value, axis, pairs)]
    ppermute x2 -> x3, waiting for transfers between devices: 1.81 us -> 0.01 us  [swapped(): return lax.ppermute(value, axis, pairs)]
    pallas_call x4 -> x5, Pallas kernels: 10.5 us -> 11.1 us  [the longest x1 3.94 us: on_device(): call(last_kernel, [array(*fine_in.shape)], SCALAR + vmem(34), hbm(1), buf...]
  transfers between devices with their start and end apart: 4 -> 5, of which waited for: 3 -> 2; matrix products, arithmetic and copies ran while one was open for 1% -> 1% of each run, Pallas kernels for 21% -> 25%
where the time goes in v6:
time: 33.6 us; the launch traced here: 33.4 us
  Pallas kernels  14.9 us (44%)
  starting transfers between devices  12.9 us (38%)
  waiting for transfers between devices  4.4 us (13%)
  between operations  0.88 us (3%)
    ppermute x3, starting transfers between devices, swapped(): return lax.ppermute(value, axis, pairs)  7.27 us
    ppermute x2, starting transfers between devices, shifted(): lax.ppermute(value, axis, [(i, i + step) for i in range(peers) if 0 <= i...  5.67 us
    ppermute x2, waiting for transfers between devices, shifted(): lax.ppermute(value, axis, [(i, i + step) for i in range(peers) if 0 <= i...  4.39 us
    pallas_call x1, Pallas kernels, on_device(): call(last_kernel, [array(*fine_in.shape)], SCALAR + vmem(34), hbm(1), buf...  3.94 us
    pallas_call x1, Pallas kernels, on_device(): call(near_kernel, [pair] + arrays(state((), (), ())[2:4] + [((2,) + LIFTE...  3.67 us
    pallas_call x1, Pallas kernels, on_device(): call(pack_kernel, [array(OWN + ZC, LANES), array(SIDE_ROWS, LANES), array...  2.31 us
    pallas_call x1, Pallas kernels, on_device(): call(first_kernel, [pair] + arrays(state((), (), ()) + [(LIFTED, BF16)]),...  1.94 us
    pallas_call x1, Pallas kernels, on_device(): call(weights_kernel, [array(1024, 512), array(1536, 512), array(128, 256)...  1.49 us
  transfers between devices with their start and end apart: 5, of which 2 were waited for; matrix products, arithmetic and copies ran while one was open for 1% of the time, Pallas kernels for 25%

profile of v6, /device:TPU:1, one launch (start us, length us, event | category | flops | bytes accessed | tf_op | source)
XLA Modules:
  0.0 33.4 jit_solution(7024268262822157524)
XLA Ops:
  0.0 2.3 %shard_map.118 = (bf16[1320,128]{1,0:T(8,128)(2,1)S(1)}, bf16[840,128]{1,0:T(8,128)(2,1)S(1)}, bf16[840,128]{1,0:T(8,128)(2,1)S(1)}) custom-call(bf16[32,8,8,80]{3,2,1,0:T(8,128)(2,1)} %x_hbm.1, s32[8,8,80]{2,1,0:T(8,128)} %refs_8_.5), custom_call_target="tpu_custom_call" | custom-call | flops 1000000000 | bytes 1000000 | tf_op jit(solution)/shard_map/pallas_call | solution.py:658
  2.4 4.4 %collective-permute-start = (bf16[840,128]{1,0:T(8,128)(2,1)S(1)}, bf16[840,128]{1,0:T(8,128)(2,1)S(1)}, u32[]{:S(2)}, u32[]{:S(2)}) collective-permute-start(bf16[840,128]{1,0:T(8,128)(2,1)S(1)} %get-tuple-element.40), channel_id=1, source_target_pairs={{0,8},{8,16},{16,24},{24,32},{32,40},{40,48},{48,56},{56,64},{64,7... | collective-permute-start | bytes 645128 | tf_op jit(solution)/shard_map/ppermute | solution.py:614
  6.7 1.3 %collective-permute-start.1 = (bf16[840,128]{1,0:T(8,128)(2,1)S(1)}, bf16[840,128]{1,0:T(8,128)(2,1)S(1)}, u32[]{:S(2)}, u32[]{:S(2)}) collective-permute-start(bf16[840,128]{1,0:T(8,128)(2,1)S(1)} %get-tuple-element.41), channel_id=1, source_target_pairs={{8,0},{16,8},{24,16},{32,24},{40,32},{48,40},{56,48},{64,56},{72,6... | collective-permute-start | bytes 645128 | tf_op jit(solution)/shard_map/ppermute | solution.py:614
  8.7 0.1 cosine_convert_fusion
  8.8 0.2 fusion
  8.9 0.0 copy-done.7
  9.0 0.0 copy-start.3
  9.0 1.5 %shard_map.119 = (bf16[1024,512]{1,0:T(8,128)(2,1)S(1)}, bf16[1536,512]{1,0:T(8,128)(2,1)S(1)}, bf16[128,256]{1,0:T(8,128)(2,1)S(1)}, bf16[512,512]{1,0:T(8,128)...) custom-call(bf16[27,32,32]{2,1,0:T(8,128)(2,1)S(1)} %copy-done.7, ...), custom_call_target="tpu_custom_call" | custom-call | flops 4000000000 | bytes 1000000 | tf_op jit(solution)/shard_map/pallas_call | solution.py:676
  10.5 0.2 collective-permute-done.low_ref
  10.7 4.2 %collective-permute-done.1.high_ref = bf16[840,128]{1,0:T(8,128)(2,1)S(1)} collective-permute-done((bf16[840,128]{1,0:T(8,128)(2,1)S(1)}, bf16[840,128]{1,0:T(8,128)(2,1)S(1)}, u32[]{:S(2)}, u32[]{:S(2)}) %collective-permute-start.1) | collective-permute-done | bytes 215072 | tf_op jit(solution)/shard_map/ppermute | solution.py:614
  14.9 0.2 shard_map.120
  15.0 1.7 %collective-permute-start.3 = (bf16[1960,128]{1,0:T(8,128)(2,1)S(1)}, bf16[1960,128]{1,0:T(8,128)(2,1)S(1)}, u32[]{:S(2)}, u32[]{:S(2)}) collective-permute-start(bf16[1960,128]{1,0:T(8,128)(2,1)S(1)} %get-tuple-element.57), channel_id=1, source_target_pairs={{0,1},{1,0},{2,3},{3,2},{4,5},{5,4},{6,7},{7,6},{8,9},{9,8},{10,11... | collective-permute-start | bytes 1505288 | tf_op jit(solution)/shard_map/ppermute | solution.py:622
  16.8 3.0 %collective-permute-start.4 = (bf16[840,128]{1,0:T(8,128)(2,1)S(1)}, bf16[840,128]{1,0:T(8,128)(2,1)S(1)}, u32[]{:S(2)}, u32[]{:S(2)}) collective-permute-start(bf16[840,128]{1,0:T(8,128)(2,1)S(1)} %get-tuple-element.60), channel_id=1, source_target_pairs={{1,2},{2,1},{3,4},{4,3},{5,6},{6,5},{9,10},{10,9},{11,12},{12,11},... | collective-permute-start | bytes 645128 | tf_op jit(solution)/shard_map/ppermute | solution.py:622
  19.8 2.5 %collective-permute-start.2 = (bf16[1120,128]{1,0:T(8,128)(2,1)S(1)}, bf16[1120,128]{1,0:T(8,128)(2,1)S(1)}, u32[]{:S(2)}, u32[]{:S(2)}) collective-permute-start(bf16[1120,128]{1,0:T(8,128)(2,1)S(1)} %get-tuple-element.43), channel_id=1, source_target_pairs={{1,2},{2,1},{3,4},{4,3},{5,6},{6,5},{9,10},{10,9},{11,12},{12,11},... | collective-permute-start | bytes 860168 | tf_op jit(solution)/shard_map/ppermute | solution.py:622
  22.3 0.0 copy-start.1
  22.4 0.0 copy-start.2
  22.4 0.0 copy-start.4
  22.4 0.0 copy-start.5
  22.4 1.4 %shard_map.121 = (bf16[4,2,320,128]{3,2,1,0:T(8,128)(2,1)S(1)}, bf16[4,2,320,128]{3,2,1,0:T(8,128)(2,1)S(1)}, bf16[2,2,320,128]{3,2,1,0:T(8,128)(2,1)S(1)}, bf16...) custom-call(bf16[1320,128]{1,0:T(8,128)(2,1)S(1)} %get-tuple-element, ...), custom_call_target="tpu_custom_call" | custom-call | flops 2000000000 | bytes 1000000 | tf_op jit(solution)/shard_map/pallas_call | solution.py:703
  23.8 0.0 collective-permute-done.3.side_ref
  23.9 3.7 %shard_map.122 = (bf16[32,2,8,80]{3,2,1,0:T(8,128)(2,1)S(1)}, bf16[2,320,128]{2,1,0:T(8,128)(2,1)S(1)}, bf16[2,192,128]{2,1,0:T(8,128)(2,1)S(1)}, bf16[2,2,192,128]{3,2,1,0:T(8,128)(2,1)S(1)}) custom-call(s32[1]{0:T(128)S(6)} %sub.3.right_ref, bf16[1960,128]{1,0:T(8,128)(2,1)S(1)} %collective-permute-done.3.side_ref, ...), custom_call_target="tpu_custom_call" | custom-call | flops 4000000000 | bytes 1000000 | tf_op jit(solution)/shard_map/pallas_call | solution.py:708
  27.5 1.9 %shard_map.123 = (bf16[32,2,8,80]{3,2,1,0:T(8,128)(2,1)S(1)}, bf16[2,320,128]{2,1,0:T(8,128)(2,1)S(1)}, bf16[2,320,128]{2,1,0:T(8,128)(2,1)S(1)}, bf16[2,320,128...) custom-call(s32[1]{0:T(128)S(6)} %sub.3.right_ref, ...), custom_call_target="tpu_custom_call" | custom-call | flops 2000000000 | bytes 1000000 | tf_op jit(solution)/shard_map/pallas_call | solution.py:717
  29.5 0.0 collective-permute-done.2.side_ref
  29.5 3.9 %shard_map.124 = bf16[32,8,8,80]{3,2,1,0:T(8,128)(2,1)} custom-call(s32[1]{0:T(128)S(6)} %sub.3.right_ref, bf16[1120,128]{1,0:T(8,128)(2,1)S(1)} %collective-permute-done.2.side_ref, bf16[1024,512]{1,0:T(8,128)(2,1)S(1)} %get-tuple-element.44.we_ref.refs_0_, f32[1,32]{1,0:T(1,128)S(1)} %bitcast.13, ...), custom_call_target="tpu_custom_call" | custom-call | flops 4000000000 | bytes 1000000 | tf_op jit(solution)/shard_map/pallas_call | solution.py:727
  (16 shorter events, 0.0 us)
Async XLA Ops:
  0.0 8.7 %copy-start = (bf16[128,256]{1,0:T(8,128)(2,1)S(1)}, bf16[128,256]{1,0:T(8,128)(2,1)}, u32[]{:S(2)}) copy-start(bf16[128,256]{1,0:T(8,128)(2,1)} %param.18) | copy-start | bytes 196612
  0.0 8.9 %copy-start.8 = (bf16[27,32,64]{2,1,0:T(8,128)(2,1)S(1)}, bf16[27,32,64]{2,1,0:T(8,128)(2,1)}, u32[]{:S(2)}) copy-start(bf16[27,32,64]{2,1,0:T(8,128)(2,1)} %wd_ref.1) | copy-start | bytes 331780
  0.0 8.9 %copy-start.6 = (bf16[27,128,128]{2,1,0:T(8,128)(2,1)S(1)}, bf16[27,128,128]{2,1,0:T(8,128)(2,1)}, u32[]{:S(2)}) copy-start(bf16[27,128,128]{2,1,0:T(8,128)(2,1)} %wc_ref.1) | copy-start | bytes 2654212
  0.0 8.9 %copy-start.9 = (bf16[128,256]{1,0:T(8,128)(2,1)S(1)}, bf16[128,256]{1,0:T(8,128)(2,1)}, u32[]{:S(2)}) copy-start(bf16[128,256]{1,0:T(8,128)(2,1)} %wn_ref.1) | copy-start | bytes 196612
  0.0 8.9 %copy-start.7 = (bf16[27,32,32]{2,1,0:T(8,128)(2,1)S(1)}, bf16[27,32,32]{2,1,0:T(8,128)(2,1)}, u32[]{:S(2)}) copy-start(bf16[27,32,32]{2,1,0:T(8,128)(2,1)} %we_ref.1) | copy-start | bytes 165892
  2.4 8.3 %collective-permute-start = (bf16[840,128]{1,0:T(8,128)(2,1)S(1)}, bf16[840,128]{1,0:T(8,128)(2,1)S(1)}, u32[]{:S(2)}, u32[]{:S(2)}) collective-permute-start(bf16[840,128]{1,0:T(8,128)(2,1)S(1)} %get-tuple-element.40), channel_id=1, source_target_pairs={{0,8},{8,16},{16,24},{24,32},{32,40},{40,48},{48,56},{56,64},{64,7... | collective-permute-start | bytes 645128 | tf_op jit(solution)/shard_map/ppermute | solution.py:614
  6.7 8.1 %collective-permute-start.1 = (bf16[840,128]{1,0:T(8,128)(2,1)S(1)}, bf16[840,128]{1,0:T(8,128)(2,1)S(1)}, u32[]{:S(2)}, u32[]{:S(2)}) collective-permute-start(bf16[840,128]{1,0:T(8,128)(2,1)S(1)} %get-tuple-element.41), channel_id=1, source_target_pairs={{8,0},{16,8},{24,16},{32,24},{40,32},{48,40},{56,48},{64,56},{72,6... | collective-permute-start | bytes 645128 | tf_op jit(solution)/shard_map/ppermute | solution.py:614
  9.0 13.4 %copy-start.3 = (f32[32]{0:T(128)S(1)}, f32[32]{0:T(128)}, u32[]{:S(2)}) copy-start(f32[32]{0:T(128)} %param.16) | copy-start | bytes 388
  15.0 8.8 %collective-permute-start.3 = (bf16[1960,128]{1,0:T(8,128)(2,1)S(1)}, bf16[1960,128]{1,0:T(8,128)(2,1)S(1)}, u32[]{:S(2)}, u32[]{:S(2)}) collective-permute-start(bf16[1960,128]{1,0:T(8,128)(2,1)S(1)} %get-tuple-element.57), channel_id=1, source_target_pairs={{0,1},{1,0},{2,3},{3,2},{4,5},{5,4},{6,7},{7,6},{8,9},{9,8},{10,11... | collective-permute-start | bytes 1505288 | tf_op jit(solution)/shard_map/ppermute | solution.py:622
  16.8 10.8 %collective-permute-start.4 = (bf16[840,128]{1,0:T(8,128)(2,1)S(1)}, bf16[840,128]{1,0:T(8,128)(2,1)S(1)}, u32[]{:S(2)}, u32[]{:S(2)}) collective-permute-start(bf16[840,128]{1,0:T(8,128)(2,1)S(1)} %get-tuple-element.60), channel_id=1, source_target_pairs={{1,2},{2,1},{3,4},{4,3},{5,6},{6,5},{9,10},{10,9},{11,12},{12,11},... | collective-permute-start | bytes 645128 | tf_op jit(solution)/shard_map/ppermute | solution.py:622
  19.8 9.7 %collective-permute-start.2 = (bf16[1120,128]{1,0:T(8,128)(2,1)S(1)}, bf16[1120,128]{1,0:T(8,128)(2,1)S(1)}, u32[]{:S(2)}, u32[]{:S(2)}) collective-permute-start(bf16[1120,128]{1,0:T(8,128)(2,1)S(1)} %get-tuple-element.43), channel_id=1, source_target_pairs={{1,2},{2,1},{3,4},{4,3},{5,6},{6,5},{9,10},{10,9},{11,12},{12,11},... | collective-permute-start | bytes 860168 | tf_op jit(solution)/shard_map/ppermute | solution.py:622
  22.3 1.5 %copy-start.1 = (s32[8,8,80]{2,1,0:T(8,128)S(1)}, s32[8,8,80]{2,1,0:T(8,128)}, u32[]{:S(2)}) copy-start(s32[8,8,80]{2,1,0:T(8,128)} %refs_8_.5) | copy-start | bytes 61444
  22.4 1.5 %copy-start.2 = (bf16[32,128]{1,0:T(8,128)(2,1)S(1)}, bf16[32,128]{1,0:T(8,128)(2,1)}, u32[]{:S(2)}) copy-start(bf16[32,128]{1,0:T(8,128)(2,1)} %refs_7_.5) | copy-start | bytes 24580
  22.4 1.5 %copy-start.4 = (f32[128]{0:T(128)S(1)}, f32[128]{0:T(128)}, u32[]{:S(2)}) copy-start(f32[128]{0:T(128)} %param.20) | copy-start | bytes 1540
  22.4 1.5 %copy-start.5 = (f32[32]{0:T(128)S(1)}, f32[32]{0:T(128)}, u32[]{:S(2)}) copy-start(f32[32]{0:T(128)} %param.23) | copy-start | bytes 388

commit v7 on v6

--- a/solution.py
+++ b/solution.py
@@ -37,6 +37,8 @@
 PLANE = 9 * PAIR
 HALF = 5 * PAIR
 MASKS = 3 * ZC
+MIDDLE = 10 * PAIR
+FLANKS = 13 * PAIR
 
 
 def one_where(truth):
@@ -111,7 +113,23 @@
     return pl.ds(pl.multiple_of(x * size, size), size)
 
 
-def mid_kernel(odd_ref, own_ref, low_ref, high_ref, tie_ref, tie2_ref, far_a_ref, far_b_ref, near_ref, ends_ref):
+def folded(pieces, right):
+    lane_a = iota(pieces[0].shape, 1) >> 6
+    even, odd = (v.astype(F32) for v in pieces)
+    return jnp.where(lane_a == right, even, pltpu.roll(odd, 64, 1)).astype(BF16)
+
+
+def edge_kernel(odd_ref, own_ref, out_ref):
+    right = odd_ref[0]
+    for i, x in enumerate((3 * right, 1 + right)):
+        out_ref[4 * PAIR * i : 4 * PAIR * (i + 1)] = own_ref[part(x, 4 * PAIR)]
+    x = 2 - right
+    pieces = [own_ref[pl.ds(pl.multiple_of((4 * x + 2 * cz) * PAIR, PAIR), 2 * PAIR)] for cz in BITS]
+    out_ref[8 * PAIR : 10 * PAIR] = folded(pieces, right)
+    out_ref[MIDDLE : MIDDLE + ZC] = own_ref[OWN : OWN + ZC]
+
+
+def mid_kernel(odd_ref, own_ref, low_ref, high_ref, tie_ref, tie2_ref, far_ref, near_ref, ends_ref):
     ends_ref[0] = low_ref[SIDE:SIDE_MASK].astype(F32)
     ends_ref[1] = high_ref[SIDE:SIDE_MASK].astype(F32)
 
@@ -126,39 +144,37 @@
         at = part(x, ZC)
         return stacked(ends_ref[0, at], ends_ref[1, at]).astype(BF16)
 
-    lane_a = iota((PAIR, LANES), 1) >> 6
-
-    def full(ref, at, x):
+    right = 1 - odd_ref[0]
+    for i, x in enumerate((3 * right, 1 + right)):
+        at = i * PLANE
         for cz in BITS:
             low, own, high = layer(x, cz)
-            ref[at : at + PAIR] = low
-            ref[at + PAIR : at + 3 * PAIR] = own
-            ref[at + 3 * PAIR : at + 4 * PAIR] = high
+            near_ref[at : at + PAIR] = low
+            near_ref[at + PAIR : at + 3 * PAIR] = own
+            near_ref[at + 3 * PAIR : at + 4 * PAIR] = high
             at = at + 4 * PAIR
-        ref[at : at + PAIR] = ends(x)
-
-    def half(ref, at, x, right):
-        pieces = []
-        for cz in BITS:
-            low, own, high = layer(x, cz)
-            pieces.append([v.astype(F32) for v in (low, own[:PAIR], own[PAIR:], high)])
-        for i in range(4):
-            v = jnp.where(lane_a == right, pieces[0][i], pltpu.roll(pieces[1][i], 64, 1))
-            ref[at + i * PAIR : at + (i + 1) * PAIR] = v.astype(BF16)
-        ref[at + 4 * PAIR : at + HALF] = ends(x)
-
-    def masks(ref, at):
-        parts = [low_ref[SIDE_MASK:SIDE_ROWS], own_ref[OWN : OWN + ZC], high_ref[SIDE_MASK:SIDE_ROWS]]
-        ref[at : at + MASKS] = stacked(*[m.astype(F32) for m in parts]).astype(BF16)
-
-    for (a_ref, a_at), (b_ref, b_at), (m_ref, m_at), right in (
-        ((far_a_ref, 0), (far_b_ref, 0), (far_a_ref, PLANE), odd_ref[0]),
-        ((near_ref, 0), (near_ref, PLANE), (near_ref, 2 * PLANE + HALF), 1 - odd_ref[0]),
-    ):
-        full(a_ref, a_at, 3 * right)
-        full(b_ref, b_at, 1 + right)
-        half(b_ref, b_at + PLANE, 2 - right, right)
-        masks(m_ref, m_at)
+        near_ref[at : at + PAIR] = ends(x)
+    x, at = 2 - right, 2 * PLANE
+    low, own, high = zip(*[layer(x, cz) for cz in BITS])
+    near_ref[at : at + PAIR] = folded(low, right)
+    near_ref[at + PAIR : at + 3 * PAIR] = folded(own, right)
+    near_ref[at + 3 * PAIR : at + 4 * PAIR] = folded(high, right)
+    near_ref[at + 4 * PAIR : at + HALF] = ends(x)
+    masks = [low_ref[SIDE_MASK:SIDE_ROWS], own_ref[OWN : OWN + ZC], high_ref[SIDE_MASK:SIDE_ROWS]]
+    near_ref[at + HALF : at + HALF + MASKS] = stacked(*[m.astype(F32) for m in masks]).astype(BF16)
+    right = odd_ref[0]
+    for i, x in enumerate((3 * right, 1 + right)):
+        at = 5 * PAIR * i
+        far_ref[at : at + 2 * PAIR] = low_ref[part(x, 2 * PAIR)]
+        far_ref[at + 2 * PAIR : at + 4 * PAIR] = high_ref[part(x, 2 * PAIR)]
+        far_ref[at + 4 * PAIR : at + 5 * PAIR] = ends(x)
+    x, at = 2 - right, 10 * PAIR
+    low, own, high = zip(*[layer(x, cz) for cz in BITS])
+    far_ref[at : at + PAIR] = folded(low, right)
+    far_ref[at + PAIR : at + 2 * PAIR] = folded(high, right)
+    far_ref[at + 2 * PAIR : at + 3 * PAIR] = ends(x)
+    masks = [low_ref[SIDE_MASK:SIDE_ROWS], high_ref[SIDE_MASK:SIDE_ROWS]]
+    far_ref[FLANKS : FLANKS + PAIR] = stacked(*[m.astype(F32) for m in masks]).astype(BF16)
 
 
 def tap_of(out_bit, in_bit, far):
@@ -292,6 +308,26 @@
     put_plane(a_ref, v_ref, [both, pltpu.roll(both, 64, 1)], ref[at + 320 : at + HALF].astype(F32))
 
 
+def load_far(mid_ref, flank_ref, a, v, k_ref):
+    for i in range(2):
+        mine, at = 4 * PAIR * i, 5 * PAIR * i
+        layers = []
+        for cz in BITS:
+            low, high = at + PAIR * cz, at + PAIR * (2 + cz)
+            own = mine + 2 * PAIR * cz
+            layers.append(
+                stacked(flank_ref[low : low + PAIR], mid_ref[own : own + 2 * PAIR], flank_ref[high : high + PAIR])
+            )
+        put_plane(a[i], v[i], layers, flank_ref[at + 4 * PAIR : at + 5 * PAIR].astype(F32))
+    at = 10 * PAIR
+    both = stacked(
+        flank_ref[at : at + PAIR], mid_ref[8 * PAIR : 10 * PAIR], flank_ref[at + PAIR : at + 2 * PAIR]
+    ).astype(F32)
+    put_plane(a[2], v[2], [both, pltpu.roll(both, 64, 1)], flank_ref[at + 2 * PAIR : at + 3 * PAIR].astype(F32))
+    masks = flank_ref[FLANKS : FLANKS + PAIR].astype(F32)
+    load_masks([masks[:ZC], mid_ref[MIDDLE : MIDDLE + ZC], masks[ZC:]], k_ref)
+
+
 def load_masks(parts, k_ref):
     for by, k in enumerate(parts):
         k = k.astype(F32)
@@ -509,74 +545,50 @@
     return right * (2 * i - 1) + 2 - i
 
 
-def first_kernel(right_ref, side_ref, *refs):
+def far_kernel(right_ref, middle_ref, flanks_ref, *refs):
     weights, misc, own = refs[:8], refs[8:13], refs[13:21]
-    e1_ref, ev1_ref, u1_ref = refs[21:24]
-    done_ref, a_ref, v_ref, e_ref, ev_ref, c_ref, d_ref, o_ref, k_ref, u_ref = refs[24:]
-    right = 1 - right_ref[0]
-    a, v, e, ev, c, d, o = own_planes(right, own)
-    a, v, c, d, o = (x + [r] for x, r in zip((a, v, c, d, o), (a_ref, v_ref, c_ref, d_ref, o_ref)))
-    e, ev = [e1_ref] + e + [e_ref], [ev1_ref] + ev + [ev_ref]
-    u = [u1_ref.at[1], u1_ref.at[0], u_ref]
-    load_full(side_ref, 0, a[2], v[2])
-    load_side_masks(side_ref, PLANE, k_ref)
-
-    def emit(i, dot, bd, perm, back, m_ref):
-        decode_finish(dot, far_place(right, i), bd, perm, back, m_ref, done_ref, 0)
-
-    w = Stages(right, weights, misc, (a, v, e, ev, c, d, o, u), k_ref, own[7], emit)
-    w.s_finish(0, w.e_finish(0, w.e_dot(0)))
-    w.c_finish(0, w.c_dot(0))
-    w.d_finish(0, w.d_dot(0))
-
-
-def last_kernel(right_ref, side_ref, *refs):
-    weights, misc, own = refs[:8], refs[8:13], refs[13:21]
-    near_done_ref, u1_ref = refs[21:23]
-    done_ref, a1_ref, v1_ref, e1_ref, ev1_ref, c1_ref, d1_ref, o1_ref, k_ref, u0_ref = refs[23:33]
-    out_hbm = refs[33]
-    a_ref, v_ref, e_ref, ev_ref, c_ref, d_ref, o_ref, u_ref, out_ref, sems = refs[34:]
+    near_done_ref, e1_ref, ev1_ref, u1_ref, out_hbm = refs[21:26]
+    a_ref, v_ref, e_ref, ev_ref, c_ref, d_ref, o_ref, k_ref, u_ref, out_ref, sems = refs[26:]
     left = right_ref[0]
     right = 1 - left
-    copies = [
-        pltpu.make_async_copy(near_done_ref, out_hbm.at[:, pl.ds(6 * left, 2)], sems.at[2]),
-        pltpu.make_async_copy(done_ref, out_hbm.at[:, pl.ds(2 * far_place(right, 0), 2)], sems.at[3]),
-    ]
-    for copy in copies:
-        copy.start()
+    copies = [pltpu.make_async_copy(near_done_ref, out_hbm.at[:, pl.ds(6 * left, 2)], sems.at[3])]
+    copies[0].start()
     a, v, e, ev, c, d, o = own_planes(right, own)
-    a, v, c, d, o = (
-        x + [g] + [r.at[i] for i in range(2)]
-        for x, g, r in zip(
-            (a, v, c, d, o), (a1_ref, v1_ref, c1_ref, d1_ref, o1_ref), (a_ref, v_ref, c_ref, d_ref, o_ref)
-        )
-    )
-    e, ev = [None] + e + [e1_ref, e_ref], [None] + ev + [ev1_ref, ev_ref]
-    u = [None, u1_ref.at[0], u0_ref, u_ref.at[0], u_ref.at[1]]
-    load_full(side_ref, 0, a[3], v[3])
-    load_half(side_ref, PLANE, a[4], v[4])
+    a, v, c, d, o = (x + [r.at[i] for i in range(3)] for x, r in zip((a, v, c, d, o), (a_ref, v_ref, c_ref, d_ref, o_ref)))
+    e = [e1_ref] + e + [e_ref.at[0], e_ref.at[1]]
+    ev = [ev1_ref] + ev + [ev_ref.at[0], ev_ref.at[1]]
+    u = [u1_ref.at[1], u1_ref.at[0]] + [u_ref.at[i] for i in range(3)]
+    load_far(middle_ref, flanks_ref, a[2:], v[2:], k_ref)
 
     def emit(i, dot, bd, perm, back, m_ref):
         xo = far_place(right, i)
-        at = pl.ds(2 * i - 2, 2)
-        decode_finish(dot, xo, bd, perm, back, m_ref, out_ref, 2 * i - 2)
-        copies.append(pltpu.make_async_copy(out_ref.at[:, at], out_hbm.at[:, pl.ds(2 * xo, 2)], sems.at[i - 1]))
+        at = pl.ds(2 * i, 2)
+        decode_finish(dot, xo, bd, perm, back, m_ref, out_ref, 2 * i)
+        copies.append(pltpu.make_async_copy(out_ref.at[:, at], out_hbm.at[:, pl.ds(2 * xo, 2)], sems.at[i]))
         copies[-1].start()
 
     w = Stages(right, weights, misc, (a, v, e, ev, c, d, o, u), k_ref, own[7], emit)
+    e0 = w.e_dot(0)
     e1 = w.e_dot(1)
+    l0 = w.e_finish(0, e0)
     e2 = w.e_dot(2)
+    w.s_finish(0, l0)
     l1 = w.e_finish(1, e1)
+    c0 = w.c_dot(0)
     w.s_finish(1, l1)
+    l2 = w.e_finish(2, e2)
+    w.c_finish(0, c0)
     c1 = w.c_dot(1)
-    l2 = w.e_finish(2, e2)
     w.s_finish(2, l2)
+    d0 = w.d_dot(0)
     w.c_finish(1, c1)
     c2 = w.c_dot(2)
+    w.d_finish(0, d0)
     d1 = w.d_dot(1)
     w.c_finish(2, c2)
+    d2 = w.d_dot(2)
     w.d_finish(1, d1)
-    w.d_finish(2, w.d_dot(2))
+    w.d_finish(2, d2)
     for copy in copies:
         copy.wait()
 
@@ -666,6 +678,11 @@
     )(pltpu.with_memory_space_constraint(fine_in, pltpu.HBM), pltpu.with_memory_space_constraint(voxel_mask, pltpu.HBM))
     low = shifted(up, "wide", 1)
     high = shifted(down, "wide", -1)
+
+    odd = lax.axis_index("narrow").astype(jnp.int32)[None] & 1
+    near_right = 1 - odd
+    middle = call(edge_kernel, [array(MIDDLE + ZC, LANES)], SCALAR + vmem(1), vmem(1), [], 8, 10**8)(odd, own)[0]
+    middle = swapped(middle, "narrow", 1)
 
     embedded = time_features(timestep, w_time.shape[0])
     film = jnp.dot(embedded[None], w_time, preferred_element_type=F32)
@@ -684,19 +701,16 @@
         4 * 10**9,
     )(w_enc, w_dec, w_down, w_coarse)
 
-    odd = lax.axis_index("narrow").astype(jnp.int32)[None] & 1
-    near_right = 1 - odd
-    far_a, far_b, near = call(
+    flanks, near = call(
         mid_kernel,
-        [array(PLANE + MASKS, LANES), array(PLANE + HALF, LANES), array(2 * PLANE + HALF + MASKS, LANES)],
+        [array(FLANKS + PAIR, LANES), array(2 * PLANE + HALF + MASKS, LANES)],
         SCALAR + vmem(5),
-        vmem(3),
+        vmem(2),
         buffers([((2, 4 * ZC, LANES), F32)]),
         8,
         10**8,
     )(odd, own, low, high, down_w, gains)
-    far_a = swapped(far_a, "narrow", 1)
-    far_b = swapped(far_b, "narrow", 1)
+    flanks = swapped(flanks, "narrow", 1)
     near = swapped(near, "narrow", 0)
 
     encoder = (enc_w, b_enc[None], down_w, gains, shifts)
@@ -714,25 +728,16 @@
         24,
         4 * 10**9,
     )(near_right, near, *some)
-    first = call(
-        first_kernel,
-        [pair] + arrays(state((), (), ()) + [(LIFTED, BF16)]),
-        SCALAR + vmem(25),
-        vmem(10),
-        [],
+    rest = pltpu.VMEM((fine_in.shape[0], 6) + fine_in.shape[2:], BF16)
+    return call(
+        far_kernel,
+        [array(*fine_in.shape)],
+        SCALAR + vmem(27),
+        hbm(1),
+        buffers(state((3,), (3,), (2,)) + [((3,) + LIFTED, BF16)]) + [rest, pltpu.SemaphoreType.DMA((4,))],
         24,
-        2 * 10**9,
-    )(near_right, far_a, *some, e1, ev1, u1)
-    rest = pltpu.VMEM((fine_in.shape[0], 4) + fine_in.shape[2:], BF16)
-    return call(
-        last_kernel,
-        [array(*fine_in.shape)],
-        SCALAR + vmem(34),
-        hbm(1),
-        buffers(state((2,), (2,), ())[:7] + [((2,) + LIFTED, BF16)]) + [rest, pltpu.SemaphoreType.DMA((4,))],
-        24,
-        4 * 10**9,
-    )(near_right, far_b, *some, near_done, u1, *first)[0]
+        5 * 10**9,
+    )(near_right, middle, flanks, *some, near_done, e1, ev1, u1)[0]
 
 
 def solution(mesh):

time: 33.6 us -> 33 us (0.982)
  Pallas kernels: 14.9 us -> 14.2 us
    pallas_call x3, Pallas kernels: 6.04 us -> 5.24 us  [the longest x1 4.99 us: on_device(): call(far_kernel, [array(*fine_in.shape)], SCALAR + vmem(27), hbm(1), buff...]
  transfers between devices with their start and end apart: 5 -> 5, of which waited for: 2 -> 3; matrix products, arithmetic and copies ran while one was open for 1% -> 1% of each run, Pallas kernels for 25% -> 21%
where the time goes in v7:
time: 33 us; the launch traced here: 32.8 us
  Pallas kernels  14.2 us (43%)
  starting transfers between devices  12.9 us (39%)
  waiting for transfers between devices  4.51 us (14%)
  between operations  0.88 us (3%)
    ppermute x3, starting transfers between devices, swapped(): return lax.ppermute(value, axis, pairs)  7.28 us
    ppermute x2, starting transfers between devices, shifted(): lax.ppermute(value, axis, [(i, i + step) for i in range(peers) if 0 <= i...  5.67 us
    pallas_call x1, Pallas kernels, on_device(): call(far_kernel, [array(*fine_in.shape)], SCALAR + vmem(27), hbm(1), buff...  4.99 us
    ppermute x2, waiting for transfers between devices, shifted(): lax.ppermute(value, axis, [(i, i + step) for i in range(peers) if 0 <= i...  4.39 us
    pallas_call x1, Pallas kernels, on_device(): call(near_kernel, [pair] + arrays(state((), (), ())[2:4] + [((2,) + LIFTE...  3.79 us
    pallas_call x1, Pallas kernels, on_device(): call(pack_kernel, [array(OWN + ZC, LANES), array(SIDE_ROWS, LANES), array...  2.31 us
    pallas_call x1, Pallas kernels, on_device(): call(weights_kernel, [array(1024, 512), array(1536, 512), array(128, 256)...  1.49 us
    pallas_call x1, Pallas kernels, on_device(): call(own_kernel, arrays(state((4,), (2,), (2,))), vmem(8), vmem(8), [], 1...  1.37 us
  transfers between devices with their start and end apart: 5, of which 3 were waited for; matrix products, arithmetic and copies ran while one was open for 1% of the time, Pallas kernels for 21%

profile of v7, /device:TPU:1, one launch (start us, length us, event | category | flops | bytes accessed | tf_op | source)
XLA Modules:
  0.0 32.8 jit_solution(4785076865891111232)
XLA Ops:
  0.0 2.3 %shard_map.118 = (bf16[1320,128]{1,0:T(8,128)(2,1)S(1)}, bf16[840,128]{1,0:T(8,128)(2,1)S(1)}, bf16[840,128]{1,0:T(8,128)(2,1)S(1)}) custom-call(bf16[32,8,8,80]{3,2,1,0:T(8,128)(2,1)} %x_hbm.1, s32[8,8,80]{2,1,0:T(8,128)} %refs_8_.3), custom_call_target="tpu_custom_call" | custom-call | flops 1000000000 | bytes 1000000 | tf_op jit(solution)/shard_map/pallas_call | solution.py:670
  2.4 4.4 %collective-permute-start.1 = (bf16[840,128]{1,0:T(8,128)(2,1)S(1)}, bf16[840,128]{1,0:T(8,128)(2,1)S(1)}, u32[]{:S(2)}, u32[]{:S(2)}) collective-permute-start(bf16[840,128]{1,0:T(8,128)(2,1)S(1)} %get-tuple-element.29), channel_id=1, source_target_pairs={{0,8},{8,16},{16,24},{24,32},{32,40},{40,48},{48,56},{56,64},{64,7... | collective-permute-start | bytes 645128 | tf_op jit(solution)/shard_map/ppermute | solution.py:626
  6.7 1.3 %collective-permute-start.2 = (bf16[840,128]{1,0:T(8,128)(2,1)S(1)}, bf16[840,128]{1,0:T(8,128)(2,1)S(1)}, u32[]{:S(2)}, u32[]{:S(2)}) collective-permute-start(bf16[840,128]{1,0:T(8,128)(2,1)S(1)} %get-tuple-element.30), channel_id=1, source_target_pairs={{8,0},{16,8},{24,16},{32,24},{40,32},{48,40},{56,48},{64,56},{72,6... | collective-permute-start | bytes 645128 | tf_op jit(solution)/shard_map/ppermute | solution.py:626
  8.7 0.1 cosine_convert_fusion
  8.8 0.2 fusion
  9.0 0.0 copy-start.7
  9.0 1.5 %shard_map.120 = (bf16[1024,512]{1,0:T(8,128)(2,1)S(1)}, bf16[1536,512]{1,0:T(8,128)(2,1)S(1)}, bf16[128,256]{1,0:T(8,128)(2,1)S(1)}, bf16[512,512]{1,0:T(8,128)...) custom-call(bf16[27,32,32]{2,1,0:T(8,128)(2,1)S(1)} %copy-done.2, ...), custom_call_target="tpu_custom_call" | custom-call | flops 4000000000 | bytes 1000000 | tf_op jit(solution)/shard_map/pallas_call | solution.py:693
  10.5 0.2 collective-permute-done.1.low_ref
  10.7 4.2 %collective-permute-done.2.high_ref = bf16[840,128]{1,0:T(8,128)(2,1)S(1)} collective-permute-done((bf16[840,128]{1,0:T(8,128)(2,1)S(1)}, bf16[840,128]{1,0:T(8,128)(2,1)S(1)}, u32[]{:S(2)}, u32[]{:S(2)}) %collective-permute-start.2) | collective-permute-done | bytes 215072 | tf_op jit(solution)/shard_map/ppermute | solution.py:626
  14.9 0.2 shard_map.121
  15.0 1.7 %collective-permute-start.4 = (bf16[1960,128]{1,0:T(8,128)(2,1)S(1)}, bf16[1960,128]{1,0:T(8,128)(2,1)S(1)}, u32[]{:S(2)}, u32[]{:S(2)}) collective-permute-start(bf16[1960,128]{1,0:T(8,128)(2,1)S(1)} %get-tuple-element.46), channel_id=1, source_target_pairs={{0,1},{1,0},{2,3},{3,2},{4,5},{5,4},{6,7},{7,6},{8,9},{9,8},{10,11... | collective-permute-start | bytes 1505288 | tf_op jit(solution)/shard_map/ppermute | solution.py:634
  16.8 0.1 shard_map.119
  16.8 3.0 %collective-permute-start = (bf16[840,128]{1,0:T(8,128)(2,1)S(1)}, bf16[840,128]{1,0:T(8,128)(2,1)S(1)}, u32[]{:S(2)}, u32[]{:S(2)}) collective-permute-start(bf16[840,128]{1,0:T(8,128)(2,1)S(1)} %shard_map.119), channel_id=1, source_target_pairs={{1,2},{2,1},{3,4},{4,3},{5,6},{6,5},{9,10},{10,9},{11,12},{12,11},... | collective-permute-start | bytes 645128 | tf_op jit(solution)/shard_map/ppermute | solution.py:634
  19.9 2.5 %collective-permute-start.3 = (bf16[1120,128]{1,0:T(8,128)(2,1)S(1)}, bf16[1120,128]{1,0:T(8,128)(2,1)S(1)}, u32[]{:S(2)}, u32[]{:S(2)}) collective-permute-start(bf16[1120,128]{1,0:T(8,128)(2,1)S(1)} %get-tuple-element.32), channel_id=1, source_target_pairs={{1,2},{2,1},{3,4},{4,3},{5,6},{6,5},{9,10},{10,9},{11,12},{12,11},... | collective-permute-start | bytes 860168 | tf_op jit(solution)/shard_map/ppermute | solution.py:634
  22.4 0.0 copy-start.5
  22.4 0.0 copy-start.6
  22.5 0.0 copy-start.8
  22.5 0.0 copy-start.9
  22.5 1.4 %shard_map.122 = (bf16[4,2,320,128]{3,2,1,0:T(8,128)(2,1)S(1)}, bf16[4,2,320,128]{3,2,1,0:T(8,128)(2,1)S(1)}, bf16[2,2,320,128]{3,2,1,0:T(8,128)(2,1)S(1)}, bf16...) custom-call(bf16[1320,128]{1,0:T(8,128)(2,1)S(1)} %get-tuple-element, ...), custom_call_target="tpu_custom_call" | custom-call | flops 2000000000 | bytes 1000000 | tf_op jit(solution)/shard_map/pallas_call | solution.py:717
  23.9 0.0 collective-permute-done.4.side_ref
  23.9 3.8 %shard_map.123 = (bf16[32,2,8,80]{3,2,1,0:T(8,128)(2,1)S(1)}, bf16[2,320,128]{2,1,0:T(8,128)(2,1)S(1)}, bf16[2,192,128]{2,1,0:T(8,128)(2,1)S(1)}, bf16[2,2,192,128]{3,2,1,0:T(8,128)(2,1)S(1)}) custom-call(s32[1]{0:T(128)S(6)} %sub.3.right_ref, bf16[1960,128]{1,0:T(8,128)(2,1)S(1)} %collective-permute-done.4.side_ref, ...), custom_call_target="tpu_custom_call" | custom-call | flops 4000000000 | bytes 1000000 | tf_op jit(solution)/shard_map/pallas_call | solution.py:722
  27.7 0.0 collective-permute-done.middle_ref
  27.7 0.1 collective-permute-done.3.flanks_ref
  27.8 5.0 %shard_map.124 = bf16[32,8,8,80]{3,2,1,0:T(8,128)(2,1)} custom-call(s32[1]{0:T(128)S(6)} %sub.3.right_ref, bf16[840,128]{1,0:T(8,128)(2,1)S(1)} %collective-permute-done.middle_ref, bf16[1120,128]{1,0:T(8,128)(2,1)S(1)} %collective-permute-done.3.flanks_ref, bf16[1024,512]{1,0:T(8,128)(2,1)S(1)} %get-tuple-element.33.we_ref.refs_0_, f32[1,32]{1,0:T(1,128)S(1)} %bitcast.12, ...), custom_call_target="tpu_custom_call" | custom-call | flops 5000000000 | bytes 1000000 | tf_op jit(solution)/shard_map/pallas_call | solution.py:732
  (16 shorter events, 0.0 us)
Async XLA Ops:
  0.0 8.7 %copy-start = (bf16[128,256]{1,0:T(8,128)(2,1)S(1)}, bf16[128,256]{1,0:T(8,128)(2,1)}, u32[]{:S(2)}) copy-start(bf16[128,256]{1,0:T(8,128)(2,1)} %param.18) | copy-start | bytes 196612
  0.0 8.9 %copy-start.2 = (bf16[27,32,32]{2,1,0:T(8,128)(2,1)S(1)}, bf16[27,32,32]{2,1,0:T(8,128)(2,1)}, u32[]{:S(2)}) copy-start(bf16[27,32,32]{2,1,0:T(8,128)(2,1)} %we_ref.1) | copy-start | bytes 165892
  0.0 8.9 %copy-start.4 = (bf16[128,256]{1,0:T(8,128)(2,1)S(1)}, bf16[128,256]{1,0:T(8,128)(2,1)}, u32[]{:S(2)}) copy-start(bf16[128,256]{1,0:T(8,128)(2,1)} %wn_ref.1) | copy-start | bytes 196612
  0.0 8.9 %copy-start.1 = (bf16[27,128,128]{2,1,0:T(8,128)(2,1)S(1)}, bf16[27,128,128]{2,1,0:T(8,128)(2,1)}, u32[]{:S(2)}) copy-start(bf16[27,128,128]{2,1,0:T(8,128)(2,1)} %wc_ref.1) | copy-start | bytes 2654212
  0.0 8.9 %copy-start.3 = (bf16[27,32,64]{2,1,0:T(8,128)(2,1)S(1)}, bf16[27,32,64]{2,1,0:T(8,128)(2,1)}, u32[]{:S(2)}) copy-start(bf16[27,32,64]{2,1,0:T(8,128)(2,1)} %wd_ref.1) | copy-start | bytes 331780
  2.4 8.3 %collective-permute-start.1 = (bf16[840,128]{1,0:T(8,128)(2,1)S(1)}, bf16[840,128]{1,0:T(8,128)(2,1)S(1)}, u32[]{:S(2)}, u32[]{:S(2)}) collective-permute-start(bf16[840,128]{1,0:T(8,128)(2,1)S(1)} %get-tuple-element.29), channel_id=1, source_target_pairs={{0,8},{8,16},{16,24},{24,32},{32,40},{40,48},{48,56},{56,64},{64,7... | collective-permute-start | bytes 645128 | tf_op jit(solution)/shard_map/ppermute | solution.py:626
  6.7 8.1 %collective-permute-start.2 = (bf16[840,128]{1,0:T(8,128)(2,1)S(1)}, bf16[840,128]{1,0:T(8,128)(2,1)S(1)}, u32[]{:S(2)}, u32[]{:S(2)}) collective-permute-start(bf16[840,128]{1,0:T(8,128)(2,1)S(1)} %get-tuple-element.30), channel_id=1, source_target_pairs={{8,0},{16,8},{24,16},{32,24},{40,32},{48,40},{56,48},{64,56},{72,6... | collective-permute-start | bytes 645128 | tf_op jit(solution)/shard_map/ppermute | solution.py:626
  9.0 13.5 %copy-start.7 = (f32[32]{0:T(128)S(1)}, f32[32]{0:T(128)}, u32[]{:S(2)}) copy-start(f32[32]{0:T(128)} %param.16) | copy-start | bytes 388
  15.0 8.8 %collective-permute-start.4 = (bf16[1960,128]{1,0:T(8,128)(2,1)S(1)}, bf16[1960,128]{1,0:T(8,128)(2,1)S(1)}, u32[]{:S(2)}, u32[]{:S(2)}) collective-permute-start(bf16[1960,128]{1,0:T(8,128)(2,1)S(1)} %get-tuple-element.46), channel_id=1, source_target_pairs={{0,1},{1,0},{2,3},{3,2},{4,5},{5,4},{6,7},{7,6},{8,9},{9,8},{10,11... | collective-permute-start | bytes 1505288 | tf_op jit(solution)/shard_map/ppermute | solution.py:634
  16.8 10.9 %collective-permute-start = (bf16[840,128]{1,0:T(8,128)(2,1)S(1)}, bf16[840,128]{1,0:T(8,128)(2,1)S(1)}, u32[]{:S(2)}, u32[]{:S(2)}) collective-permute-start(bf16[840,128]{1,0:T(8,128)(2,1)S(1)} %shard_map.119), channel_id=1, source_target_pairs={{1,2},{2,1},{3,4},{4,3},{5,6},{6,5},{9,10},{10,9},{11,12},{12,11},... | collective-permute-start | bytes 645128 | tf_op jit(solution)/shard_map/ppermute | solution.py:634
  19.9 8.0 %collective-permute-start.3 = (bf16[1120,128]{1,0:T(8,128)(2,1)S(1)}, bf16[1120,128]{1,0:T(8,128)(2,1)S(1)}, u32[]{:S(2)}, u32[]{:S(2)}) collective-permute-start(bf16[1120,128]{1,0:T(8,128)(2,1)S(1)} %get-tuple-element.32), channel_id=1, source_target_pairs={{1,2},{2,1},{3,4},{4,3},{5,6},{6,5},{9,10},{10,9},{11,12},{12,11},... | collective-permute-start | bytes 860168 | tf_op jit(solution)/shard_map/ppermute | solution.py:634
  22.4 1.4 %copy-start.5 = (s32[8,8,80]{2,1,0:T(8,128)S(1)}, s32[8,8,80]{2,1,0:T(8,128)}, u32[]{:S(2)}) copy-start(s32[8,8,80]{2,1,0:T(8,128)} %refs_8_.3) | copy-start | bytes 61444
  22.4 1.4 %copy-start.6 = (bf16[32,128]{1,0:T(8,128)(2,1)S(1)}, bf16[32,128]{1,0:T(8,128)(2,1)}, u32[]{:S(2)}) copy-start(bf16[32,128]{1,0:T(8,128)(2,1)} %refs_7_.3) | copy-start | bytes 24580
  22.5 1.4 %copy-start.8 = (f32[128]{0:T(128)S(1)}, f32[128]{0:T(128)}, u32[]{:S(2)}) copy-start(f32[128]{0:T(128)} %param.20) | copy-start | bytes 1540
  22.5 1.4 %copy-start.9 = (f32[32]{0:T(128)S(1)}, f32[32]{0:T(128)}, u32[]{:S(2)}) copy-start(f32[32]{0:T(128)} %param.23) | copy-start | bytes 388

commit v8 on v7

--- a/solution.py
+++ b/solution.py
@@ -34,9 +34,6 @@
 SIDE = 8 * PAIR
 SIDE_MASK = SIDE + 4 * ZC
 SIDE_ROWS = SIDE_MASK + ZC
-PLANE = 9 * PAIR
-HALF = 5 * PAIR
-MASKS = 3 * ZC
 MIDDLE = 10 * PAIR
 FLANKS = 13 * PAIR
 
@@ -119,62 +116,38 @@
     return jnp.where(lane_a == right, even, pltpu.roll(odd, 64, 1)).astype(BF16)
 
 
-def edge_kernel(odd_ref, own_ref, out_ref):
-    right = odd_ref[0]
-    for i, x in enumerate((3 * right, 1 + right)):
-        out_ref[4 * PAIR * i : 4 * PAIR * (i + 1)] = own_ref[part(x, 4 * PAIR)]
-    x = 2 - right
-    pieces = [own_ref[pl.ds(pl.multiple_of((4 * x + 2 * cz) * PAIR, PAIR), 2 * PAIR)] for cz in BITS]
-    out_ref[8 * PAIR : 10 * PAIR] = folded(pieces, right)
-    out_ref[MIDDLE : MIDDLE + ZC] = own_ref[OWN : OWN + ZC]
-
-
-def mid_kernel(odd_ref, own_ref, low_ref, high_ref, tie_ref, tie2_ref, far_ref, near_ref, ends_ref):
+def edge_kernel(odd_ref, own_ref, far_ref, near_ref):
+    for out_ref, right in ((far_ref, odd_ref[0]), (near_ref, 1 - odd_ref[0])):
+        for i, x in enumerate((3 * right, 1 + right)):
+            out_ref[4 * PAIR * i : 4 * PAIR * (i + 1)] = own_ref[part(x, 4 * PAIR)]
+        x = 2 - right
+        pieces = [own_ref[pl.ds(pl.multiple_of((4 * x + 2 * cz) * PAIR, PAIR), 2 * PAIR)] for cz in BITS]
+        out_ref[8 * PAIR : 10 * PAIR] = folded(pieces, right)
+        out_ref[MIDDLE : MIDDLE + ZC] = own_ref[OWN : OWN + ZC]
+
+
+def mid_kernel(odd_ref, low_ref, high_ref, tie_ref, tie2_ref, far_ref, near_ref, ends_ref):
     ends_ref[0] = low_ref[SIDE:SIDE_MASK].astype(F32)
     ends_ref[1] = high_ref[SIDE:SIDE_MASK].astype(F32)
-
-    def layer(x, cz):
-        return (
-            low_ref[pl.ds(pl.multiple_of(x * 2 * PAIR + cz * PAIR, PAIR), PAIR)],
-            own_ref[pl.ds(pl.multiple_of(x * 4 * PAIR + 2 * cz * PAIR, PAIR), 2 * PAIR)],
-            high_ref[pl.ds(pl.multiple_of(x * 2 * PAIR + cz * PAIR, PAIR), PAIR)],
-        )
 
     def ends(x):
         at = part(x, ZC)
         return stacked(ends_ref[0, at], ends_ref[1, at]).astype(BF16)
 
-    right = 1 - odd_ref[0]
-    for i, x in enumerate((3 * right, 1 + right)):
-        at = i * PLANE
-        for cz in BITS:
-            low, own, high = layer(x, cz)
-            near_ref[at : at + PAIR] = low
-            near_ref[at + PAIR : at + 3 * PAIR] = own
-            near_ref[at + 3 * PAIR : at + 4 * PAIR] = high
-            at = at + 4 * PAIR
-        near_ref[at : at + PAIR] = ends(x)
-    x, at = 2 - right, 2 * PLANE
-    low, own, high = zip(*[layer(x, cz) for cz in BITS])
-    near_ref[at : at + PAIR] = folded(low, right)
-    near_ref[at + PAIR : at + 3 * PAIR] = folded(own, right)
-    near_ref[at + 3 * PAIR : at + 4 * PAIR] = folded(high, right)
-    near_ref[at + 4 * PAIR : at + HALF] = ends(x)
-    masks = [low_ref[SIDE_MASK:SIDE_ROWS], own_ref[OWN : OWN + ZC], high_ref[SIDE_MASK:SIDE_ROWS]]
-    near_ref[at + HALF : at + HALF + MASKS] = stacked(*[m.astype(F32) for m in masks]).astype(BF16)
-    right = odd_ref[0]
-    for i, x in enumerate((3 * right, 1 + right)):
-        at = 5 * PAIR * i
-        far_ref[at : at + 2 * PAIR] = low_ref[part(x, 2 * PAIR)]
-        far_ref[at + 2 * PAIR : at + 4 * PAIR] = high_ref[part(x, 2 * PAIR)]
-        far_ref[at + 4 * PAIR : at + 5 * PAIR] = ends(x)
-    x, at = 2 - right, 10 * PAIR
-    low, own, high = zip(*[layer(x, cz) for cz in BITS])
-    far_ref[at : at + PAIR] = folded(low, right)
-    far_ref[at + PAIR : at + 2 * PAIR] = folded(high, right)
-    far_ref[at + 2 * PAIR : at + 3 * PAIR] = ends(x)
-    masks = [low_ref[SIDE_MASK:SIDE_ROWS], high_ref[SIDE_MASK:SIDE_ROWS]]
-    far_ref[FLANKS : FLANKS + PAIR] = stacked(*[m.astype(F32) for m in masks]).astype(BF16)
+    for out_ref, right in ((far_ref, odd_ref[0]), (near_ref, 1 - odd_ref[0])):
+        for i, x in enumerate((3 * right, 1 + right)):
+            at = 5 * PAIR * i
+            out_ref[at : at + 2 * PAIR] = low_ref[part(x, 2 * PAIR)]
+            out_ref[at + 2 * PAIR : at + 4 * PAIR] = high_ref[part(x, 2 * PAIR)]
+            out_ref[at + 4 * PAIR : at + 5 * PAIR] = ends(x)
+        x, at = 2 - right, 10 * PAIR
+        for ref in (low_ref, high_ref):
+            pieces = [ref[pl.ds(pl.multiple_of((2 * x + cz) * PAIR, PAIR), PAIR)] for cz in BITS]
+            out_ref[at : at + PAIR] = folded(pieces, right)
+            at = at + PAIR
+        out_ref[at : at + PAIR] = ends(x)
+        masks = [low_ref[SIDE_MASK:SIDE_ROWS], high_ref[SIDE_MASK:SIDE_ROWS]]
+        out_ref[FLANKS : FLANKS + PAIR] = stacked(*[m.astype(F32) for m in masks]).astype(BF16)
 
 
 def tap_of(out_bit, in_bit, far):
@@ -298,17 +271,7 @@
         put_plane(a_ref.at[x], v_ref.at[x], layers, stacked(low_ends[z], high_ends[z]))
 
 
-def load_full(ref, at, a_ref, v_ref):
-    layers = [ref[at + 320 * cz : at + 320 * cz + 320] for cz in BITS]
-    put_plane(a_ref, v_ref, layers, ref[at + 640 : at + PLANE].astype(F32))
-
-
-def load_half(ref, at, a_ref, v_ref):
-    both = ref[at : at + 320].astype(F32)
-    put_plane(a_ref, v_ref, [both, pltpu.roll(both, 64, 1)], ref[at + 320 : at + HALF].astype(F32))
-
-
-def load_far(mid_ref, flank_ref, a, v, k_ref):
+def load_side(mid_ref, flank_ref, a, v, k_ref):
     for i in range(2):
         mine, at = 4 * PAIR * i, 5 * PAIR * i
         layers = []
@@ -336,11 +299,6 @@
         m = jnp.maximum(m, pltpu.roll(m, LANES - 64, 1))
         k_ref[0, by, 0:ZC] = k
         k_ref[1, by, 0:ZC] = m
-
-
-def load_side_masks(ref, at, k_ref):
-    masks = ref[at : at + MASKS].astype(F32)
-    load_masks([masks[ZC * i : ZC * i + ZC] for i in range(3)], k_ref)
 
 
 def spread(k, index):
@@ -431,7 +389,7 @@
     return nn(beside(*lhs), wd_ref[...])
 
 
-def decode_finish(o, xo, bd, perm, back, m_ref, out_ref, at):
+def decode_finish(o, xo, bd, perm, back, m_ref, out_ref, at, send=None):
     z4 = depth_of(160)
     first, last = z4 == 0, z4 == ZC - 1
     d0 = o[:, 0:128] + moved(o[:, 256:384], 1, first) + bd
@@ -443,6 +401,8 @@
     for a in BITS:
         t = jnp.transpose(d[:, 256 * a : 256 * a + 256])[:, :Z].reshape(CH, 8, Z)
         out_ref[:, at + a] = jnp.where(m_ref[2 * xo + a][None] > 0, t, 0.0).astype(BF16)
+        if send is not None:
+            send(at + a, 2 * xo + a)
 
 
 def own_kernel(
@@ -505,7 +465,7 @@
         self.emit(i, dot, self.bd, self.perm, self.back, self.m)
 
 
-def near_kernel(right_ref, side_ref, *refs):
+def near_kernel(right_ref, middle_ref, flanks_ref, *refs):
     weights, misc, own = refs[:8], refs[8:13], refs[13:21]
     done_ref, e1_ref, ev1_ref, u1_ref = refs[21:25]
     a_ref, v_ref, e_ref, ev_ref, c_ref, d_ref, o_ref, k_ref, u_ref = refs[25:]
@@ -514,10 +474,7 @@
     a, v, c, d, o = (x + [r.at[i] for i in range(3)] for x, r in zip((a, v, c, d, o), (a_ref, v_ref, c_ref, d_ref, o_ref)))
     e, ev = [None] + e + [e1_ref, e_ref.at[0]], [None] + ev + [ev1_ref, ev_ref.at[0]]
     u = [None, None, u1_ref.at[0], u1_ref.at[1], u_ref.at[0]]
-    for i in range(2):
-        load_full(side_ref, i * PLANE, a[2 + i], v[2 + i])
-    load_half(side_ref, 2 * PLANE, a[4], v[4])
-    load_side_masks(side_ref, 2 * PLANE + HALF, k_ref)
+    load_side(middle_ref, flanks_ref, a[2:], v[2:], k_ref)
 
     def emit(i, dot, bd, perm, back, m_ref):
         decode_finish(dot, 3 * right, bd, perm, back, m_ref, done_ref, 0)
@@ -551,21 +508,23 @@
     a_ref, v_ref, e_ref, ev_ref, c_ref, d_ref, o_ref, k_ref, u_ref, out_ref, sems = refs[26:]
     left = right_ref[0]
     right = 1 - left
-    copies = [pltpu.make_async_copy(near_done_ref, out_hbm.at[:, pl.ds(6 * left, 2)], sems.at[3])]
+    copies = [pltpu.make_async_copy(near_done_ref, out_hbm.at[:, pl.ds(6 * left, 2)], sems.at[6])]
     copies[0].start()
     a, v, e, ev, c, d, o = own_planes(right, own)
     a, v, c, d, o = (x + [r.at[i] for i in range(3)] for x, r in zip((a, v, c, d, o), (a_ref, v_ref, c_ref, d_ref, o_ref)))
     e = [e1_ref] + e + [e_ref.at[0], e_ref.at[1]]
     ev = [ev1_ref] + ev + [ev_ref.at[0], ev_ref.at[1]]
     u = [u1_ref.at[1], u1_ref.at[0]] + [u_ref.at[i] for i in range(3)]
-    load_far(middle_ref, flanks_ref, a[2:], v[2:], k_ref)
+    load_side(middle_ref, flanks_ref, a[2:], v[2:], k_ref)
+
+    def send(source, place):
+        copies.append(
+            pltpu.make_async_copy(out_ref.at[:, pl.ds(source, 1)], out_hbm.at[:, pl.ds(place, 1)], sems.at[source])
+        )
+        copies[-1].start()
 
     def emit(i, dot, bd, perm, back, m_ref):
-        xo = far_place(right, i)
-        at = pl.ds(2 * i, 2)
-        decode_finish(dot, xo, bd, perm, back, m_ref, out_ref, 2 * i)
-        copies.append(pltpu.make_async_copy(out_ref.at[:, at], out_hbm.at[:, pl.ds(2 * xo, 2)], sems.at[i]))
-        copies[-1].start()
+        decode_finish(dot, far_place(right, i), bd, perm, back, m_ref, out_ref, 2 * i, send)
 
     w = Stages(right, weights, misc, (a, v, e, ev, c, d, o, u), k_ref, own[7], emit)
     e0 = w.e_dot(0)
@@ -681,8 +640,10 @@
 
     odd = lax.axis_index("narrow").astype(jnp.int32)[None] & 1
     near_right = 1 - odd
-    middle = call(edge_kernel, [array(MIDDLE + ZC, LANES)], SCALAR + vmem(1), vmem(1), [], 8, 10**8)(odd, own)[0]
+    message = array(MIDDLE + ZC, LANES)
+    middle, middle_near = call(edge_kernel, [message, message], SCALAR + vmem(1), vmem(2), [], 8, 10**8)(odd, own)
     middle = swapped(middle, "narrow", 1)
+    middle_near = swapped(middle_near, "narrow", 0)
 
     embedded = time_features(timestep, w_time.shape[0])
     film = jnp.dot(embedded[None], w_time, preferred_element_type=F32)
@@ -701,15 +662,10 @@
         4 * 10**9,
     )(w_enc, w_dec, w_down, w_coarse)
 
+    message = array(FLANKS + PAIR, LANES)
     flanks, near = call(
-        mid_kernel,
-        [array(FLANKS + PAIR, LANES), array(2 * PLANE + HALF + MASKS, LANES)],
-        SCALAR + vmem(5),
-        vmem(2),
-        buffers([((2, 4 * ZC, LANES), F32)]),
-        8,
-        10**8,
-    )(odd, own, low, high, down_w, gains)
+        mid_kernel, [message, message], SCALAR + vmem(4), vmem(2), buffers([((2, 4 * ZC, LANES), F32)]), 8, 10**8
+    )(odd, low, high, down_w, gains)
     flanks = swapped(flanks, "narrow", 1)
     near = swapped(near, "narrow", 0)
 
@@ -722,19 +678,19 @@
     near_done, e1, ev1, u1 = call(
         near_kernel,
         [pair] + arrays(state((), (), ())[2:4] + [((2,) + LIFTED, BF16)]),
-        SCALAR + vmem(22),
+        SCALAR + vmem(23),
         vmem(4),
         buffers(state((3,), (3,), (1,)) + [((1,) + LIFTED, BF16)]),
         24,
         4 * 10**9,
-    )(near_right, near, *some)
+    )(near_right, middle_near, near, *some)
     rest = pltpu.VMEM((fine_in.shape[0], 6) + fine_in.shape[2:], BF16)
     return call(
         far_kernel,
         [array(*fine_in.shape)],
         SCALAR + vmem(27),
         hbm(1),
-        buffers(state((3,), (3,), (2,)) + [((3,) + LIFTED, BF16)]) + [rest, pltpu.SemaphoreType.DMA((4,))],
+        buffers(state((3,), (3,), (2,)) + [((3,) + LIFTED, BF16)]) + [rest, pltpu.SemaphoreType.DMA((7,))],
         24,
         5 * 10**9,
     )(near_right, middle, flanks, *some, near_done, e1, ev1, u1)[0]

time: 33 us -> 33.4 us (1.012)
  waiting for transfers between devices: 4.51 us -> 5.06 us
    ppermute x3 -> x4, waiting for transfers between devices: 0.13 us -> 0.66 us  [swapped(): return lax.ppermute(value, axis, pairs)]
    ppermute x3 -> x4, starting transfers between devices: 7.28 us -> 7.38 us  [swapped(): return lax.ppermute(value, axis, pairs)]
  transfers between devices with their start and end apart: 5 -> 6, of which waited for: 3 -> 3; matrix products, arithmetic and copies ran while one was open for 1% -> 1% of each run, Pallas kernels for 21% -> 20%
where the time goes in v8:
time: 33.4 us; the launch traced here: 33.2 us
  Pallas kernels  13.9 us (42%)
  starting transfers between devices  13 us (39%)
  waiting for transfers between devices  5.06 us (15%)
  between operations  0.89 us (3%)
    ppermute x4, starting transfers between devices, swapped(): return lax.ppermute(value, axis, pairs)  7.38 us
    ppermute x2, starting transfers between devices, shifted(): lax.ppermute(value, axis, [(i, i + step) for i in range(peers) if 0 <= i...  5.67 us
    pallas_call x1, Pallas kernels, on_device(): call(far_kernel, [array(*fine_in.shape)], SCALAR + vmem(27), hbm(1), buff...  4.82 us
    ppermute x2, waiting for transfers between devices, shifted(): lax.ppermute(value, axis, [(i, i + step) for i in range(peers) if 0 <= i...  4.4 us
    pallas_call x1, Pallas kernels, on_device(): call(near_kernel, [pair] + arrays(state((), (), ())[2:4] + [((2,) + LIFTE...  3.71 us
    pallas_call x1, Pallas kernels, on_device(): call(pack_kernel, [array(OWN + ZC, LANES), array(SIDE_ROWS, LANES), array...  2.31 us
    pallas_call x1, Pallas kernels, on_device(): call(weights_kernel, [array(1024, 512), array(1536, 512), array(128, 256)...  1.48 us
    pallas_call x1, Pallas kernels, on_device(): call(own_kernel, arrays(state((4,), (2,), (2,))), vmem(8), vmem(8), [], 1...  1.37 us
  transfers between devices with their start and end apart: 6, of which 3 were waited for; matrix products, arithmetic and copies ran while one was open for 1% of the time, Pallas kernels for 20%

profile of v8, /device:TPU:1, one launch (start us, length us, event | category | flops | bytes accessed | tf_op | source)
XLA Modules:
  0.0 33.2 jit_solution(1287361676579176869)
XLA Ops:
  0.0 2.3 %shard_map.118 = (bf16[1320,128]{1,0:T(8,128)(2,1)S(1)}, bf16[840,128]{1,0:T(8,128)(2,1)S(1)}, bf16[840,128]{1,0:T(8,128)(2,1)S(1)}) custom-call(bf16[32,8,8,80]{3,2,1,0:T(8,128)(2,1)} %x_hbm.1, s32[8,8,80]{2,1,0:T(8,128)} %refs_8_.3), custom_call_target="tpu_custom_call" | custom-call | flops 1000000000 | bytes 1000000 | tf_op jit(solution)/shard_map/pallas_call | solution.py:629
  2.4 4.4 %collective-permute-start.1 = (bf16[840,128]{1,0:T(8,128)(2,1)S(1)}, bf16[840,128]{1,0:T(8,128)(2,1)S(1)}, u32[]{:S(2)}, u32[]{:S(2)}) collective-permute-start(bf16[840,128]{1,0:T(8,128)(2,1)S(1)} %get-tuple-element.32), channel_id=1, source_target_pairs={{0,8},{8,16},{16,24},{24,32},{32,40},{40,48},{48,56},{56,64},{64,7... | collective-permute-start | bytes 645128 | tf_op jit(solution)/shard_map/ppermute | solution.py:585
  6.7 1.3 %collective-permute-start.2 = (bf16[840,128]{1,0:T(8,128)(2,1)S(1)}, bf16[840,128]{1,0:T(8,128)(2,1)S(1)}, u32[]{:S(2)}, u32[]{:S(2)}) collective-permute-start(bf16[840,128]{1,0:T(8,128)(2,1)S(1)} %get-tuple-element.33), channel_id=1, source_target_pairs={{8,0},{16,8},{24,16},{32,24},{40,32},{48,40},{56,48},{64,56},{72,6... | collective-permute-start | bytes 645128 | tf_op jit(solution)/shard_map/ppermute | solution.py:585
  8.7 0.1 cosine_convert_fusion
  8.8 0.2 fusion
  9.0 0.0 copy-start.7
  9.0 1.5 %shard_map.120 = (bf16[1024,512]{1,0:T(8,128)(2,1)S(1)}, bf16[1536,512]{1,0:T(8,128)(2,1)S(1)}, bf16[128,256]{1,0:T(8,128)(2,1)S(1)}, bf16[512,512]{1,0:T(8,128)...) custom-call(bf16[27,32,32]{2,1,0:T(8,128)(2,1)S(1)} %copy-done.2, ...), custom_call_target="tpu_custom_call" | custom-call | flops 4000000000 | bytes 1000000 | tf_op jit(solution)/shard_map/pallas_call | solution.py:654
  10.5 0.2 collective-permute-done.1.low_ref
  10.7 4.2 %collective-permute-done.2.high_ref = bf16[840,128]{1,0:T(8,128)(2,1)S(1)} collective-permute-done((bf16[840,128]{1,0:T(8,128)(2,1)S(1)}, bf16[840,128]{1,0:T(8,128)(2,1)S(1)}, u32[]{:S(2)}, u32[]{:S(2)}) %collective-permute-start.2) | collective-permute-done | bytes 215072 | tf_op jit(solution)/shard_map/ppermute | solution.py:585
  14.9 0.1 shard_map.121
  15.0 1.7 %collective-permute-start.5 = (bf16[1120,128]{1,0:T(8,128)(2,1)S(1)}, bf16[1120,128]{1,0:T(8,128)(2,1)S(1)}, u32[]{:S(2)}, u32[]{:S(2)}) collective-permute-start(bf16[1120,128]{1,0:T(8,128)(2,1)S(1)} %get-tuple-element.50), channel_id=1, source_target_pairs={{0,1},{1,0},{2,3},{3,2},{4,5},{5,4},{6,7},{7,6},{8,9},{9,8},{10,11... | collective-permute-start | bytes 860168 | tf_op jit(solution)/shard_map/ppermute | solution.py:593
  16.7 0.1 shard_map.119
  16.8 0.1 collective-permute-start.4
  16.9 3.5 %collective-permute-start = (bf16[840,128]{1,0:T(8,128)(2,1)S(1)}, bf16[840,128]{1,0:T(8,128)(2,1)S(1)}, u32[]{:S(2)}, u32[]{:S(2)}) collective-permute-start(bf16[840,128]{1,0:T(8,128)(2,1)S(1)} %get-tuple-element.31), channel_id=1, source_target_pairs={{1,2},{2,1},{3,4},{4,3},{5,6},{6,5},{9,10},{10,9},{11,12},{12,11},... | collective-permute-start | bytes 645128 | tf_op jit(solution)/shard_map/ppermute | solution.py:593
  20.4 2.1 %collective-permute-start.3 = (bf16[1120,128]{1,0:T(8,128)(2,1)S(1)}, bf16[1120,128]{1,0:T(8,128)(2,1)S(1)}, u32[]{:S(2)}, u32[]{:S(2)}) collective-permute-start(bf16[1120,128]{1,0:T(8,128)(2,1)S(1)} %get-tuple-element.35), channel_id=1, source_target_pairs={{1,2},{2,1},{3,4},{4,3},{5,6},{6,5},{9,10},{10,9},{11,12},{12,11},... | collective-permute-start | bytes 860168 | tf_op jit(solution)/shard_map/ppermute | solution.py:593
  22.5 0.0 copy-start.5
  22.5 0.0 copy-start.6
  22.6 0.0 copy-start.8
  22.6 0.0 copy-start.9
  22.6 1.4 %shard_map.122 = (bf16[4,2,320,128]{3,2,1,0:T(8,128)(2,1)S(1)}, bf16[4,2,320,128]{3,2,1,0:T(8,128)(2,1)S(1)}, bf16[2,2,320,128]{3,2,1,0:T(8,128)(2,1)S(1)}, bf16...) custom-call(bf16[1320,128]{1,0:T(8,128)(2,1)S(1)} %get-tuple-element, ...), custom_call_target="tpu_custom_call" | custom-call | flops 2000000000 | bytes 1000000 | tf_op jit(solution)/shard_map/pallas_call | solution.py:673
  24.0 0.0 collective-permute-done.4.middle_ref
  24.0 3.7 %shard_map.123 = (bf16[32,2,8,80]{3,2,1,0:T(8,128)(2,1)S(1)}, bf16[2,320,128]{2,1,0:T(8,128)(2,1)S(1)}, bf16[2,192,128]{2,1,0:T(8,128)(2,1)S(1)}, bf16[2,2,192,128]{3,2,1,0:T(8,128)(2,1)S(1)}) custom-call(s32[1]{0:T(128)S(6)} %sub.3.right_ref, bf16[840,128]{1,0:T(8,128)(2,1)S(1)} %collective-permute-done.4.middle_ref, ...), custom_call_target="tpu_custom_call" | custom-call | flops 4000000000 | bytes 1000000 | tf_op jit(solution)/shard_map/pallas_call | solution.py:678
  27.7 0.7 %collective-permute-done.3.flanks_ref = bf16[1120,128]{1,0:T(8,128)(2,1)S(1)} collective-permute-done((bf16[1120,128]{1,0:T(8,128)(2,1)S(1)}, bf16[1120,128]{1,0:T(8,128)(2,1)S(1)}, u32[]{:S(2)}, u32[]{:S(2)}) %collective-permute-start.3) | collective-permute-done | bytes 286752 | tf_op jit(solution)/shard_map/ppermute | solution.py:593
  28.4 4.8 %shard_map.124 = bf16[32,8,8,80]{3,2,1,0:T(8,128)(2,1)} custom-call(s32[1]{0:T(128)S(6)} %sub.3.right_ref, bf16[840,128]{1,0:T(8,128)(2,1)S(1)} %collective-permute-done.middle_ref, bf16[1120,128]{1,0:T(8,128)(2,1)S(1)} %collective-permute-done.3.flanks_ref, bf16[1024,512]{1,0:T(8,128)(2,1)S(1)} %get-tuple-element.36.we_ref.refs_0_, f32[1,32]{1,0:T(1,128)S(1)} %bitcast.12, ...), custom_call_target="tpu_custom_call" | custom-call | flops 5000000000 | bytes 1000000 | tf_op jit(solution)/shard_map/pallas_call | solution.py:688
  (18 shorter events, 0.0 us)
Async XLA Ops:
  0.0 8.7 %copy-start = (bf16[128,256]{1,0:T(8,128)(2,1)S(1)}, bf16[128,256]{1,0:T(8,128)(2,1)}, u32[]{:S(2)}) copy-start(bf16[128,256]{1,0:T(8,128)(2,1)} %param.18) | copy-start | bytes 196612
  0.0 8.9 %copy-start.2 = (bf16[27,32,32]{2,1,0:T(8,128)(2,1)S(1)}, bf16[27,32,32]{2,1,0:T(8,128)(2,1)}, u32[]{:S(2)}) copy-start(bf16[27,32,32]{2,1,0:T(8,128)(2,1)} %we_ref.1) | copy-start | bytes 165892
  0.0 8.9 %copy-start.4 = (bf16[128,256]{1,0:T(8,128)(2,1)S(1)}, bf16[128,256]{1,0:T(8,128)(2,1)}, u32[]{:S(2)}) copy-start(bf16[128,256]{1,0:T(8,128)(2,1)} %wn_ref.1) | copy-start | bytes 196612
  0.0 8.9 %copy-start.1 = (bf16[27,128,128]{2,1,0:T(8,128)(2,1)S(1)}, bf16[27,128,128]{2,1,0:T(8,128)(2,1)}, u32[]{:S(2)}) copy-start(bf16[27,128,128]{2,1,0:T(8,128)(2,1)} %wc_ref.1) | copy-start | bytes 2654212
  0.0 8.9 %copy-start.3 = (bf16[27,32,64]{2,1,0:T(8,128)(2,1)S(1)}, bf16[27,32,64]{2,1,0:T(8,128)(2,1)}, u32[]{:S(2)}) copy-start(bf16[27,32,64]{2,1,0:T(8,128)(2,1)} %wd_ref.1) | copy-start | bytes 331780
  2.4 8.3 %collective-permute-start.1 = (bf16[840,128]{1,0:T(8,128)(2,1)S(1)}, bf16[840,128]{1,0:T(8,128)(2,1)S(1)}, u32[]{:S(2)}, u32[]{:S(2)}) collective-permute-start(bf16[840,128]{1,0:T(8,128)(2,1)S(1)} %get-tuple-element.32), channel_id=1, source_target_pairs={{0,8},{8,16},{16,24},{24,32},{32,40},{40,48},{48,56},{56,64},{64,7... | collective-permute-start | bytes 645128 | tf_op jit(solution)/shard_map/ppermute | solution.py:585
  6.7 8.1 %collective-permute-start.2 = (bf16[840,128]{1,0:T(8,128)(2,1)S(1)}, bf16[840,128]{1,0:T(8,128)(2,1)S(1)}, u32[]{:S(2)}, u32[]{:S(2)}) collective-permute-start(bf16[840,128]{1,0:T(8,128)(2,1)S(1)} %get-tuple-element.33), channel_id=1, source_target_pairs={{8,0},{16,8},{24,16},{32,24},{40,32},{48,40},{56,48},{64,56},{72,6... | collective-permute-start | bytes 645128 | tf_op jit(solution)/shard_map/ppermute | solution.py:585
  9.0 13.6 %copy-start.7 = (f32[32]{0:T(128)S(1)}, f32[32]{0:T(128)}, u32[]{:S(2)}) copy-start(f32[32]{0:T(128)} %param.16) | copy-start | bytes 388
  15.0 9.0 %collective-permute-start.5 = (bf16[1120,128]{1,0:T(8,128)(2,1)S(1)}, bf16[1120,128]{1,0:T(8,128)(2,1)S(1)}, u32[]{:S(2)}, u32[]{:S(2)}) collective-permute-start(bf16[1120,128]{1,0:T(8,128)(2,1)S(1)} %get-tuple-element.50), channel_id=1, source_target_pairs={{0,1},{1,0},{2,3},{3,2},{4,5},{5,4},{6,7},{7,6},{8,9},{9,8},{10,11... | collective-permute-start | bytes 860168 | tf_op jit(solution)/shard_map/ppermute | solution.py:593
  16.8 7.1 %collective-permute-start.4 = (bf16[840,128]{1,0:T(8,128)(2,1)S(1)}, bf16[840,128]{1,0:T(8,128)(2,1)S(1)}, u32[]{:S(2)}, u32[]{:S(2)}) collective-permute-start(bf16[840,128]{1,0:T(8,128)(2,1)S(1)} %get-tuple-element.49), channel_id=1, source_target_pairs={{0,1},{1,0},{2,3},{3,2},{4,5},{5,4},{6,7},{7,6},{8,9},{9,8},{10,11... | collective-permute-start | bytes 645128 | tf_op jit(solution)/shard_map/ppermute | solution.py:593
  16.9 10.8 %collective-permute-start = (bf16[840,128]{1,0:T(8,128)(2,1)S(1)}, bf16[840,128]{1,0:T(8,128)(2,1)S(1)}, u32[]{:S(2)}, u32[]{:S(2)}) collective-permute-start(bf16[840,128]{1,0:T(8,128)(2,1)S(1)} %get-tuple-element.31), channel_id=1, source_target_pairs={{1,2},{2,1},{3,4},{4,3},{5,6},{6,5},{9,10},{10,9},{11,12},{12,11},... | collective-permute-start | bytes 645128 | tf_op jit(solution)/shard_map/ppermute | solution.py:593
  20.4 8.0 %collective-permute-start.3 = (bf16[1120,128]{1,0:T(8,128)(2,1)S(1)}, bf16[1120,128]{1,0:T(8,128)(2,1)S(1)}, u32[]{:S(2)}, u32[]{:S(2)}) collective-permute-start(bf16[1120,128]{1,0:T(8,128)(2,1)S(1)} %get-tuple-element.35), channel_id=1, source_target_pairs={{1,2},{2,1},{3,4},{4,3},{5,6},{6,5},{9,10},{10,9},{11,12},{12,11},... | collective-permute-start | bytes 860168 | tf_op jit(solution)/shard_map/ppermute | solution.py:593
  22.5 1.4 %copy-start.5 = (s32[8,8,80]{2,1,0:T(8,128)S(1)}, s32[8,8,80]{2,1,0:T(8,128)}, u32[]{:S(2)}) copy-start(s32[8,8,80]{2,1,0:T(8,128)} %refs_8_.3) | copy-start | bytes 61444
  22.5 1.4 %copy-start.6 = (bf16[32,128]{1,0:T(8,128)(2,1)S(1)}, bf16[32,128]{1,0:T(8,128)(2,1)}, u32[]{:S(2)}) copy-start(bf16[32,128]{1,0:T(8,128)(2,1)} %refs_7_.3) | copy-start | bytes 24580
  22.6 1.4 %copy-start.8 = (f32[128]{0:T(128)S(1)}, f32[128]{0:T(128)}, u32[]{:S(2)}) copy-start(f32[128]{0:T(128)} %param.20) | copy-start | bytes 1540
  22.6 1.4 %copy-start.9 = (f32[32]{0:T(128)S(1)}, f32[32]{0:T(128)}, u32[]{:S(2)}) copy-start(f32[32]{0:T(128)} %param.23) | copy-start | bytes 388

commit v9 on v7

--- a/solution.py
+++ b/solution.py
@@ -431,7 +431,7 @@
     return nn(beside(*lhs), wd_ref[...])
 
 
-def decode_finish(o, xo, bd, perm, back, m_ref, out_ref, at):
+def decode_finish(o, xo, bd, perm, back, m_ref, out_ref, at, send=None):
     z4 = depth_of(160)
     first, last = z4 == 0, z4 == ZC - 1
     d0 = o[:, 0:128] + moved(o[:, 256:384], 1, first) + bd
@@ -443,6 +443,8 @@
     for a in BITS:
         t = jnp.transpose(d[:, 256 * a : 256 * a + 256])[:, :Z].reshape(CH, 8, Z)
         out_ref[:, at + a] = jnp.where(m_ref[2 * xo + a][None] > 0, t, 0.0).astype(BF16)
+        if send is not None:
+            send(at + a, 2 * xo + a)
 
 
 def own_kernel(
@@ -551,7 +553,7 @@
     a_ref, v_ref, e_ref, ev_ref, c_ref, d_ref, o_ref, k_ref, u_ref, out_ref, sems = refs[26:]
     left = right_ref[0]
     right = 1 - left
-    copies = [pltpu.make_async_copy(near_done_ref, out_hbm.at[:, pl.ds(6 * left, 2)], sems.at[3])]
+    copies = [pltpu.make_async_copy(near_done_ref, out_hbm.at[:, pl.ds(6 * left, 2)], sems.at[6])]
     copies[0].start()
     a, v, e, ev, c, d, o = own_planes(right, own)
     a, v, c, d, o = (x + [r.at[i] for i in range(3)] for x, r in zip((a, v, c, d, o), (a_ref, v_ref, c_ref, d_ref, o_ref)))
@@ -560,12 +562,14 @@
     u = [u1_ref.at[1], u1_ref.at[0]] + [u_ref.at[i] for i in range(3)]
     load_far(middle_ref, flanks_ref, a[2:], v[2:], k_ref)
 
+    def send(source, place):
+        copies.append(
+            pltpu.make_async_copy(out_ref.at[:, pl.ds(source, 1)], out_hbm.at[:, pl.ds(place, 1)], sems.at[source])
+        )
+        copies[-1].start()
+
     def emit(i, dot, bd, perm, back, m_ref):
-        xo = far_place(right, i)
-        at = pl.ds(2 * i, 2)
-        decode_finish(dot, xo, bd, perm, back, m_ref, out_ref, 2 * i)
-        copies.append(pltpu.make_async_copy(out_ref.at[:, at], out_hbm.at[:, pl.ds(2 * xo, 2)], sems.at[i]))
-        copies[-1].start()
+        decode_finish(dot, far_place(right, i), bd, perm, back, m_ref, out_ref, 2 * i, send)
 
     w = Stages(right, weights, misc, (a, v, e, ev, c, d, o, u), k_ref, own[7], emit)
     e0 = w.e_dot(0)
@@ -734,7 +738,7 @@
         [array(*fine_in.shape)],
         SCALAR + vmem(27),
         hbm(1),
-        buffers(state((3,), (3,), (2,)) + [((3,) + LIFTED, BF16)]) + [rest, pltpu.SemaphoreType.DMA((4,))],
+        buffers(state((3,), (3,), (2,)) + [((3,) + LIFTED, BF16)]) + [rest, pltpu.SemaphoreType.DMA((7,))],
         24,
         5 * 10**9,
     )(near_right, middle, flanks, *some, near_done, e1, ev1, u1)[0]

time: 33 us -> 33.1 us (level)
  no operation moved by 1% of the time
where the time goes in v9:
time: 33.1 us; the launch traced here: 32.9 us
  Pallas kernels  14.2 us (43%)
  starting transfers between devices  12.9 us (39%)
  waiting for transfers between devices  4.51 us (14%)
  between operations  0.88 us (3%)
    ppermute x3, starting transfers between devices, swapped(): return lax.ppermute(value, axis, pairs)  7.28 us
    ppermute x2, starting transfers between devices, shifted(): lax.ppermute(value, axis, [(i, i + step) for i in range(peers) if 0 <= i...  5.67 us
    pallas_call x1, Pallas kernels, on_device(): call(far_kernel, [array(*fine_in.shape)], SCALAR + vmem(27), hbm(1), buff...  5.01 us
    ppermute x2, waiting for transfers between devices, shifted(): lax.ppermute(value, axis, [(i, i + step) for i in range(peers) if 0 <= i...  4.39 us
    pallas_call x1, Pallas kernels, on_device(): call(near_kernel, [pair] + arrays(state((), (), ())[2:4] + [((2,) + LIFTE...  3.79 us
    pallas_call x1, Pallas kernels, on_device(): call(pack_kernel, [array(OWN + ZC, LANES), array(SIDE_ROWS, LANES), array...  2.31 us
    pallas_call x1, Pallas kernels, on_device(): call(weights_kernel, [array(1024, 512), array(1536, 512), array(128, 256)...  1.49 us
    pallas_call x1, Pallas kernels, on_device(): call(own_kernel, arrays(state((4,), (2,), (2,))), vmem(8), vmem(8), [], 1...  1.37 us
  transfers between devices with their start and end apart: 5, of which 3 were waited for; matrix products, arithmetic and copies ran while one was open for 1% of the time, Pallas kernels for 21%

profile of v9, /device:TPU:1, one launch (start us, length us, event | category | flops | bytes accessed | tf_op | source)
XLA Modules:
  0.0 32.9 jit_solution(13933983641465011692)
XLA Ops:
  0.0 2.3 %shard_map.118 = (bf16[1320,128]{1,0:T(8,128)(2,1)S(1)}, bf16[840,128]{1,0:T(8,128)(2,1)S(1)}, bf16[840,128]{1,0:T(8,128)(2,1)S(1)}) custom-call(bf16[32,8,8,80]{3,2,1,0:T(8,128)(2,1)} %x_hbm.1, s32[8,8,80]{2,1,0:T(8,128)} %refs_8_.3), custom_call_target="tpu_custom_call" | custom-call | flops 1000000000 | bytes 1000000 | tf_op jit(solution)/shard_map/pallas_call | solution.py:674
  2.4 4.4 %collective-permute-start.1 = (bf16[840,128]{1,0:T(8,128)(2,1)S(1)}, bf16[840,128]{1,0:T(8,128)(2,1)S(1)}, u32[]{:S(2)}, u32[]{:S(2)}) collective-permute-start(bf16[840,128]{1,0:T(8,128)(2,1)S(1)} %get-tuple-element.29), channel_id=1, source_target_pairs={{0,8},{8,16},{16,24},{24,32},{32,40},{40,48},{48,56},{56,64},{64,7... | collective-permute-start | bytes 645128 | tf_op jit(solution)/shard_map/ppermute | solution.py:630
  6.7 1.3 %collective-permute-start.2 = (bf16[840,128]{1,0:T(8,128)(2,1)S(1)}, bf16[840,128]{1,0:T(8,128)(2,1)S(1)}, u32[]{:S(2)}, u32[]{:S(2)}) collective-permute-start(bf16[840,128]{1,0:T(8,128)(2,1)S(1)} %get-tuple-element.30), channel_id=1, source_target_pairs={{8,0},{16,8},{24,16},{32,24},{40,32},{48,40},{56,48},{64,56},{72,6... | collective-permute-start | bytes 645128 | tf_op jit(solution)/shard_map/ppermute | solution.py:630
  8.7 0.1 cosine_convert_fusion
  8.8 0.2 fusion
  9.0 0.0 copy-start.7
  9.0 1.5 %shard_map.120 = (bf16[1024,512]{1,0:T(8,128)(2,1)S(1)}, bf16[1536,512]{1,0:T(8,128)(2,1)S(1)}, bf16[128,256]{1,0:T(8,128)(2,1)S(1)}, bf16[512,512]{1,0:T(8,128)...) custom-call(bf16[27,32,32]{2,1,0:T(8,128)(2,1)S(1)} %copy-done.2, ...), custom_call_target="tpu_custom_call" | custom-call | flops 4000000000 | bytes 1000000 | tf_op jit(solution)/shard_map/pallas_call | solution.py:697
  10.5 0.2 collective-permute-done.1.low_ref
  10.7 4.2 %collective-permute-done.2.high_ref = bf16[840,128]{1,0:T(8,128)(2,1)S(1)} collective-permute-done((bf16[840,128]{1,0:T(8,128)(2,1)S(1)}, bf16[840,128]{1,0:T(8,128)(2,1)S(1)}, u32[]{:S(2)}, u32[]{:S(2)}) %collective-permute-start.2) | collective-permute-done | bytes 215072 | tf_op jit(solution)/shard_map/ppermute | solution.py:630
  14.9 0.2 shard_map.121
  15.0 1.7 %collective-permute-start.4 = (bf16[1960,128]{1,0:T(8,128)(2,1)S(1)}, bf16[1960,128]{1,0:T(8,128)(2,1)S(1)}, u32[]{:S(2)}, u32[]{:S(2)}) collective-permute-start(bf16[1960,128]{1,0:T(8,128)(2,1)S(1)} %get-tuple-element.46), channel_id=1, source_target_pairs={{0,1},{1,0},{2,3},{3,2},{4,5},{5,4},{6,7},{7,6},{8,9},{9,8},{10,11... | collective-permute-start | bytes 1505288 | tf_op jit(solution)/shard_map/ppermute | solution.py:638
  16.8 0.1 shard_map.119
  16.8 3.0 %collective-permute-start = (bf16[840,128]{1,0:T(8,128)(2,1)S(1)}, bf16[840,128]{1,0:T(8,128)(2,1)S(1)}, u32[]{:S(2)}, u32[]{:S(2)}) collective-permute-start(bf16[840,128]{1,0:T(8,128)(2,1)S(1)} %shard_map.119), channel_id=1, source_target_pairs={{1,2},{2,1},{3,4},{4,3},{5,6},{6,5},{9,10},{10,9},{11,12},{12,11},... | collective-permute-start | bytes 645128 | tf_op jit(solution)/shard_map/ppermute | solution.py:638
  19.9 2.5 %collective-permute-start.3 = (bf16[1120,128]{1,0:T(8,128)(2,1)S(1)}, bf16[1120,128]{1,0:T(8,128)(2,1)S(1)}, u32[]{:S(2)}, u32[]{:S(2)}) collective-permute-start(bf16[1120,128]{1,0:T(8,128)(2,1)S(1)} %get-tuple-element.32), channel_id=1, source_target_pairs={{1,2},{2,1},{3,4},{4,3},{5,6},{6,5},{9,10},{10,9},{11,12},{12,11},... | collective-permute-start | bytes 860168 | tf_op jit(solution)/shard_map/ppermute | solution.py:638
  22.4 0.0 copy-start.5
  22.4 0.0 copy-start.6
  22.5 0.0 copy-start.8
  22.5 0.0 copy-start.9
  22.5 1.4 %shard_map.122 = (bf16[4,2,320,128]{3,2,1,0:T(8,128)(2,1)S(1)}, bf16[4,2,320,128]{3,2,1,0:T(8,128)(2,1)S(1)}, bf16[2,2,320,128]{3,2,1,0:T(8,128)(2,1)S(1)}, bf16...) custom-call(bf16[1320,128]{1,0:T(8,128)(2,1)S(1)} %get-tuple-element, ...), custom_call_target="tpu_custom_call" | custom-call | flops 2000000000 | bytes 1000000 | tf_op jit(solution)/shard_map/pallas_call | solution.py:721
  23.9 0.0 collective-permute-done.4.side_ref
  23.9 3.8 %shard_map.123 = (bf16[32,2,8,80]{3,2,1,0:T(8,128)(2,1)S(1)}, bf16[2,320,128]{2,1,0:T(8,128)(2,1)S(1)}, bf16[2,192,128]{2,1,0:T(8,128)(2,1)S(1)}, bf16[2,2,192,128]{3,2,1,0:T(8,128)(2,1)S(1)}) custom-call(s32[1]{0:T(128)S(6)} %sub.3.right_ref, bf16[1960,128]{1,0:T(8,128)(2,1)S(1)} %collective-permute-done.4.side_ref, ...), custom_call_target="tpu_custom_call" | custom-call | flops 4000000000 | bytes 1000000 | tf_op jit(solution)/shard_map/pallas_call | solution.py:726
  27.7 0.0 collective-permute-done.middle_ref
  27.7 0.1 collective-permute-done.3.flanks_ref
  27.8 5.0 %shard_map.124 = bf16[32,8,8,80]{3,2,1,0:T(8,128)(2,1)} custom-call(s32[1]{0:T(128)S(6)} %sub.3.right_ref, bf16[840,128]{1,0:T(8,128)(2,1)S(1)} %collective-permute-done.middle_ref, bf16[1120,128]{1,0:T(8,128)(2,1)S(1)} %collective-permute-done.3.flanks_ref, bf16[1024,512]{1,0:T(8,128)(2,1)S(1)} %get-tuple-element.33.we_ref.refs_0_, f32[1,32]{1,0:T(1,128)S(1)} %bitcast.12, ...), custom_call_target="tpu_custom_call" | custom-call | flops 5000000000 | bytes 1000000 | tf_op jit(solution)/shard_map/pallas_call | solution.py:736
  (16 shorter events, 0.0 us)
Async XLA Ops:
  0.0 8.7 %copy-start = (bf16[128,256]{1,0:T(8,128)(2,1)S(1)}, bf16[128,256]{1,0:T(8,128)(2,1)}, u32[]{:S(2)}) copy-start(bf16[128,256]{1,0:T(8,128)(2,1)} %param.18) | copy-start | bytes 196612
  0.0 8.9 %copy-start.2 = (bf16[27,32,32]{2,1,0:T(8,128)(2,1)S(1)}, bf16[27,32,32]{2,1,0:T(8,128)(2,1)}, u32[]{:S(2)}) copy-start(bf16[27,32,32]{2,1,0:T(8,128)(2,1)} %we_ref.1) | copy-start | bytes 165892
  0.0 8.9 %copy-start.4 = (bf16[128,256]{1,0:T(8,128)(2,1)S(1)}, bf16[128,256]{1,0:T(8,128)(2,1)}, u32[]{:S(2)}) copy-start(bf16[128,256]{1,0:T(8,128)(2,1)} %wn_ref.1) | copy-start | bytes 196612
  0.0 8.9 %copy-start.1 = (bf16[27,128,128]{2,1,0:T(8,128)(2,1)S(1)}, bf16[27,128,128]{2,1,0:T(8,128)(2,1)}, u32[]{:S(2)}) copy-start(bf16[27,128,128]{2,1,0:T(8,128)(2,1)} %wc_ref.1) | copy-start | bytes 2654212
  0.0 8.9 %copy-start.3 = (bf16[27,32,64]{2,1,0:T(8,128)(2,1)S(1)}, bf16[27,32,64]{2,1,0:T(8,128)(2,1)}, u32[]{:S(2)}) copy-start(bf16[27,32,64]{2,1,0:T(8,128)(2,1)} %wd_ref.1) | copy-start | bytes 331780
  2.4 8.3 %collective-permute-start.1 = (bf16[840,128]{1,0:T(8,128)(2,1)S(1)}, bf16[840,128]{1,0:T(8,128)(2,1)S(1)}, u32[]{:S(2)}, u32[]{:S(2)}) collective-permute-start(bf16[840,128]{1,0:T(8,128)(2,1)S(1)} %get-tuple-element.29), channel_id=1, source_target_pairs={{0,8},{8,16},{16,24},{24,32},{32,40},{40,48},{48,56},{56,64},{64,7... | collective-permute-start | bytes 645128 | tf_op jit(solution)/shard_map/ppermute | solution.py:630
  6.7 8.1 %collective-permute-start.2 = (bf16[840,128]{1,0:T(8,128)(2,1)S(1)}, bf16[840,128]{1,0:T(8,128)(2,1)S(1)}, u32[]{:S(2)}, u32[]{:S(2)}) collective-permute-start(bf16[840,128]{1,0:T(8,128)(2,1)S(1)} %get-tuple-element.30), channel_id=1, source_target_pairs={{8,0},{16,8},{24,16},{32,24},{40,32},{48,40},{56,48},{64,56},{72,6... | collective-permute-start | bytes 645128 | tf_op jit(solution)/shard_map/ppermute | solution.py:630
  9.0 13.5 %copy-start.7 = (f32[32]{0:T(128)S(1)}, f32[32]{0:T(128)}, u32[]{:S(2)}) copy-start(f32[32]{0:T(128)} %param.16) | copy-start | bytes 388
  15.0 8.8 %collective-permute-start.4 = (bf16[1960,128]{1,0:T(8,128)(2,1)S(1)}, bf16[1960,128]{1,0:T(8,128)(2,1)S(1)}, u32[]{:S(2)}, u32[]{:S(2)}) collective-permute-start(bf16[1960,128]{1,0:T(8,128)(2,1)S(1)} %get-tuple-element.46), channel_id=1, source_target_pairs={{0,1},{1,0},{2,3},{3,2},{4,5},{5,4},{6,7},{7,6},{8,9},{9,8},{10,11... | collective-permute-start | bytes 1505288 | tf_op jit(solution)/shard_map/ppermute | solution.py:638
  16.8 10.9 %collective-permute-start = (bf16[840,128]{1,0:T(8,128)(2,1)S(1)}, bf16[840,128]{1,0:T(8,128)(2,1)S(1)}, u32[]{:S(2)}, u32[]{:S(2)}) collective-permute-start(bf16[840,128]{1,0:T(8,128)(2,1)S(1)} %shard_map.119), channel_id=1, source_target_pairs={{1,2},{2,1},{3,4},{4,3},{5,6},{6,5},{9,10},{10,9},{11,12},{12,11},... | collective-permute-start | bytes 645128 | tf_op jit(solution)/shard_map/ppermute | solution.py:638
  19.9 8.0 %collective-permute-start.3 = (bf16[1120,128]{1,0:T(8,128)(2,1)S(1)}, bf16[1120,128]{1,0:T(8,128)(2,1)S(1)}, u32[]{:S(2)}, u32[]{:S(2)}) collective-permute-start(bf16[1120,128]{1,0:T(8,128)(2,1)S(1)} %get-tuple-element.32), channel_id=1, source_target_pairs={{1,2},{2,1},{3,4},{4,3},{5,6},{6,5},{9,10},{10,9},{11,12},{12,11},... | collective-permute-start | bytes 860168 | tf_op jit(solution)/shard_map/ppermute | solution.py:638
  22.4 1.4 %copy-start.5 = (s32[8,8,80]{2,1,0:T(8,128)S(1)}, s32[8,8,80]{2,1,0:T(8,128)}, u32[]{:S(2)}) copy-start(s32[8,8,80]{2,1,0:T(8,128)} %refs_8_.3) | copy-start | bytes 61444
  22.4 1.4 %copy-start.6 = (bf16[32,128]{1,0:T(8,128)(2,1)S(1)}, bf16[32,128]{1,0:T(8,128)(2,1)}, u32[]{:S(2)}) copy-start(bf16[32,128]{1,0:T(8,128)(2,1)} %refs_7_.3) | copy-start | bytes 24580
  22.5 1.4 %copy-start.8 = (f32[128]{0:T(128)S(1)}, f32[128]{0:T(128)}, u32[]{:S(2)}) copy-start(f32[128]{0:T(128)} %param.20) | copy-start | bytes 1540
  22.5 1.4 %copy-start.9 = (f32[32]{0:T(128)S(1)}, f32[32]{0:T(128)}, u32[]{:S(2)}) copy-start(f32[32]{0:T(128)} %param.23) | copy-start | bytes 388

commit v10 on v9

--- a/solution.py
+++ b/solution.py
@@ -183,11 +183,13 @@
     return in_bit - out_bit + 1
 
 
-def placed(w_ref, rows, taps, group):
-    total = jnp.zeros((CH, LANES), F32)
+def placed(w_ref, rows, taps, masks):
+    full = None not in taps
+    total = None if full else jnp.zeros((CH, LANES), BF16)
     for g, tap in enumerate(taps):
         if tap is not None:
-            total = jnp.where(group == g, w_ref[rows : rows + CH, LANES * tap : LANES * tap + LANES], total)
+            value = w_ref[rows : rows + CH, LANES * tap : LANES * tap + LANES]
+            total = value if total is None else jnp.where(masks[g], value, total)
     return total
 
 
@@ -213,21 +215,28 @@
 
 
 def weights_kernel(
-    we_ref, wd_ref, wn_ref, wc_ref, oe_ref, od_ref, on_ref, op_ref, ob_ref, oc_ref, re_ref, rd_ref, te_ref, td_ref
+    time_ref, wt_ref, we_ref, wd_ref, wn_ref, wc_ref, og_ref, os_ref, oe_ref, od_ref, on_ref, op_ref, ob_ref, oc_ref,
+    re_ref, rd_ref, te_ref, td_ref
 ):
+    lane = iota((16, LANES), 1)
+    angles = time_ref[...].astype(F32) * jnp.exp(-math.log(10000.0) * (lane & 63).astype(F32) / 64.0)
+    embedded = jnp.where(lane < 64, jnp.sin(angles), jnp.cos(angles)).astype(BF16)
+    film = nn(embedded, wt_ref[...])
+    og_ref[...] = 1.0 + film[0:1, :LANES]
+    os_ref[...] = film[0:1, LANES:]
     for tap in range(27):
         for g in range(4):
             at = LANES * tap + CH * g
             re_ref[at : at + CH] = we_ref[tap]
             rd_ref[at : at + CH] = wd_ref[tap]
     one = (iota((CH, CH), 0) == iota((CH, CH), 1)).astype(F32).astype(BF16)
-    te_ref[...] = nt(one, re_ref[...])
+    te_ref[...] = nt(one, re_ref[...]).astype(BF16)
     one = (iota((2 * CH, 2 * CH), 0) == iota((2 * CH, 2 * CH), 1)).astype(F32).astype(BF16)
-    td_ref[...] = nt(one, rd_ref[...])
+    td_ref[...] = nt(one, rd_ref[...]).astype(BF16)
     one = one_where(iota((LANES, LANES), 0) == iota((LANES, LANES), 1))
     for i in range(9):
         oc_ref[LANES * i : LANES * i + LANES] = nt(one, wc_ref[3 * i : 3 * i + 3].reshape(384, LANES)).astype(BF16)
-    group = iota((CH, LANES), 1) >> 5
+    group = [one_where((iota((CH, LANES), 1) >> 5) == g) > 0.5 for g in range(4)]
     for w_ref, o_ref in ((te_ref, oe_ref), (td_ref, od_ref)):
         for t, (fx, fy) in enumerate(KINDS):
             for cz in BITS:
@@ -237,15 +246,15 @@
                         for s in BITS:
                             for co in BITS:
                                 v = block(w_ref, 0, group, fx, fy, a, b, cz, s, co)
-                                o_ref[base : base + CH, 256 * s + 128 * co : 256 * s + 128 * co + LANES] = v.astype(BF16)
+                                o_ref[base : base + CH, 256 * s + 128 * co : 256 * s + 128 * co + LANES] = v
     for t, (fx, fy) in enumerate(KINDS):
         for a in BITS:
             for b in BITS:
                 base = 1024 + 128 * t + 64 * a + 32 * b
                 for s in BITS:
                     for co in BITS:
-                        v = block(td_ref, CH, group, fx, fy, a, b, 0, s, co)
-                        v = v + block(td_ref, CH, group, fx, fy, a, b, 1, s, co)
+                        v = block(td_ref, CH, group, fx, fy, a, b, 0, s, co).astype(F32)
+                        v = v + block(td_ref, CH, group, fx, fy, a, b, 1, s, co).astype(F32)
                         od_ref[base : base + CH, 256 * s + 128 * co : 256 * s + 128 * co + LANES] = v.astype(BF16)
     k = iota((8 * CH, LANES), 0)
     goal = (((k >> 5) & 1) << 7) + ((k >> 6) << 5) + (k & 31) - iota((8 * CH, LANES), 1)
@@ -638,13 +647,6 @@
     return lax.ppermute(value, axis, pairs)
 
 
-def time_features(timestep, embed_width):
-    halves = embed_width // 2
-    freqs = jnp.exp(-math.log(10000.0) * jnp.arange(halves, dtype=F32) / halves)
-    angles = timestep[0].astype(F32) * freqs
-    return jnp.concatenate([jnp.sin(angles), jnp.cos(angles)]).astype(BF16)
-
-
 SCALAR = [pl.BlockSpec(memory_space=pltpu.SMEM)]
 
 
@@ -688,22 +690,18 @@
     middle = call(edge_kernel, [array(MIDDLE + ZC, LANES)], SCALAR + vmem(1), vmem(1), [], 8, 10**8)(odd, own)[0]
     middle = swapped(middle, "narrow", 1)
 
-    embedded = time_features(timestep, w_time.shape[0])
-    film = jnp.dot(embedded[None], w_time, preferred_element_type=F32)
-    chans = w_down.shape[0]
-    gains = 1.0 + film[:, :chans]
-    shifts = film[:, chans:]
     taps = 27 * LANES
-    enc_w, dec_w, down_w, perm, back, coarse_w = call(
+    gains, shifts, enc_w, dec_w, down_w, perm, back, coarse_w = call(
         weights_kernel,
-        [array(1024, 512), array(1536, 512), array(128, 256), array(512, 512), array(Z, LANES)]
+        [array(1, LANES, kind=F32), array(1, LANES, kind=F32)]
+        + [array(1024, 512), array(1536, 512), array(128, 256), array(512, 512), array(Z, LANES)]
         + [array(9 * LANES, 384)],
-        vmem(4),
         vmem(6),
-        buffers([((taps, 32), BF16), ((taps, 64), BF16), ((32, taps), F32), ((64, taps), F32)]),
+        vmem(8),
+        buffers([((taps, 32), BF16), ((taps, 64), BF16), ((32, taps), BF16), ((64, taps), BF16)]),
         16,
         4 * 10**9,
-    )(w_enc, w_dec, w_down, w_coarse)
+    )(timestep[None], w_time, w_enc, w_dec, w_down, w_coarse)
 
     flanks, near = call(
         mid_kernel,

time: 33.1 us -> 33.1 us (level)
  transfers between devices with their start and end apart: 5 -> 5, of which waited for: 3 -> 2; matrix products, arithmetic and copies ran while one was open for 1% -> 0% of each run, Pallas kernels for 21% -> 21%
where the time goes in v10:
time: 33.1 us; the launch traced here: 32.9 us
  Pallas kernels  14.3 us (43%)
  starting transfers between devices  12.9 us (39%)
  waiting for transfers between devices  4.73 us (14%)
  between operations  0.88 us (3%)
    ppermute x3, starting transfers between devices, swapped(): return lax.ppermute(value, axis, pairs)  7.28 us
    ppermute x2, starting transfers between devices, shifted(): lax.ppermute(value, axis, [(i, i + step) for i in range(peers) if 0 <= i...  5.67 us
    pallas_call x1, Pallas kernels, on_device(): call(far_kernel, [array(*fine_in.shape)], SCALAR + vmem(27), hbm(1), buff...  5.07 us
    ppermute x2, waiting for transfers between devices, shifted(): lax.ppermute(value, axis, [(i, i + step) for i in range(peers) if 0 <= i...  4.68 us
    pallas_call x1, Pallas kernels, on_device(): call(near_kernel, [pair] + arrays(state((), (), ())[2:4] + [((2,) + LIFTE...  3.84 us
    pallas_call x1, Pallas kernels, on_device(): call(pack_kernel, [array(OWN + ZC, LANES), array(SIDE_ROWS, LANES), array...  2.31 us
    pallas_call x1, Pallas kernels, on_device(): call(weights_kernel, [array(1, LANES, kind=F32), array(1, LANES, kind=F32...  1.43 us
    pallas_call x1, Pallas kernels, on_device(): call(own_kernel, arrays(state((4,), (2,), (2,))), vmem(8), vmem(8), [], 1...  1.39 us
  transfers between devices with their start and end apart: 5, of which 2 were waited for; matrix products, arithmetic and copies ran while one was open for 0% of the time, Pallas kernels for 21%

profile of v10, /device:TPU:1, one launch (start us, length us, event | category | flops | bytes accessed | tf_op | source)
XLA Modules:
  0.0 32.9 jit_solution(12421464484362774622)
XLA Ops:
  0.0 0.0 copy-start
  0.0 0.0 copy-start.2
  0.0 2.3 %shard_map.118 = (bf16[1320,128]{1,0:T(8,128)(2,1)S(1)}, bf16[840,128]{1,0:T(8,128)(2,1)S(1)}, bf16[840,128]{1,0:T(8,128)(2,1)S(1)}) custom-call(bf16[32,8,8,80]{3,2,1,0:T(8,128)(2,1)} %x_hbm.1, s32[8,8,80]{2,1,0:T(8,128)} %refs_8_.3), custom_call_target="tpu_custom_call" | custom-call | flops 1000000000 | bytes 1000000 | tf_op jit(solution)/shard_map/pallas_call | solution.py:676
  2.3 4.4 %collective-permute-start.1 = (bf16[840,128]{1,0:T(8,128)(2,1)S(1)}, bf16[840,128]{1,0:T(8,128)(2,1)S(1)}, u32[]{:S(2)}, u32[]{:S(2)}) collective-permute-start(bf16[840,128]{1,0:T(8,128)(2,1)S(1)} %get-tuple-element.31), channel_id=1, source_target_pairs={{0,8},{8,16},{16,24},{24,32},{32,40},{40,48},{48,56},{56,64},{64,7... | collective-permute-start | bytes 645128 | tf_op jit(solution)/shard_map/ppermute | solution.py:639
  6.7 1.3 %collective-permute-start.2 = (bf16[840,128]{1,0:T(8,128)(2,1)S(1)}, bf16[840,128]{1,0:T(8,128)(2,1)S(1)}, u32[]{:S(2)}, u32[]{:S(2)}) collective-permute-start(bf16[840,128]{1,0:T(8,128)(2,1)S(1)} %get-tuple-element.32), channel_id=1, source_target_pairs={{8,0},{16,8},{24,16},{32,24},{40,32},{48,40},{56,48},{64,56},{72,6... | collective-permute-start | bytes 645128 | tf_op jit(solution)/shard_map/ppermute | solution.py:639
  8.7 0.0 copy-start.7
  8.7 1.4 %shard_map.120 = (f32[1,128]{1,0:T(1,128)S(1)}, f32[1,128]{1,0:T(1,128)S(1)}, bf16[1024,512]{1,0:T(8,128)(2,1)S(1)}, bf16[1536,512]{1,0:T(8,128)(2,1)S(1)}, bf16...) custom-call(s32[1,1]{1,0:T(1,128)} %bitcast.5.time_ref, ...), custom_call_target="tpu_custom_call" | custom-call | flops 4000000000 | bytes 1000000 | tf_op jit(solution)/shard_map/pallas_call | solution.py:694
  10.2 0.5 %collective-permute-done.1.low_ref = bf16[840,128]{1,0:T(8,128)(2,1)S(1)} collective-permute-done((bf16[840,128]{1,0:T(8,128)(2,1)S(1)}, bf16[840,128]{1,0:T(8,128)(2,1)S(1)}, u32[]{:S(2)}, u32[]{:S(2)}) %collective-permute-start.1) | collective-permute-done | bytes 215072 | tf_op jit(solution)/shard_map/ppermute | solution.py:639
  10.7 4.2 %collective-permute-done.2.high_ref = bf16[840,128]{1,0:T(8,128)(2,1)S(1)} collective-permute-done((bf16[840,128]{1,0:T(8,128)(2,1)S(1)}, bf16[840,128]{1,0:T(8,128)(2,1)S(1)}, u32[]{:S(2)}, u32[]{:S(2)}) %collective-permute-start.2) | collective-permute-done | bytes 215072 | tf_op jit(solution)/shard_map/ppermute | solution.py:639
  14.9 0.2 shard_map.121
  15.0 1.7 %collective-permute-start.4 = (bf16[1960,128]{1,0:T(8,128)(2,1)S(1)}, bf16[1960,128]{1,0:T(8,128)(2,1)S(1)}, u32[]{:S(2)}, u32[]{:S(2)}) collective-permute-start(bf16[1960,128]{1,0:T(8,128)(2,1)S(1)} %get-tuple-element.50), channel_id=1, source_target_pairs={{0,1},{1,0},{2,3},{3,2},{4,5},{5,4},{6,7},{7,6},{8,9},{9,8},{10,11... | collective-permute-start | bytes 1505288 | tf_op jit(solution)/shard_map/ppermute | solution.py:647
  16.8 0.1 shard_map.119
  16.8 3.0 %collective-permute-start = (bf16[840,128]{1,0:T(8,128)(2,1)S(1)}, bf16[840,128]{1,0:T(8,128)(2,1)S(1)}, u32[]{:S(2)}, u32[]{:S(2)}) collective-permute-start(bf16[840,128]{1,0:T(8,128)(2,1)S(1)} %shard_map.119), channel_id=1, source_target_pairs={{1,2},{2,1},{3,4},{4,3},{5,6},{6,5},{9,10},{10,9},{11,12},{12,11},... | collective-permute-start | bytes 645128 | tf_op jit(solution)/shard_map/ppermute | solution.py:647
  19.9 2.5 %collective-permute-start.3 = (bf16[1120,128]{1,0:T(8,128)(2,1)S(1)}, bf16[1120,128]{1,0:T(8,128)(2,1)S(1)}, u32[]{:S(2)}, u32[]{:S(2)}) collective-permute-start(bf16[1120,128]{1,0:T(8,128)(2,1)S(1)} %get-tuple-element.35), channel_id=1, source_target_pairs={{1,2},{2,1},{3,4},{4,3},{5,6},{6,5},{9,10},{10,9},{11,12},{12,11},... | collective-permute-start | bytes 860168 | tf_op jit(solution)/shard_map/ppermute | solution.py:647
  22.4 0.0 copy-start.5
  22.4 0.0 copy-start.6
  22.5 0.0 copy-start.8
  22.5 0.0 copy-start.9
  22.5 1.4 %shard_map.122 = (bf16[4,2,320,128]{3,2,1,0:T(8,128)(2,1)S(1)}, bf16[4,2,320,128]{3,2,1,0:T(8,128)(2,1)S(1)}, bf16[2,2,320,128]{3,2,1,0:T(8,128)(2,1)S(1)}, bf16...) custom-call(bf16[1320,128]{1,0:T(8,128)(2,1)S(1)} %get-tuple-element, ...), custom_call_target="tpu_custom_call" | custom-call | flops 2000000000 | bytes 1000000 | tf_op jit(solution)/shard_map/pallas_call | solution.py:719
  23.9 0.0 collective-permute-done.4.side_ref
  23.9 3.8 %shard_map.123 = (bf16[32,2,8,80]{3,2,1,0:T(8,128)(2,1)S(1)}, bf16[2,320,128]{2,1,0:T(8,128)(2,1)S(1)}, bf16[2,192,128]{2,1,0:T(8,128)(2,1)S(1)}, bf16[2,2,192,128]{3,2,1,0:T(8,128)(2,1)S(1)}) custom-call(s32[1]{0:T(128)S(6)} %sub.3.right_ref, bf16[1960,128]{1,0:T(8,128)(2,1)S(1)} %collective-permute-done.4.side_ref, ...), custom_call_target="tpu_custom_call" | custom-call | flops 4000000000 | bytes 1000000 | tf_op jit(solution)/shard_map/pallas_call | solution.py:724
  27.8 0.0 collective-permute-done.middle_ref
  27.8 0.0 collective-permute-done.3.flanks_ref
  27.8 5.1 %shard_map.124 = bf16[32,8,8,80]{3,2,1,0:T(8,128)(2,1)} custom-call(s32[1]{0:T(128)S(6)} %sub.3.right_ref, bf16[840,128]{1,0:T(8,128)(2,1)S(1)} %collective-permute-done.middle_ref, bf16[1120,128]{1,0:T(8,128)(2,1)S(1)} %collective-permute-done.3.flanks_ref, bf16[1024,512]{1,0:T(8,128)(2,1)S(1)} %get-tuple-element.36.we_ref.refs_0_, f32[1,32]{1,0:T(1,128)S(1)} %bitcast.8, ...), custom_call_target="tpu_custom_call" | custom-call | flops 5000000000 | bytes 1000000 | tf_op jit(solution)/shard_map/pallas_call | solution.py:734
  (13 shorter events, 0.0 us)
Async XLA Ops:
  0.0 8.7 %copy-start.1 = (bf16[27,32,32]{2,1,0:T(8,128)(2,1)S(1)}, bf16[27,32,32]{2,1,0:T(8,128)(2,1)}, u32[]{:S(2)}) copy-start(bf16[27,32,32]{2,1,0:T(8,128)(2,1)} %we_ref.1) | copy-start | bytes 165892
  0.0 8.7 %copy-start.4 = (bf16[128,256]{1,0:T(8,128)(2,1)S(1)}, bf16[128,256]{1,0:T(8,128)(2,1)}, u32[]{:S(2)}) copy-start(bf16[128,256]{1,0:T(8,128)(2,1)} %wn_ref.1) | copy-start | bytes 196612
  0.0 8.7 %copy-start.3 = (bf16[128,256]{1,0:T(8,128)(2,1)S(1)}, bf16[128,256]{1,0:T(8,128)(2,1)}, u32[]{:S(2)}) copy-start(bf16[128,256]{1,0:T(8,128)(2,1)} %wt_ref.1) | copy-start | bytes 196612
  0.0 8.7 %copy-start = (bf16[27,128,128]{2,1,0:T(8,128)(2,1)S(1)}, bf16[27,128,128]{2,1,0:T(8,128)(2,1)}, u32[]{:S(2)}) copy-start(bf16[27,128,128]{2,1,0:T(8,128)(2,1)} %wc_ref.1) | copy-start | bytes 2654212
  0.0 8.7 %copy-start.2 = (bf16[27,32,64]{2,1,0:T(8,128)(2,1)S(1)}, bf16[27,32,64]{2,1,0:T(8,128)(2,1)}, u32[]{:S(2)}) copy-start(bf16[27,32,64]{2,1,0:T(8,128)(2,1)} %wd_ref.1) | copy-start | bytes 331780
  2.3 8.3 %collective-permute-start.1 = (bf16[840,128]{1,0:T(8,128)(2,1)S(1)}, bf16[840,128]{1,0:T(8,128)(2,1)S(1)}, u32[]{:S(2)}, u32[]{:S(2)}) collective-permute-start(bf16[840,128]{1,0:T(8,128)(2,1)S(1)} %get-tuple-element.31), channel_id=1, source_target_pairs={{0,8},{8,16},{16,24},{24,32},{32,40},{40,48},{48,56},{56,64},{64,7... | collective-permute-start | bytes 645128 | tf_op jit(solution)/shard_map/ppermute | solution.py:639
  6.7 8.1 %collective-permute-start.2 = (bf16[840,128]{1,0:T(8,128)(2,1)S(1)}, bf16[840,128]{1,0:T(8,128)(2,1)S(1)}, u32[]{:S(2)}, u32[]{:S(2)}) collective-permute-start(bf16[840,128]{1,0:T(8,128)(2,1)S(1)} %get-tuple-element.32), channel_id=1, source_target_pairs={{8,0},{16,8},{24,16},{32,24},{40,32},{48,40},{56,48},{64,56},{72,6... | collective-permute-start | bytes 645128 | tf_op jit(solution)/shard_map/ppermute | solution.py:639
  8.7 13.7 %copy-start.7 = (f32[32]{0:T(128)S(1)}, f32[32]{0:T(128)}, u32[]{:S(2)}) copy-start(f32[32]{0:T(128)} %param.16) | copy-start | bytes 388
  15.0 8.9 %collective-permute-start.4 = (bf16[1960,128]{1,0:T(8,128)(2,1)S(1)}, bf16[1960,128]{1,0:T(8,128)(2,1)S(1)}, u32[]{:S(2)}, u32[]{:S(2)}) collective-permute-start(bf16[1960,128]{1,0:T(8,128)(2,1)S(1)} %get-tuple-element.50), channel_id=1, source_target_pairs={{0,1},{1,0},{2,3},{3,2},{4,5},{5,4},{6,7},{7,6},{8,9},{9,8},{10,11... | collective-permute-start | bytes 1505288 | tf_op jit(solution)/shard_map/ppermute | solution.py:647
  16.8 10.9 %collective-permute-start = (bf16[840,128]{1,0:T(8,128)(2,1)S(1)}, bf16[840,128]{1,0:T(8,128)(2,1)S(1)}, u32[]{:S(2)}, u32[]{:S(2)}) collective-permute-start(bf16[840,128]{1,0:T(8,128)(2,1)S(1)} %shard_map.119), channel_id=1, source_target_pairs={{1,2},{2,1},{3,4},{4,3},{5,6},{6,5},{9,10},{10,9},{11,12},{12,11},... | collective-permute-start | bytes 645128 | tf_op jit(solution)/shard_map/ppermute | solution.py:647
  19.9 8.0 %collective-permute-start.3 = (bf16[1120,128]{1,0:T(8,128)(2,1)S(1)}, bf16[1120,128]{1,0:T(8,128)(2,1)S(1)}, u32[]{:S(2)}, u32[]{:S(2)}) collective-permute-start(bf16[1120,128]{1,0:T(8,128)(2,1)S(1)} %get-tuple-element.35), channel_id=1, source_target_pairs={{1,2},{2,1},{3,4},{4,3},{5,6},{6,5},{9,10},{10,9},{11,12},{12,11},... | collective-permute-start | bytes 860168 | tf_op jit(solution)/shard_map/ppermute | solution.py:647
  22.4 1.5 %copy-start.5 = (s32[8,8,80]{2,1,0:T(8,128)S(1)}, s32[8,8,80]{2,1,0:T(8,128)}, u32[]{:S(2)}) copy-start(s32[8,8,80]{2,1,0:T(8,128)} %refs_8_.3) | copy-start | bytes 61444
  22.4 1.5 %copy-start.6 = (bf16[32,128]{1,0:T(8,128)(2,1)S(1)}, bf16[32,128]{1,0:T(8,128)(2,1)}, u32[]{:S(2)}) copy-start(bf16[32,128]{1,0:T(8,128)(2,1)} %refs_7_.3) | copy-start | bytes 24580
  22.5 1.5 %copy-start.8 = (f32[128]{0:T(128)S(1)}, f32[128]{0:T(128)}, u32[]{:S(2)}) copy-start(f32[128]{0:T(128)} %param.20) | copy-start | bytes 1540
  22.5 1.5 %copy-start.9 = (f32[32]{0:T(128)S(1)}, f32[32]{0:T(128)}, u32[]{:S(2)}) copy-start(f32[32]{0:T(128)} %param.23) | copy-start | bytes 388

commit v11 on v10

--- a/solution.py
+++ b/solution.py
@@ -80,19 +80,23 @@
     own_ref[OWN : OWN + ZC] = cols
     up_ref[SIDE_MASK:SIDE_ROWS] = cols
     dn_ref[SIDE_MASK:SIDE_ROWS] = cols
-    sides = [[], []]
-    for cx in range(4):
-        copies[1 + cx].wait()
-        for a in BITS:
-            x = 2 * cx + a
-            tile = x_ref[:, x].astype(F32)
-            tile = jnp.where(m_ref[x][None] > 0, tile, 0.0)
-            sides[a].append(nt(sel, tile.reshape(8 * CH, Z).astype(BF16)).astype(BF16))
-    both = beside(stacked(*sides[0]), stacked(*sides[1]))
-    cols = [nn(both, perm[cy]) for cy in range(4)]
+    cols = [[] for _ in range(4)]
+    for pair in range(2):
+        sides = [[], []]
+        for cx in (2 * pair, 2 * pair + 1):
+            copies[1 + cx].wait()
+            for a in BITS:
+                x = 2 * cx + a
+                tile = x_ref[:, x].astype(F32)
+                tile = jnp.where(m_ref[x][None] > 0, tile, 0.0)
+                sides[a].append(nt(sel, tile.reshape(8 * CH, Z).astype(BF16)).astype(BF16))
+        both = beside(stacked(*sides[0]), stacked(*sides[1]))
+        for cy in range(4):
+            v = nn(both, perm[cy])
+            cols[cy] += [v[:Z], v[Z:]]
     ups, downs = [], []
     for cx in range(4):
-        col = [v[Z * cx : Z * cx + Z] for v in cols]
+        col = [v[cx] for v in cols]
         for cz in BITS:
             z = slice(ZC * cz, ZC * cz + ZC)
             first = stacked(col[0][z], col[1][z]).astype(BF16)

time: 33.1 us -> 33.2 us (level)
  transfers between devices with their start and end apart: 5 -> 5, of which waited for: 2 -> 2; matrix products, arithmetic and copies ran while one was open for 0% -> 0% of each run, Pallas kernels for 21% -> 20%
where the time goes in v11:
time: 33.2 us; the launch traced here: 33 us
  Pallas kernels  14.4 us (43%)
  starting transfers between devices  12.9 us (39%)
  waiting for transfers between devices  4.73 us (14%)
  between operations  0.88 us (3%)
    ppermute x3, starting transfers between devices, swapped(): return lax.ppermute(value, axis, pairs)  7.28 us
    ppermute x2, starting transfers between devices, shifted(): lax.ppermute(value, axis, [(i, i + step) for i in range(peers) if 0 <= i...  5.67 us
    pallas_call x1, Pallas kernels, on_device(): call(far_kernel, [array(*fine_in.shape)], SCALAR + vmem(27), hbm(1), buff...  5.06 us
    ppermute x2, waiting for transfers between devices, shifted(): lax.ppermute(value, axis, [(i, i + step) for i in range(peers) if 0 <= i...  4.69 us
    pallas_call x1, Pallas kernels, on_device(): call(near_kernel, [pair] + arrays(state((), (), ())[2:4] + [((2,) + LIFTE...  3.84 us
    pallas_call x1, Pallas kernels, on_device(): call(pack_kernel, [array(OWN + ZC, LANES), array(SIDE_ROWS, LANES), array...  2.44 us
    pallas_call x1, Pallas kernels, on_device(): call(weights_kernel, [array(1, LANES, kind=F32), array(1, LANES, kind=F32...  1.43 us
    pallas_call x1, Pallas kernels, on_device(): call(own_kernel, arrays(state((4,), (2,), (2,))), vmem(8), vmem(8), [], 1...  1.39 us
  transfers between devices with their start and end apart: 5, of which 2 were waited for; matrix products, arithmetic and copies ran while one was open for 0% of the time, Pallas kernels for 20%

profile of v11, /device:TPU:1, one launch (start us, length us, event | category | flops | bytes accessed | tf_op | source)
XLA Modules:
  0.0 33.0 jit_solution(17843747327298759913)
XLA Ops:
  0.0 0.0 copy-start
  0.0 0.0 copy-start.2
  0.0 2.4 %shard_map.118 = (bf16[1320,128]{1,0:T(8,128)(2,1)S(1)}, bf16[840,128]{1,0:T(8,128)(2,1)S(1)}, bf16[840,128]{1,0:T(8,128)(2,1)S(1)}) custom-call(bf16[32,8,8,80]{3,2,1,0:T(8,128)(2,1)} %x_hbm.1, s32[8,8,80]{2,1,0:T(8,128)} %refs_8_.3), custom_call_target="tpu_custom_call" | custom-call | flops 1000000000 | bytes 1000000 | tf_op jit(solution)/shard_map/pallas_call | solution.py:680
  2.5 4.4 %collective-permute-start.1 = (bf16[840,128]{1,0:T(8,128)(2,1)S(1)}, bf16[840,128]{1,0:T(8,128)(2,1)S(1)}, u32[]{:S(2)}, u32[]{:S(2)}) collective-permute-start(bf16[840,128]{1,0:T(8,128)(2,1)S(1)} %get-tuple-element.31), channel_id=1, source_target_pairs={{0,8},{8,16},{16,24},{24,32},{32,40},{40,48},{48,56},{56,64},{64,7... | collective-permute-start | bytes 645128 | tf_op jit(solution)/shard_map/ppermute | solution.py:643
  6.9 1.3 %collective-permute-start.2 = (bf16[840,128]{1,0:T(8,128)(2,1)S(1)}, bf16[840,128]{1,0:T(8,128)(2,1)S(1)}, u32[]{:S(2)}, u32[]{:S(2)}) collective-permute-start(bf16[840,128]{1,0:T(8,128)(2,1)S(1)} %get-tuple-element.32), channel_id=1, source_target_pairs={{8,0},{16,8},{24,16},{32,24},{40,32},{48,40},{56,48},{64,56},{72,6... | collective-permute-start | bytes 645128 | tf_op jit(solution)/shard_map/ppermute | solution.py:643
  8.9 0.0 copy-start.7
  8.9 1.4 %shard_map.120 = (f32[1,128]{1,0:T(1,128)S(1)}, f32[1,128]{1,0:T(1,128)S(1)}, bf16[1024,512]{1,0:T(8,128)(2,1)S(1)}, bf16[1536,512]{1,0:T(8,128)(2,1)S(1)}, bf16...) custom-call(s32[1,1]{1,0:T(1,128)} %bitcast.5.time_ref, ...), custom_call_target="tpu_custom_call" | custom-call | flops 4000000000 | bytes 1000000 | tf_op jit(solution)/shard_map/pallas_call | solution.py:698
  10.3 0.5 %collective-permute-done.1.low_ref = bf16[840,128]{1,0:T(8,128)(2,1)S(1)} collective-permute-done((bf16[840,128]{1,0:T(8,128)(2,1)S(1)}, bf16[840,128]{1,0:T(8,128)(2,1)S(1)}, u32[]{:S(2)}, u32[]{:S(2)}) %collective-permute-start.1) | collective-permute-done | bytes 215072 | tf_op jit(solution)/shard_map/ppermute | solution.py:643
  10.8 4.2 %collective-permute-done.2.high_ref = bf16[840,128]{1,0:T(8,128)(2,1)S(1)} collective-permute-done((bf16[840,128]{1,0:T(8,128)(2,1)S(1)}, bf16[840,128]{1,0:T(8,128)(2,1)S(1)}, u32[]{:S(2)}, u32[]{:S(2)}) %collective-permute-start.2) | collective-permute-done | bytes 215072 | tf_op jit(solution)/shard_map/ppermute | solution.py:643
  15.0 0.2 shard_map.121
  15.2 1.7 %collective-permute-start.4 = (bf16[1960,128]{1,0:T(8,128)(2,1)S(1)}, bf16[1960,128]{1,0:T(8,128)(2,1)S(1)}, u32[]{:S(2)}, u32[]{:S(2)}) collective-permute-start(bf16[1960,128]{1,0:T(8,128)(2,1)S(1)} %get-tuple-element.50), channel_id=1, source_target_pairs={{0,1},{1,0},{2,3},{3,2},{4,5},{5,4},{6,7},{7,6},{8,9},{9,8},{10,11... | collective-permute-start | bytes 1505288 | tf_op jit(solution)/shard_map/ppermute | solution.py:651
  16.9 0.1 shard_map.119
  17.0 3.0 %collective-permute-start = (bf16[840,128]{1,0:T(8,128)(2,1)S(1)}, bf16[840,128]{1,0:T(8,128)(2,1)S(1)}, u32[]{:S(2)}, u32[]{:S(2)}) collective-permute-start(bf16[840,128]{1,0:T(8,128)(2,1)S(1)} %shard_map.119), channel_id=1, source_target_pairs={{1,2},{2,1},{3,4},{4,3},{5,6},{6,5},{9,10},{10,9},{11,12},{12,11},... | collective-permute-start | bytes 645128 | tf_op jit(solution)/shard_map/ppermute | solution.py:651
  20.0 2.5 %collective-permute-start.3 = (bf16[1120,128]{1,0:T(8,128)(2,1)S(1)}, bf16[1120,128]{1,0:T(8,128)(2,1)S(1)}, u32[]{:S(2)}, u32[]{:S(2)}) collective-permute-start(bf16[1120,128]{1,0:T(8,128)(2,1)S(1)} %get-tuple-element.35), channel_id=1, source_target_pairs={{1,2},{2,1},{3,4},{4,3},{5,6},{6,5},{9,10},{10,9},{11,12},{12,11},... | collective-permute-start | bytes 860168 | tf_op jit(solution)/shard_map/ppermute | solution.py:651
  22.6 0.0 copy-start.5
  22.6 0.0 copy-start.6
  22.6 0.0 copy-start.8
  22.6 0.0 copy-start.9
  22.6 1.4 %shard_map.122 = (bf16[4,2,320,128]{3,2,1,0:T(8,128)(2,1)S(1)}, bf16[4,2,320,128]{3,2,1,0:T(8,128)(2,1)S(1)}, bf16[2,2,320,128]{3,2,1,0:T(8,128)(2,1)S(1)}, bf16...) custom-call(bf16[1320,128]{1,0:T(8,128)(2,1)S(1)} %get-tuple-element, ...), custom_call_target="tpu_custom_call" | custom-call | flops 2000000000 | bytes 1000000 | tf_op jit(solution)/shard_map/pallas_call | solution.py:723
  24.0 0.0 collective-permute-done.4.side_ref
  24.1 3.8 %shard_map.123 = (bf16[32,2,8,80]{3,2,1,0:T(8,128)(2,1)S(1)}, bf16[2,320,128]{2,1,0:T(8,128)(2,1)S(1)}, bf16[2,192,128]{2,1,0:T(8,128)(2,1)S(1)}, bf16[2,2,192,128]{3,2,1,0:T(8,128)(2,1)S(1)}) custom-call(s32[1]{0:T(128)S(6)} %sub.3.right_ref, bf16[1960,128]{1,0:T(8,128)(2,1)S(1)} %collective-permute-done.4.side_ref, ...), custom_call_target="tpu_custom_call" | custom-call | flops 4000000000 | bytes 1000000 | tf_op jit(solution)/shard_map/pallas_call | solution.py:728
  27.9 0.0 collective-permute-done.middle_ref
  27.9 0.0 collective-permute-done.3.flanks_ref
  28.0 5.1 %shard_map.124 = bf16[32,8,8,80]{3,2,1,0:T(8,128)(2,1)} custom-call(s32[1]{0:T(128)S(6)} %sub.3.right_ref, bf16[840,128]{1,0:T(8,128)(2,1)S(1)} %collective-permute-done.middle_ref, bf16[1120,128]{1,0:T(8,128)(2,1)S(1)} %collective-permute-done.3.flanks_ref, bf16[1024,512]{1,0:T(8,128)(2,1)S(1)} %get-tuple-element.36.we_ref.refs_0_, f32[1,32]{1,0:T(1,128)S(1)} %bitcast.8, ...), custom_call_target="tpu_custom_call" | custom-call | flops 5000000000 | bytes 1000000 | tf_op jit(solution)/shard_map/pallas_call | solution.py:738
  (13 shorter events, 0.0 us)
Async XLA Ops:
  0.0 8.8 %copy-start.1 = (bf16[27,32,32]{2,1,0:T(8,128)(2,1)S(1)}, bf16[27,32,32]{2,1,0:T(8,128)(2,1)}, u32[]{:S(2)}) copy-start(bf16[27,32,32]{2,1,0:T(8,128)(2,1)} %we_ref.1) | copy-start | bytes 165892
  0.0 8.8 %copy-start.4 = (bf16[128,256]{1,0:T(8,128)(2,1)S(1)}, bf16[128,256]{1,0:T(8,128)(2,1)}, u32[]{:S(2)}) copy-start(bf16[128,256]{1,0:T(8,128)(2,1)} %wn_ref.1) | copy-start | bytes 196612
  0.0 8.8 %copy-start.3 = (bf16[128,256]{1,0:T(8,128)(2,1)S(1)}, bf16[128,256]{1,0:T(8,128)(2,1)}, u32[]{:S(2)}) copy-start(bf16[128,256]{1,0:T(8,128)(2,1)} %wt_ref.1) | copy-start | bytes 196612
  0.0 8.8 %copy-start = (bf16[27,128,128]{2,1,0:T(8,128)(2,1)S(1)}, bf16[27,128,128]{2,1,0:T(8,128)(2,1)}, u32[]{:S(2)}) copy-start(bf16[27,128,128]{2,1,0:T(8,128)(2,1)} %wc_ref.1) | copy-start | bytes 2654212
  0.0 8.8 %copy-start.2 = (bf16[27,32,64]{2,1,0:T(8,128)(2,1)S(1)}, bf16[27,32,64]{2,1,0:T(8,128)(2,1)}, u32[]{:S(2)}) copy-start(bf16[27,32,64]{2,1,0:T(8,128)(2,1)} %wd_ref.1) | copy-start | bytes 331780
  2.5 8.3 %collective-permute-start.1 = (bf16[840,128]{1,0:T(8,128)(2,1)S(1)}, bf16[840,128]{1,0:T(8,128)(2,1)S(1)}, u32[]{:S(2)}, u32[]{:S(2)}) collective-permute-start(bf16[840,128]{1,0:T(8,128)(2,1)S(1)} %get-tuple-element.31), channel_id=1, source_target_pairs={{0,8},{8,16},{16,24},{24,32},{32,40},{40,48},{48,56},{56,64},{64,7... | collective-permute-start | bytes 645128 | tf_op jit(solution)/shard_map/ppermute | solution.py:643
  6.9 8.1 %collective-permute-start.2 = (bf16[840,128]{1,0:T(8,128)(2,1)S(1)}, bf16[840,128]{1,0:T(8,128)(2,1)S(1)}, u32[]{:S(2)}, u32[]{:S(2)}) collective-permute-start(bf16[840,128]{1,0:T(8,128)(2,1)S(1)} %get-tuple-element.32), channel_id=1, source_target_pairs={{8,0},{16,8},{24,16},{32,24},{40,32},{48,40},{56,48},{64,56},{72,6... | collective-permute-start | bytes 645128 | tf_op jit(solution)/shard_map/ppermute | solution.py:643
  8.9 13.7 %copy-start.7 = (f32[32]{0:T(128)S(1)}, f32[32]{0:T(128)}, u32[]{:S(2)}) copy-start(f32[32]{0:T(128)} %param.16) | copy-start | bytes 388
  15.2 8.9 %collective-permute-start.4 = (bf16[1960,128]{1,0:T(8,128)(2,1)S(1)}, bf16[1960,128]{1,0:T(8,128)(2,1)S(1)}, u32[]{:S(2)}, u32[]{:S(2)}) collective-permute-start(bf16[1960,128]{1,0:T(8,128)(2,1)S(1)} %get-tuple-element.50), channel_id=1, source_target_pairs={{0,1},{1,0},{2,3},{3,2},{4,5},{5,4},{6,7},{7,6},{8,9},{9,8},{10,11... | collective-permute-start | bytes 1505288 | tf_op jit(solution)/shard_map/ppermute | solution.py:651
  17.0 10.9 %collective-permute-start = (bf16[840,128]{1,0:T(8,128)(2,1)S(1)}, bf16[840,128]{1,0:T(8,128)(2,1)S(1)}, u32[]{:S(2)}, u32[]{:S(2)}) collective-permute-start(bf16[840,128]{1,0:T(8,128)(2,1)S(1)} %shard_map.119), channel_id=1, source_target_pairs={{1,2},{2,1},{3,4},{4,3},{5,6},{6,5},{9,10},{10,9},{11,12},{12,11},... | collective-permute-start | bytes 645128 | tf_op jit(solution)/shard_map/ppermute | solution.py:651
  20.0 8.0 %collective-permute-start.3 = (bf16[1120,128]{1,0:T(8,128)(2,1)S(1)}, bf16[1120,128]{1,0:T(8,128)(2,1)S(1)}, u32[]{:S(2)}, u32[]{:S(2)}) collective-permute-start(bf16[1120,128]{1,0:T(8,128)(2,1)S(1)} %get-tuple-element.35), channel_id=1, source_target_pairs={{1,2},{2,1},{3,4},{4,3},{5,6},{6,5},{9,10},{10,9},{11,12},{12,11},... | collective-permute-start | bytes 860168 | tf_op jit(solution)/shard_map/ppermute | solution.py:651
  22.6 1.5 %copy-start.5 = (s32[8,8,80]{2,1,0:T(8,128)S(1)}, s32[8,8,80]{2,1,0:T(8,128)}, u32[]{:S(2)}) copy-start(s32[8,8,80]{2,1,0:T(8,128)} %refs_8_.3) | copy-start | bytes 61444
  22.6 1.5 %copy-start.6 = (bf16[32,128]{1,0:T(8,128)(2,1)S(1)}, bf16[32,128]{1,0:T(8,128)(2,1)}, u32[]{:S(2)}) copy-start(bf16[32,128]{1,0:T(8,128)(2,1)} %refs_7_.3) | copy-start | bytes 24580
  22.6 1.5 %copy-start.8 = (f32[128]{0:T(128)S(1)}, f32[128]{0:T(128)}, u32[]{:S(2)}) copy-start(f32[128]{0:T(128)} %param.20) | copy-start | bytes 1540
  22.6 1.5 %copy-start.9 = (f32[32]{0:T(128)S(1)}, f32[32]{0:T(128)}, u32[]{:S(2)}) copy-start(f32[32]{0:T(128)} %param.23) | copy-start | bytes 388
